TPU v7x, 32 devices: a whole 2x2x4 slice. The times are simulated.
32 devices in a mesh: dp: 2 (over x), row: 4 (over y, core), col: 4 (over z).
Axes of the slice: x: 2, y: 2, z: 4, core: 2. Of those that a mesh axis runs over, the one named last changes fastest.
Arguments:
- x_img: bfloat16 [4, 1024, 1536], P('dp', 'row', 'col'), may hold values from -3 to 3
- x_txt: bfloat16 [4, 128, 1536], P('dp', 'row', 'col'), may hold values from -3 to 3
- condition: bfloat16 [4, 1536], P('dp', 'row'), may hold values from -6 to 6
- w_qkv: bfloat16 [2, 1536, 3, 1536], P(None, 'row', None, 'col'), may hold values from -0.15625 to 0.15625
- b_qv: float32 [2, 2, 1536], P(None, None, 'col'), may hold values from -3 to 3
- w_out: bfloat16 [2, 1536, 1536], P(None, 'col', 'row'), may hold values from -0.625 to 0.625
- b_out: float32 [2, 1536], P(None, 'col'), may hold values from -3 to 3
- w_up: bfloat16 [2, 1536, 6144], P(None, 'row', 'col'), may hold values from -0.15625 to 0.15625
- b_up: float32 [2, 6144], P(None, 'col'), may hold values from -3 to 3
- w_down: bfloat16 [2, 6144, 1536], P(None, 'col', 'row'), may hold values from -0.078125 to 0.078125
- b_down: float32 [2, 1536], P(None, 'col'), may hold values from -3 to 3
- w_ada: bfloat16 [2, 1536, 6, 1536], P(None, 'row', None, 'col'), may hold values from -0.21875 to 0.21875
- b_ada: float32 [2, 6, 1536], P(None, None, 'col'), may hold values from -3 to 3
- cot_img: bfloat16 [4, 1024, 1536], P('dp', 'row', 'col'), may hold values from -6 to 6
- cot_txt: bfloat16 [4, 128, 1536], P('dp', 'row', 'col'), may hold values from -6 to 6
Outputs:
- out_img: bfloat16 [4, 1024, 1536], P('dp', 'row', 'col')
- out_txt: bfloat16 [4, 128, 1536], P('dp', 'row', 'col')
- dx_img: float32 [4, 1024, 1536], P('dp', 'row', 'col')
- dx_txt: float32 [4, 128, 1536], P('dp', 'row', 'col')
- d_condition: float32 [4, 1536], P('dp', 'row')
- d_w_qkv: float32 [2, 1536, 3, 1536], P(None, 'row', None, 'col')
- d_b_qv: float32 [2, 2, 1536], P(None, None, 'col')
- d_w_out: float32 [2, 1536, 1536], P(None, 'col', 'row')
- d_b_out: float32 [2, 1536], P(None, 'col')
- d_w_up: float32 [2, 1536, 6144], P(None, 'row', 'col')
- d_b_up: float32 [2, 6144], P(None, 'col')
- d_w_down: float32 [2, 6144, 1536], P(None, 'col', 'row')
- d_b_down: float32 [2, 1536], P(None, 'col')
- d_w_ada: float32 [2, 1536, 6, 1536], P(None, 'row', None, 'col')
- d_b_ada: float32 [2, 6, 1536], P(None, None, 'col')
All inputs are finite; a program needn't handle non-finite values.
Results may differ from a plain program's by a relative error of at most 0.017.
The roundings to bfloat16 on the way count: a program that leaves them out, or rounds other values in their place, can miss the bound.
Values may be sent and summed in bfloat16 or wider, within the bound.
A program may use at most 192 MiB of HBM per device.

v0:
```python
from functools import partial

import jax
import jax.numpy as jnp
from jax import lax
from jax.sharding import PartitionSpec as P

HD = 64


EPSILON = 1e-06
GELU_ROOT = 0.7978845608028654
GELU_CUBIC = 0.044715


def gelu_pair(inputs):
    inner = GELU_ROOT * (inputs + GELU_CUBIC * inputs * inputs * inputs)
    tanh_value = jnp.tanh(inner)
    result = 0.5 * inputs * (1.0 + tanh_value)
    derivative = 0.5 * (1.0 + tanh_value) + 0.5 * inputs * (
        1.0 - tanh_value * tanh_value
    ) * GELU_ROOT * (1.0 + 3.0 * GELU_CUBIC * inputs * inputs)
    return (result, derivative)


def mean_pair(first_part, second_part, full_width):
    total_img, total_txt = lax.psum(
        (jnp.sum(first_part, axis=-1), jnp.sum(second_part, axis=-1)), "col"
    )
    return (total_img[..., None] / full_width, total_txt[..., None] / full_width)


def norm_forward(first_part, second_part, full_width):
    mean_img, mean_txt = mean_pair(first_part, second_part, full_width)
    centred_img = first_part - mean_img
    centred_txt = second_part - mean_txt
    var_img, var_txt = mean_pair(centred_img * centred_img, centred_txt * centred_txt, full_width)
    inverse_img = lax.rsqrt(var_img + EPSILON)
    inverse_txt = lax.rsqrt(var_txt + EPSILON)
    return ([centred_img * inverse_img, centred_txt * inverse_txt], [inverse_img, inverse_txt])


def norm_backward(grad_img, normed_img, inverse_img, grad_txt, normed_txt, inverse_txt, full_width):
    sum_img, cross_img, sum_txt, cross_txt = lax.psum(
        (
            jnp.sum(grad_img, axis=-1),
            jnp.sum(grad_img * normed_img, axis=-1),
            jnp.sum(grad_txt, axis=-1),
            jnp.sum(grad_txt * normed_txt, axis=-1),
        ),
        "col",
    )
    back_img = inverse_img * (
        grad_img - sum_img[..., None] / full_width - normed_img * cross_img[..., None] / full_width
    )
    back_txt = inverse_txt * (
        grad_txt - sum_txt[..., None] / full_width - normed_txt * cross_txt[..., None] / full_width
    )
    return [back_img, back_txt]


def gather_features(part_img, part_txt):
    return (
        lax.all_gather(part_img, "col", axis=2, tiled=True),
        lax.all_gather(part_txt, "col", axis=2, tiled=True),
    )


def reduce_columns(term_img, term_txt):
    return (
        lax.psum_scatter(term_img, "col", scatter_dimension=2, tiled=True),
        lax.psum_scatter(term_txt, "col", scatter_dimension=2, tiled=True),
    )


def to_sequences(item_block):
    return lax.all_to_all(item_block, "row", split_axis=0, concat_axis=1, tiled=True)


def to_tokens(item_block):
    return lax.all_to_all(item_block, "row", split_axis=1, concat_axis=0, tiled=True)


def head_items(array):
    heads_local = array.shape[-1] // HD
    split = array.reshape(array.shape[:-1] + (heads_local, HD))
    moved = jnp.moveaxis(split, -2, 1)
    return moved.reshape((moved.shape[0] * heads_local,) + moved.shape[2:])


def token_items(array, seq_count):
    grouped = array.reshape((seq_count, array.shape[0] // seq_count) + array.shape[1:])
    moved = jnp.moveaxis(grouped, 1, -2)
    return moved.reshape(moved.shape[:-2] + (moved.shape[-2] * moved.shape[-1],))


def mod_row(modulation, position):
    return modulation[:, position, None, :]


def modulate(normed, modulation, position):
    return (
        normed * (1.0 + mod_row(modulation, position + 1)) + mod_row(modulation, position)
    ).astype(jnp.bfloat16)


def attend_packed(packed, score_scale):
    queries, key_block, value_block = packed
    scores = jnp.dot(queries, key_block.T, preferred_element_type=jnp.float32) * score_scale
    highest = jnp.max(scores, axis=-1, keepdims=True)
    log_total = highest + jnp.log(jnp.sum(jnp.exp(scores - highest), axis=-1, keepdims=True))
    soft_weights = jnp.exp(scores - log_total).astype(jnp.bfloat16)
    attended = jnp.dot(soft_weights, value_block, preferred_element_type=jnp.float32).astype(
        jnp.bfloat16
    )
    return (attended, log_total[:, 0])


def attend_back_packed(packed, score_scale):
    queries, key_block, value_block, attended, log_total, d_attended = packed
    scores = jnp.dot(queries, key_block.T, preferred_element_type=jnp.float32) * score_scale
    soft_weights = jnp.exp(scores - log_total[:, None])
    soft_bf = soft_weights.astype(jnp.bfloat16)
    d_values = jnp.dot(soft_bf.T, d_attended, preferred_element_type=jnp.float32).astype(
        jnp.bfloat16
    )
    d_soft = jnp.dot(d_attended, value_block.T, preferred_element_type=jnp.float32)
    centre = jnp.sum(
        d_attended.astype(jnp.float32) * attended.astype(jnp.float32), axis=-1, keepdims=True
    )
    d_scores = (soft_weights * (d_soft - centre)).astype(jnp.bfloat16)
    d_queries = (
        jnp.dot(d_scores, key_block, preferred_element_type=jnp.float32) * score_scale
    ).astype(jnp.bfloat16)
    d_keys = (
        jnp.dot(d_scores.T, queries, preferred_element_type=jnp.float32) * score_scale
    ).astype(jnp.bfloat16)
    return (d_queries, d_keys, d_values)


def weight_terms(hidden_one, d_qkv, attn_in, d_branch, hidden_two, d_pre, act_in, d_mlp):
    grad_qkv = jnp.einsum("std,stke->dke", hidden_one, d_qkv, preferred_element_type=jnp.float32)
    grad_out = jnp.einsum("std,ste->de", attn_in, d_branch, preferred_element_type=jnp.float32)
    grad_up = jnp.einsum("std,stf->df", hidden_two, d_pre, preferred_element_type=jnp.float32)
    grad_down = jnp.einsum("stf,std->fd", act_in, d_mlp, preferred_element_type=jnp.float32)
    return (grad_qkv, grad_out, grad_up, grad_down)


def local(
    x_img,
    x_txt,
    condition,
    w_qkv,
    b_qv,
    w_out,
    b_out,
    w_up,
    b_up,
    w_down,
    b_down,
    w_ada,
    b_ada,
    cot_img,
    cot_txt,
):
    col_count = lax.axis_size("col")
    row_count = lax.axis_size("row")
    local_width = x_img.shape[2]
    full_width = local_width * col_count
    img_rows = x_img.shape[1]
    seq_count = x_img.shape[0]
    score_scale = HD ** (-0.5)
    cond_wide = condition.astype(jnp.float32)
    cond_act = jax.nn.silu(cond_wide).astype(jnp.bfloat16)
    ada_terms = [
        jnp.einsum("sc,ckd->skd", cond_act, w_ada[stream], preferred_element_type=jnp.float32)
        for stream in range(2)
    ]
    mod_img, mod_txt = lax.psum((ada_terms[0], ada_terms[1]), "row")
    modulation = [mod_img + b_ada[0], mod_txt + b_ada[1]]
    qkv_full, out_full, up_full, down_full = (
        lax.all_gather(w_qkv, "row", axis=1, tiled=True),
        lax.all_gather(w_out, "row", axis=2, tiled=True),
        lax.all_gather(w_up, "row", axis=1, tiled=True),
        lax.all_gather(w_down, "row", axis=2, tiled=True),
    )
    resid = [x_img.astype(jnp.float32), x_txt.astype(jnp.float32)]
    normed_one, inverse_one = norm_forward(resid[0], resid[1], full_width)
    hidden_one = [modulate(normed_one[stream], modulation[stream], 0) for stream in range(2)]
    hidden_one_full = gather_features(hidden_one[0], hidden_one[1])
    qkv_parts = []
    for stream in range(2):
        bias_rows = jnp.stack(
            [b_qv[stream, 0], jnp.zeros_like(b_qv[stream, 0]), b_qv[stream, 1]], axis=0
        )
        projected = jnp.einsum(
            "std,dke->stke",
            hidden_one_full[stream],
            qkv_full[stream],
            preferred_element_type=jnp.float32,
        )
        qkv_parts.append((projected + bias_rows).astype(jnp.bfloat16))
    by_items = to_sequences(head_items(jnp.concatenate(qkv_parts, axis=1)))
    queries = by_items[:, :, 0]
    key_block = by_items[:, :, 1]
    value_block = by_items[:, :, 2]
    attended, log_total = lax.map(
        partial(attend_packed, score_scale=score_scale), (queries, key_block, value_block)
    )
    attn_tokens = token_items(to_tokens(attended), seq_count)
    attn_parts = [attn_tokens[:, :img_rows], attn_tokens[:, img_rows:]]
    out_terms = [
        jnp.einsum(
            "std,de->ste", attn_parts[stream], out_full[stream], preferred_element_type=jnp.float32
        )
        for stream in range(2)
    ]
    attn_img, attn_txt = reduce_columns(out_terms[0], out_terms[1])
    attn_branch = [attn_img + b_out[0], attn_txt + b_out[1]]
    middle = [
        resid[stream] + mod_row(modulation[stream], 2) * attn_branch[stream] for stream in range(2)
    ]
    normed_two, inverse_two = norm_forward(middle[0], middle[1], full_width)
    hidden_two = [modulate(normed_two[stream], modulation[stream], 3) for stream in range(2)]
    hidden_two_full = gather_features(hidden_two[0], hidden_two[1])
    slopes = []
    act_bf = []
    down_terms = []
    for stream in range(2):
        pre_value = (
            jnp.einsum(
                "std,df->stf",
                hidden_two_full[stream],
                up_full[stream],
                preferred_element_type=jnp.float32,
            )
            + b_up[stream]
        )
        gelu_value, gelu_slope = gelu_pair(pre_value)
        slopes.append(gelu_slope)
        act_bf.append(gelu_value.astype(jnp.bfloat16))
        down_terms.append(
            jnp.einsum(
                "stf,fd->std", act_bf[stream], down_full[stream], preferred_element_type=jnp.float32
            )
        )
    mlp_img, mlp_txt = reduce_columns(down_terms[0], down_terms[1])
    mlp_branch = [mlp_img + b_down[0], mlp_txt + b_down[1]]
    results = [
        (middle[stream] + mod_row(modulation[stream], 5) * mlp_branch[stream]).astype(jnp.bfloat16)
        for stream in range(2)
    ]
    grads = [cot_img.astype(jnp.float32), cot_txt.astype(jnp.float32)]
    d_mlp = [grads[stream] * mod_row(modulation[stream], 5) for stream in range(2)]
    d_mlp_bf = [d_mlp[stream].astype(jnp.bfloat16) for stream in range(2)]
    d_mlp_full = gather_features(d_mlp_bf[0], d_mlp_bf[1])
    d_pre = [
        jnp.einsum(
            "std,fd->stf", d_mlp_full[stream], down_full[stream], preferred_element_type=jnp.float32
        )
        * slopes[stream]
        for stream in range(2)
    ]
    d_pre_bf = [d_pre[stream].astype(jnp.bfloat16) for stream in range(2)]
    up_back = [
        jnp.einsum(
            "stf,df->std", d_pre_bf[stream], up_full[stream], preferred_element_type=jnp.float32
        )
        for stream in range(2)
    ]
    d_hidden_two = reduce_columns(up_back[0], up_back[1])
    back_two = norm_backward(
        d_hidden_two[0] * (1.0 + mod_row(modulation[0], 4)),
        normed_two[0],
        inverse_two[0],
        d_hidden_two[1] * (1.0 + mod_row(modulation[1], 4)),
        normed_two[1],
        inverse_two[1],
        full_width,
    )
    d_middle = [grads[stream] + back_two[stream] for stream in range(2)]
    d_branch = [d_middle[stream] * mod_row(modulation[stream], 2) for stream in range(2)]
    d_branch_bf = [d_branch[stream].astype(jnp.bfloat16) for stream in range(2)]
    d_branch_full = gather_features(d_branch_bf[0], d_branch_bf[1])
    d_att_parts = [
        jnp.einsum(
            "std,ed->ste",
            d_branch_full[stream],
            out_full[stream],
            preferred_element_type=jnp.float32,
        ).astype(jnp.bfloat16)
        for stream in range(2)
    ]
    d_att_items = to_sequences(head_items(jnp.concatenate(d_att_parts, axis=1)))
    d_queries, d_keys, d_values = lax.map(
        partial(attend_back_packed, score_scale=score_scale),
        (queries, key_block, value_block, attended, log_total, d_att_items),
    )
    d_joint = jnp.stack([d_queries, d_keys, d_values], axis=2)
    d_qkv_tokens = token_items(to_tokens(d_joint), seq_count)
    d_qkv = [d_qkv_tokens[:, :img_rows], d_qkv_tokens[:, img_rows:]]
    qkv_back = [
        jnp.einsum(
            "stke,dke->std", d_qkv[stream], qkv_full[stream], preferred_element_type=jnp.float32
        )
        for stream in range(2)
    ]
    d_hidden_one = reduce_columns(qkv_back[0], qkv_back[1])
    back_one = norm_backward(
        d_hidden_one[0] * (1.0 + mod_row(modulation[0], 1)),
        normed_one[0],
        inverse_one[0],
        d_hidden_one[1] * (1.0 + mod_row(modulation[1], 1)),
        normed_one[1],
        inverse_one[1],
        full_width,
    )
    d_inputs = [d_middle[stream] + back_one[stream] for stream in range(2)]
    mods_local = []
    for stream in range(2):
        mods_local.append(
            jnp.stack(
                [
                    jnp.sum(d_hidden_one[stream], axis=1),
                    jnp.sum(d_hidden_one[stream] * normed_one[stream], axis=1),
                    jnp.sum(d_middle[stream] * attn_branch[stream], axis=1),
                    jnp.sum(d_hidden_two[stream], axis=1),
                    jnp.sum(d_hidden_two[stream] * normed_two[stream], axis=1),
                    jnp.sum(grads[stream] * mlp_branch[stream], axis=1),
                ],
                axis=1,
            )
        )
    bias_qv_local = jnp.stack(
        [
            jnp.stack(
                [
                    jnp.sum(d_qkv[stream][:, :, 0].astype(jnp.float32), axis=(0, 1)),
                    jnp.sum(d_qkv[stream][:, :, 2].astype(jnp.float32), axis=(0, 1)),
                ],
                axis=0,
            )
            for stream in range(2)
        ],
        axis=0,
    )
    bias_out_local = jnp.stack(
        [jnp.sum(d_branch[stream], axis=(0, 1)) for stream in range(2)], axis=0
    )
    bias_up_local = jnp.stack([jnp.sum(d_pre[stream], axis=(0, 1)) for stream in range(2)], axis=0)
    bias_down_local = jnp.stack(
        [jnp.sum(d_mlp[stream], axis=(0, 1)) for stream in range(2)], axis=0
    )
    d_mods_img, d_mods_txt, grad_bqv, grad_bout, grad_bup, grad_bdown = lax.psum(
        (
            mods_local[0],
            mods_local[1],
            bias_qv_local,
            bias_out_local,
            bias_up_local,
            bias_down_local,
        ),
        "row",
    )
    d_mods = [d_mods_img, d_mods_txt]
    cond_terms = jnp.einsum(
        "skd,ckd->sc", d_mods[0], w_ada[0].astype(jnp.float32), precision=lax.Precision.HIGHEST
    ) + jnp.einsum(
        "skd,ckd->sc", d_mods[1], w_ada[1].astype(jnp.float32), precision=lax.Precision.HIGHEST
    )
    d_silu = lax.psum(cond_terms, "col")
    sigmoid_cond = jax.nn.sigmoid(cond_wide)
    d_condition = d_silu * sigmoid_cond * (1.0 + cond_wide * (1.0 - sigmoid_cond))
    grad_ada = jnp.stack(
        [
            jnp.einsum(
                "sc,skd->ckd",
                cond_act.astype(jnp.float32),
                d_mods[stream],
                precision=lax.Precision.HIGHEST,
            )
            for stream in range(2)
        ],
        axis=0,
    )
    grad_bada = jnp.stack([jnp.sum(d_mods[stream], axis=0) for stream in range(2)], axis=0)

    def spread(array):
        flat = array.reshape(array.shape[:2] + (-1,))
        return jnp.tile(flat, (1, 1, row_count))

    moved = (
        lax.all_to_all(hidden_one_full[0], "row", split_axis=2, concat_axis=1, tiled=True),
        lax.all_to_all(spread(d_qkv[0]), "row", split_axis=2, concat_axis=1, tiled=True),
        lax.all_to_all(spread(attn_parts[0]), "row", split_axis=2, concat_axis=1, tiled=True),
        lax.all_to_all(d_branch_full[0], "row", split_axis=2, concat_axis=1, tiled=True),
        lax.all_to_all(hidden_two_full[0], "row", split_axis=2, concat_axis=1, tiled=True),
        lax.all_to_all(spread(d_pre_bf[0]), "row", split_axis=2, concat_axis=1, tiled=True),
        lax.all_to_all(spread(act_bf[0]), "row", split_axis=2, concat_axis=1, tiled=True),
        lax.all_to_all(d_mlp_full[0], "row", split_axis=2, concat_axis=1, tiled=True),
        lax.all_to_all(hidden_one_full[1], "row", split_axis=2, concat_axis=1, tiled=True),
        lax.all_to_all(spread(d_qkv[1]), "row", split_axis=2, concat_axis=1, tiled=True),
        lax.all_to_all(spread(attn_parts[1]), "row", split_axis=2, concat_axis=1, tiled=True),
        lax.all_to_all(d_branch_full[1], "row", split_axis=2, concat_axis=1, tiled=True),
        lax.all_to_all(hidden_two_full[1], "row", split_axis=2, concat_axis=1, tiled=True),
        lax.all_to_all(spread(d_pre_bf[1]), "row", split_axis=2, concat_axis=1, tiled=True),
        lax.all_to_all(spread(act_bf[1]), "row", split_axis=2, concat_axis=1, tiled=True),
        lax.all_to_all(d_mlp_full[1], "row", split_axis=2, concat_axis=1, tiled=True),
    )
    qkv_img = moved[1].reshape(moved[1].shape[:2] + (3, -1))
    qkv_txt = moved[9].reshape(moved[9].shape[:2] + (3, -1))
    terms_img = weight_terms(
        moved[0], qkv_img, moved[2], moved[3], moved[4], moved[5], moved[6], moved[7]
    )
    terms_txt = weight_terms(
        moved[8], qkv_txt, moved[10], moved[11], moved[12], moved[13], moved[14], moved[15]
    )
    grad_qkv = jnp.stack([terms_img[0], terms_txt[0]], axis=0)
    grad_out = jnp.stack([terms_img[1], terms_txt[1]], axis=0)
    grad_up = jnp.stack([terms_img[2], terms_txt[2]], axis=0)
    grad_down = jnp.stack([terms_img[3], terms_txt[3]], axis=0)
    summed = lax.psum(
        (
            grad_qkv,
            grad_bqv,
            grad_out,
            grad_bout,
            grad_up,
            grad_bup,
            grad_down,
            grad_bdown,
            grad_ada,
            grad_bada,
        ),
        "dp",
    )
    return (
        results[0],
        results[1],
        d_inputs[0],
        d_inputs[1],
        d_condition,
        summed[0],
        summed[1],
        summed[2],
        summed[3],
        summed[4],
        summed[5],
        summed[6],
        summed[7],
        summed[8],
        summed[9],
    )


def solution(mesh):
    placed = (
        P("dp", "row", "col"),
        P("dp", "row", "col"),
        P("dp", "row"),
        P(None, "row", None, "col"),
        P(None, None, "col"),
        P(None, "col", "row"),
        P(None, "col"),
        P(None, "row", "col"),
        P(None, "col"),
        P(None, "col", "row"),
        P(None, "col"),
        P(None, "row", None, "col"),
        P(None, None, "col"),
        P("dp", "row", "col"),
        P("dp", "row", "col"),
    )
    return jax.shard_map(
        local,
        mesh=mesh,
        in_specs=placed,
        out_specs=(
            P("dp", "row", "col"),
            P("dp", "row", "col"),
            P("dp", "row", "col"),
            P("dp", "row", "col"),
            P("dp", "row"),
            P(None, "row", None, "col"),
            P(None, None, "col"),
            P(None, "col", "row"),
            P(None, "col"),
            P(None, "row", "col"),
            P(None, "col"),
            P(None, "col", "row"),
            P(None, "col"),
            P(None, "row", None, "col"),
            P(None, None, "col"),
        ),
        check_vma=False,
    )
```

profile of v0, /device:TPU:0, one launch (start us, length us, event | category | flops | bytes accessed | tf_op | source)
XLA Modules:
  0.0 1684.8 jit_solution(6033964019715565224)
XLA Ops:
  48.5 15.1 all_gather.38
  63.7 19.6 %all-gather.9.cloned.1.call-done = bf16[2,256,1536]{2,1,0:T(8,128)(2,1)} async-done(((bf16[2,256,384]{2,1,0:T(8,128)(2,1)}), bf16[2,256,1536]{2,1,0:T(8,128)(2,1)}) %all-gather.9.cloned.1.call-update) | async-done | bytes 1572880 | tf_op jit(solution)/shard_map/all_gather | solution.py:64
  83.2 51.6 %all-gather.11.cloned.1.call-done = bf16[2,1536,3,384]{3,1,2,0:T(8,128)(2,1)} async-done(((bf16[2,384,3,384]{3,1,2,0:T(8,128)(2,1)}), bf16[2,1536,3,384]{3,1,2,0:T(8,128)(2,1)}) %all-gather.11.cloned.1.call-update) | async-done | bytes 7077904 | tf_op jit(solution)/shard_map/all_gather | solution.py:182
  149.3 30.3 %all-to-all-done = bf16[12,288,3,64]{1,3,2,0:T(8,128)(2,1)S(1)} async-done(((bf16[12,288,3,64]{1,3,2,0:T(8,128)(2,1)}), bf16[12,288,3,64]{1,3,2,0:T(8,128)(2,1)S(1)}, u32[]{:S(2)}, u32[]{:S(2)}) %all-to-all-start) | async-done | bytes 1327136 | tf_op jit(solution)/shard_map/all_to_all | solution.py:77
  228.2 15.3 reduce-scatter.13.cloned.1.call-done
  244.5 60.4 %reduce-scatter.9.cloned.1.call-done = f32[2,256,384]{2,1,0:T(8,128)} async-done(((f32[2,256,1536]{2,1,0:T(8,128)}), f32[2,256,384]{2,1,0:T(8,128)}) %reduce-scatter.9.cloned.1.call-update) | async-done | bytes 786448 | tf_op jit(solution)/shard_map/reduce_scatter | solution.py:71
  328.4 13.6 all_gather.46
  342.2 13.6 all_gather.43
  355.8 14.7 all-gather.17.cloned.1.call-done
  374.5 61.7 %all-gather.19.cloned.1.call-done = bf16[2,1536,1536]{2,1,0:T(8,128)(2,1)} async-done(((bf16[2,1536,384]{2,1,0:T(8,128)(2,1)}), bf16[2,1536,1536]{2,1,0:T(8,128)(2,1)}) %all-gather.19.cloned.1.call-update) | async-done | bytes 9437200 | tf_op jit(solution)/shard_map/all_gather | solution.py:185
  443.6 31.3 %all-gather.15.cloned.1.call-done = bf16[2,256,1536]{2,1,0:T(8,128)(2,1)} async-done(((bf16[2,256,384]{2,1,0:T(8,128)(2,1)}), bf16[2,256,1536]{2,1,0:T(8,128)(2,1)}) %all-gather.15.cloned.1.call-update) | async-done | bytes 1572880 | tf_op jit(solution)/shard_map/all_gather | solution.py:64
  483.1 29.9 %all-gather.21.cloned.1.call-done = bf16[2,256,1536]{2,1,0:T(8,128)(2,1)} async-done(((bf16[2,256,384]{2,1,0:T(8,128)(2,1)}), bf16[2,256,1536]{2,1,0:T(8,128)(2,1)}) %all-gather.21.cloned.1.call-update) | async-done | bytes 1572880 | tf_op jit(solution)/shard_map/all_gather | solution.py:64
  582.3 15.6 all-to-all-start.17
  617.7 43.4 %reduce-scatter.11.cloned.1.call-done = f32[2,256,384]{2,1,0:T(8,128)} async-done(((f32[2,256,1536]{2,1,0:T(8,128)}), f32[2,256,384]{2,1,0:T(8,128)}) %reduce-scatter.11.cloned.1.call-update) | async-done | bytes 786448 | tf_op jit(solution)/shard_map/reduce_scatter | solution.py:71
  683.9 16.7 all-to-all-done.8
  732.4 13.7 all_gather.47
  785.0 13.7 all-to-all-done.12
  810.9 37.6 %while.27 = (s32[]{:T(128)}, bf16[3,1152,64]{1,2,0:T(8,128)(2,1)S(1)}, bf16[3,1152,64]{1,2,0:T(8,128)(2,1)}, bf16[3,1152,64]{1,2,0:T(8,128)(2,1)}, bf16[3,1152,6...) while((s32[]{:T(128)}, ...), condition=%wide.region_38.39_spmd, body=%wide.region_36.38_spmd.sunk | while | flops 857971584 | bytes 43240104 | solution.py:295
  859.3 20.6 %all-to-all-done.13 = bf16[2,256,6144]{1,0,2:T(2,128)(2,1)} async-done(((bf16[2,256,6144]{1,0,2:T(2,128)(2,1)}), bf16[2,256,6144]{1,0,2:T(2,128)(2,1)}, u32[]{:S(2)}, u32[]{:S(2)}) %all-to-all-start.13) | async-done | bytes 6291488 | tf_op jit(solution)/shard_map/all_to_all | solution.py:398
  887.2 13.7 all-to-all-done.3
  1003.9 16.2 copy.321
  1100.6 27.3 %all-to-all-done.5 = bf16[2,256,4608]{1,0,2:T(2,128)(2,1)} async-done(((bf16[2,256,4608]{1,0,2:T(2,128)(2,1)}), bf16[2,256,4608]{1,0,2:T(2,128)(2,1)}, u32[]{:S(2)}, u32[]{:S(2)}) %all-to-all-start.5) | async-done | bytes 4718624 | tf_op jit(solution)/shard_map/all_to_all | solution.py:394
  1130.9 19.2 %copy.295 = bf16[2,4,256,1152]{2,1,3,0:T(4,128)(2,1)} copy(bf16[2,4,256,1152]{2,3,1,0:T(8,128)(2,1)S(1)} %bitcast.491) | data formatting | bytes 9437184 | tf_op jit(solution)/shard_map/all_to_all | solution.py:394
  1224.4 436.4 %all-reduce.12.cloned.1.call-done = (f32[2,384,3,384]{3,1,2,0:T(8,128)}, f32[2,384,384]{2,1,0:T(8,128)}, f32[2,384,1536]{2,1,0:T(8,128)}, f32[2,1536,384]{2,1,0:T(8,128)}, f32[2,384,6,384]{3,1,2,0:T(8,128)}) async-done(((f32[2,384,3,384]{3,1,2,0:T(8,128)}, f32[2,384,384]{2,1,0:T(8,128)}, f32[2,384,1536]{2,1,0:T(8,128)}, f32[2,1536,384]{2,1,0:T(8,128)}, f32[2,384,6,384]{3,1,2,0:T(8,128)}), ...) | async-done | bytes 21233680 | tf_op jit(solution)/shard_map/psum | solution.py:422
  (543 shorter events, 687.0 us)
Async XLA Ops:
  7.2 76.0 %all-gather.9.cloned.1.call-start = ((), (), s32[]{:S(2)}) async-start(), calls=%async_computation.28 | async-start | bytes 1966080 | tf_op jit(solution)/shard_map/all_gather | solution.py:64
  46.9 87.9 %all-gather.11.cloned.1.call-start = ((), (), s32[]{:S(2)}) async-start(), calls=%async_computation.29 | async-start | bytes 8847360 | tf_op jit(solution)/shard_map/all_gather | solution.py:182
  144.9 34.7 %all-to-all-start = ((bf16[12,288,3,64]{1,3,2,0:T(8,128)(2,1)}), bf16[12,288,3,64]{1,3,2,0:T(8,128)(2,1)S(1)}, u32[]{:S(2)}, u32[]{:S(2)}) async-start(bf16[12,288,3,64]{1,3,2,0:T(8,128)(2,1)} %bitcast.509), calls=%async_computation | async-start | bytes 3538944 | tf_op jit(solution)/shard_map/all_to_all | solution.py:77
  148.5 71.5 %all-gather.13.cloned.1.call-start = ((), (), s32[]{:S(2)}) async-start(), calls=%async_computation.30 | async-start | bytes 2949120 | tf_op jit(solution)/shard_map/all_gather | solution.py:183
  149.2 94.2 %reduce-scatter.13.cloned.1.call-start = ((), (), s32[]{:S(2)}) async-start(), calls=%async_computation.36 | async-start | bytes 491520 | tf_op jit(solution)/shard_map/reduce_scatter | solution.py:72
  222.5 82.4 %reduce-scatter.9.cloned.1.call-start = ((), (), s32[]{:S(2)}) async-start(), calls=%async_computation.31 | async-start | bytes 3932160 | tf_op jit(solution)/shard_map/reduce_scatter | solution.py:71
  226.6 143.8 %all-gather.17.cloned.1.call-start = ((), (), s32[]{:S(2)}) async-start(), calls=%async_computation.33 | async-start | bytes 11796480 | tf_op jit(solution)/shard_map/all_gather | solution.py:184
  227.3 208.8 %all-gather.19.cloned.1.call-start = ((), (), s32[]{:S(2)}) async-start(), calls=%async_computation.34 | async-start | bytes 11796480 | tf_op jit(solution)/shard_map/all_gather | solution.py:185
  228.0 246.8 %all-gather.15.cloned.1.call-start = ((), (), s32[]{:S(2)}) async-start(), calls=%async_computation.32 | async-start | bytes 1966080 | tf_op jit(solution)/shard_map/all_gather | solution.py:64
  326.4 186.6 %all-gather.21.cloned.1.call-start = ((), (), s32[]{:S(2)}) async-start(), calls=%async_computation.38 | async-start | bytes 1966080 | tf_op jit(solution)/shard_map/all_gather | solution.py:64
  328.3 273.8 %reduce-scatter.19.cloned.1.call-start = ((), (), s32[]{:S(2)}) async-start(), calls=%async_computation.41 | async-start | bytes 491520 | tf_op jit(solution)/shard_map/reduce_scatter | solution.py:72
  443.5 160.3 %reduce-scatter.17.cloned.1.call-start = ((), (), s32[]{:S(2)}) async-start(), calls=%async_computation.39 | async-start | bytes 3932160 | tf_op jit(solution)/shard_map/reduce_scatter | solution.py:71
  529.2 131.8 %reduce-scatter.11.cloned.1.call-start = ((), (), s32[]{:S(2)}) async-start(), calls=%async_computation.35 | async-start | bytes 3932160 | tf_op jit(solution)/shard_map/reduce_scatter | solution.py:71
  582.3 82.5 %all-to-all-start.17 = ((bf16[2,256,1536]{1,0,2:T(2,128)(2,1)}), bf16[2,256,1536]{1,0,2:T(2,128)(2,1)}, u32[]{:S(2)}, u32[]{:S(2)}) async-start(bf16[2,256,1536]{1,0,2:T(2,128)(2,1)} %copy.330), calls=%async_computation.25 | async-start | bytes 3145728 | tf_op jit(solution)/shard_map/all_to_all | solution.py:400
  598.0 132.2 %reduce-scatter.15.cloned.1.call-start = ((), (), s32[]{:S(2)}) async-start(), calls=%async_computation.37 | async-start | bytes 491520 | tf_op jit(solution)/shard_map/reduce_scatter | solution.py:72
  668.8 83.2 %all-gather.23.cloned.1.call-start = ((), (), s32[]{:S(2)}) async-start(), calls=%async_computation.40 | async-start | bytes 1966080 | tf_op jit(solution)/shard_map/all_gather | solution.py:64
  700.6 26.0 %all-to-all-start.14 = ((bf16[4,2,12288]{2,1,0:T(2,128)(2,1)}), bf16[4,2,12288]{2,1,0:T(2,128)(2,1)}, u32[]{:S(2)}, u32[]{:S(2)}) async-start(bf16[4,2,12288]{2,1,0:T(2,128)(2,1)} %reshape.234), calls=%async_computation.22 | async-start | bytes 393216 | tf_op jit(solution)/shard_map/all_to_all | solution.py:405
  804.0 75.9 %all-to-all-start.13 = ((bf16[2,256,6144]{1,0,2:T(2,128)(2,1)}), bf16[2,256,6144]{1,0,2:T(2,128)(2,1)}, u32[]{:S(2)}, u32[]{:S(2)}) async-start(bf16[2,256,6144]{1,0,2:T(2,128)(2,1)} %bitcast.488), calls=%async_computation.21 | async-start | bytes 12582912 | tf_op jit(solution)/shard_map/all_to_all | solution.py:398
  905.2 76.0 %all-to-all-start.16 = ((bf16[2,256,6144]{1,0,2:T(2,128)(2,1)}), bf16[2,256,6144]{1,0,2:T(2,128)(2,1)}, u32[]{:S(2)}, u32[]{:S(2)}) async-start(bf16[2,256,6144]{1,0,2:T(2,128)(2,1)} %bitcast.489), calls=%async_computation.24 | async-start | bytes 12582912 | tf_op jit(solution)/shard_map/all_to_all | solution.py:399
  910.5 188.3 %reduce-scatter.23.cloned.1.call-start = ((), (), s32[]{:S(2)}) async-start(), calls=%async_computation.43 | async-start | bytes 491520 | tf_op jit(solution)/shard_map/reduce_scatter | solution.py:72
  990.8 47.7 %all-to-all-start.9 = ((bf16[2,256,1536]{1,0,2:T(2,128)(2,1)}), bf16[2,256,1536]{1,0,2:T(2,128)(2,1)S(1)}, u32[]{:S(2)}, u32[]{:S(2)}) async-start(bf16[2,256,1536]{1,0,2:T(2,128)(2,1)} %copy.308), calls=%async_computation.17 | async-start | bytes 3145728 | tf_op jit(solution)/shard_map/all_to_all | solution.py:396
  994.4 171.7 %reduce-scatter.21.cloned.1.call-start = ((), (), s32[]{:S(2)}) async-start(), calls=%async_computation.42 | async-start | bytes 3932160 | tf_op jit(solution)/shard_map/reduce_scatter | solution.py:71
  1069.2 58.8 %all-to-all-start.5 = ((bf16[2,256,4608]{1,0,2:T(2,128)(2,1)}), bf16[2,256,4608]{1,0,2:T(2,128)(2,1)}, u32[]{:S(2)}, u32[]{:S(2)}) async-start(bf16[2,256,4608]{1,0,2:T(2,128)(2,1)} %bitcast.490), calls=%async_computation.13 | async-start | bytes 9437184 | tf_op jit(solution)/shard_map/all_to_all | solution.py:394
  1074.2 586.7 %all-reduce.12.cloned.1.call-start = ((), (), s32[]{:S(2)}) async-start(), calls=%async_computation.44 | async-start | bytes 42467328 | tf_op jit(solution)/shard_map/psum | solution.py:422
  (110 other events, 2293.2 us)
Sparse Core Ops, SparseCore 0:
  47.0 36.1 all-gather.8
  84.8 49.9 all-gather.10
  150.9 33.8 all-gather.12
  222.6 20.8 reduce-scatter.12
  246.2 58.6 reduce-scatter.8
  306.3 64.1 all-gather.16
  372.0 64.0 all-gather.18
  438.2 36.5 all-gather.14
  477.0 35.9 all-gather.20
  515.7 20.1 reduce-scatter.18
  538.7 58.6 reduce-scatter.16
  600.2 60.8 reduce-scatter.10
  663.9 20.6 reduce-scatter.14
  686.1 34.8 all-gather.22
  968.2 20.9 reduce-scatter.22
  1000.6 60.6 reduce-scatter.20
  1186.8 474.0 all-reduce.11
where the time goes:
time: 1700 us; the launch traced here: 1680 us
  waiting for transfers between devices  928 us (55%)
  local copies, waits for them, and re-layouts  279 us (16%)
  blocking collectives  166 us (10%)
  matrix products  150 us (9%)
  starting transfers between devices  89.8 us (5%)
  other arithmetic  56 us (3%)
    psum x1, waiting for transfers between devices, local(): lax.psum((grad_qkv, grad_bqv, grad_out, grad_bout, grad_up, grad_bup, gra...  436 us
    reduce_scatter x4, waiting for transfers between devices, reduce_columns(): lax.psum_scatter(term_img, 'col', scatter_dimension=2, tiled=True)  104 us
    all_gather x4, waiting for transfers between devices, gather_features(): lax.all_gather(part_img, 'col', axis=2, tiled=True)  80.8 us
    unnamed x226, local copies, waits for them, and re-layouts  72.3 us
    all_gather x1, waiting for transfers between devices, local(): lax.all_gather(w_down, 'row', axis=2, tiled=True)  61.7 us
    all_gather x4, blocking collectives, gather_features(): lax.all_gather(part_txt, 'col', axis=2, tiled=True)  56 us
    all_gather x1, waiting for transfers between devices, local(): lax.all_gather(w_qkv, 'row', axis=1, tiled=True)  51.6 us
    psum x4, blocking collectives, mean_pair(): lax.psum((jnp.sum(first_part, axis=-1), jnp.sum(second_part, axis=-1)), '...  39 us
  transfers between devices with their start and end apart: 36, of which 23 were waited for; matrix products, arithmetic and copies ran while one was open for 25% of the time, Pallas kernels for 0%

commit v1 on v0

v1 whole, which is shorter than its diff:
```python
from functools import partial

import jax
import jax.numpy as jnp
from jax import lax
from jax.experimental import pallas as pl
from jax.experimental.pallas import tpu as pltpu
from jax.sharding import PartitionSpec as P

HD = 64
EPSILON = 1e-06
GELU_ROOT = 0.7978845608028654
GELU_CUBIC = 0.044715
BF = jnp.bfloat16
F32 = jnp.float32
MESH = pl.DeviceIdType.MESH
ANY = pl.BlockSpec(memory_space=pl.ANY)
VM = pl.BlockSpec(memory_space=pltpu.VMEM)
VMEM_LIMIT = 60 * 1024 * 1024


def struct(shape, dtype):
    return jax.ShapeDtypeStruct(shape, dtype)


def aligned(index, size):
    return pl.ds(pl.multiple_of(index * size, size), size)


def send(src, dst, send_sem, recv_sem, axis, index):
    return pltpu.make_async_remote_copy(
        src_ref=src,
        dst_ref=dst,
        send_sem=send_sem,
        recv_sem=recv_sem,
        device_id={axis: index},
        device_id_type=MESH,
    )


def flip(index):
    return index + 1 - 2 * lax.rem(index, 2)


def flip_far(index):
    return lax.rem(index + 2, 4)


def greet(pairs):
    barrier = pltpu.get_barrier_semaphore()
    for axis, index in pairs:
        pl.semaphore_signal(barrier, inc=1, device_id={axis: index}, device_id_type=MESH)
    pl.semaphore_wait(barrier, len(pairs))


def others(axis, count):
    me = lax.axis_index(axis)
    return [(axis, lax.rem(me + step, count)) for step in range(1, count)]


class LineGather:
    def __init__(self, view, count, place, send_sems, recv_sems):
        self.view, self.count, self.place = view, count, place
        self.send_sems, self.recv_sems = send_sems, recv_sems

    def copy(self, side, step, arriving):
        place = self.place
        if side == 0:
            block = place - step - (1 if arriving else 0)
            peer = place + 1
        else:
            block = place + step + (1 if arriving else 0)
            peer = place - 1
        view = self.view(block)
        return send(
            view, view, self.send_sems.at[side, step], self.recv_sems.at[side, step], "col", peer
        )

    def sends(self, side, step):
        if side == 0:
            return jnp.logical_and(self.place - step >= 0, self.place < self.count - 1)
        return jnp.logical_and(self.place + step <= self.count - 1, self.place > 0)

    def arrives(self, side, step):
        if side == 0:
            return self.place - 1 - step >= 0
        return self.place + 1 + step <= self.count - 1

    def start(self, step):
        for side in range(2):

            @pl.when(self.sends(side, step))
            def _():
                self.copy(side, step, False).start()

    def arrive(self, step):
        for side in range(2):

            @pl.when(self.arrives(side, step))
            def _():
                self.copy(side, step, True).wait_recv()

    def finish(self):
        for step in range(self.count - 1):
            for side in range(2):

                @pl.when(self.sends(side, step))
                def _():
                    self.copy(side, step, False).wait_send()


class LineReduce:
    def __init__(self, load, count, place, out_bufs, in_bufs, send_sems, recv_sems):
        self.load, self.count, self.place = load, count, place
        self.out_bufs, self.in_bufs = out_bufs, in_bufs
        self.send_sems, self.recv_sems = send_sems, recv_sems

    def copy(self, side, slot):
        peer = self.place + 1 if side == 0 else self.place - 1
        return send(
            self.out_bufs.at[side, slot],
            self.in_bufs.at[side, slot],
            self.send_sems.at[side, slot],
            self.recv_sems.at[side, slot],
            "col",
            peer,
        )

    def has_behind(self, side):
        return self.place > 0 if side == 0 else self.place < self.count - 1

    def target(self, side, slot):
        return self.place + 1 + slot if side == 0 else self.place - 1 - slot

    def sends(self, side, slot):
        target = self.target(side, slot)
        return target <= self.count - 1 if side == 0 else target >= 0

    def step(self, number):
        slot = self.count - 2 - number
        for side in range(2):

            @pl.when(self.sends(side, slot))
            def _():
                target = self.target(side, slot)
                if slot < self.count - 2:

                    @pl.when(self.has_behind(side))
                    def _():
                        self.copy(side, slot + 1).wait_recv()
                        self.out_bufs[side, slot] = (
                            self.load(target).astype(F32) + self.in_bufs[side, slot + 1].astype(F32)
                        ).astype(BF)

                    @pl.when(jnp.logical_not(self.has_behind(side)))
                    def _():
                        self.out_bufs[side, slot] = self.load(target)

                else:
                    self.out_bufs[side, slot] = self.load(target)
                self.copy(side, slot).start()

    def total(self, store):
        own = self.load(self.place).astype(F32)

        @pl.when(self.place == 0)
        def _():
            self.copy(1, 0).wait_recv()
            store(own + self.in_bufs[1, 0].astype(F32))

        @pl.when(self.place == self.count - 1)
        def _():
            self.copy(0, 0).wait_recv()
            store(own + self.in_bufs[0, 0].astype(F32))

        @pl.when(jnp.logical_and(self.place > 0, self.place < self.count - 1))
        def _():
            self.copy(0, 0).wait_recv()
            self.copy(1, 0).wait_recv()
            store(own + self.in_bufs[0, 0].astype(F32) + self.in_bufs[1, 0].astype(F32))

    def finish(self):
        for slot in range(self.count - 1):
            for side in range(2):

                @pl.when(self.sends(side, slot))
                def _():
                    self.copy(side, slot).wait_send()


def communicate(kernel, name, collective_id, **kwargs):
    return pl.pallas_call(
        kernel,
        name=name,
        compiler_params=pltpu.CompilerParams(
            collective_id=collective_id, has_side_effects=True, vmem_limit_bytes=VMEM_LIMIT
        ),
        **kwargs,
    )


class WeightFlow:
    def __init__(self, kinds, shards, fulls, subs, send_sems, recv_sems):
        self.kinds, self.shards, self.fulls, self.subs = kinds, shards, fulls, subs
        self.send_sems, self.recv_sems = send_sems, recv_sems
        self.pieces = [(n, s, u) for n in range(len(kinds)) for s in range(2) for u in range(subs)]
        self.row = lax.axis_index("row")
        self.half = lax.rem(lax.axis_index("dp"), 2)
        self.mate = flip(lax.axis_index("dp"))
        self.sib, self.far = flip(self.row), flip_far(self.row)

    @staticmethod
    def sem_shape(count, subs):
        return (count * 2 * subs, 5)

    def split(self, depth, sub, part):
        if part is None:
            size = depth // self.subs
            return pl.ds(sub * size, size)
        size = depth // (2 * self.subs)
        return aligned(2 * sub + part, size)

    def view(self, piece, block, part):
        number, stream, sub = self.pieces[piece]
        kind, ref, shard = self.kinds[number], self.fulls[number], self.shards[number]
        if kind == "qkv" or kind == "up":
            depth = shard.shape[-2]
            if part is None:
                size = depth // self.subs
                rows = aligned(block * self.subs + sub, size)
            else:
                rows = aligned(block * 2 * self.subs + 2 * sub + part, depth // (2 * self.subs))
            return ref.at[stream, :, rows, :] if kind == "qkv" else ref.at[stream, rows, :]
        return ref.at[stream, self.split(shard.shape[1], sub, part), aligned(block, shard.shape[2])]

    def source(self, piece, part):
        number, stream, sub = self.pieces[piece]
        ref = self.shards[number]
        rows = self.split(ref.shape[-2], sub, part)
        return ref.at[stream, :, rows, :] if self.kinds[number] == "qkv" else ref.at[stream, rows, :]

    def copy(self, piece, kind):
        sems = (self.send_sems.at[piece, kind], self.recv_sems.at[piece, kind])
        if kind == 0:
            return send(self.source(piece, None), self.view(piece, self.row, None), *sems, "row", self.sib)
        if kind == 1:
            return send(self.source(piece, self.half), self.view(piece, self.row, self.half), *sems, "row", self.far)
        at = self.view(piece, self.far, 1 - self.half if kind == 4 else self.half)
        if kind == 2:
            return send(at, at, *sems, "dp", self.mate)
        return send(at, at, *sems, "row", self.sib)

    def land(self, piece, kind):
        if kind == 0:
            at = self.view(piece, self.sib, None)
        elif kind == 1:
            at = self.view(piece, self.far, self.half)
        elif kind == 2:
            at = self.view(piece, self.far, 1 - self.half)
        elif kind == 3:
            at = self.view(piece, flip(self.far), self.half)
        else:
            at = self.view(piece, flip(self.far), 1 - self.half)
        send(at, at, self.send_sems.at[piece, kind], self.recv_sems.at[piece, kind], "row", self.sib).wait_recv()

    def start(self, kind):
        for piece in range(len(self.pieces)):
            self.copy(piece, kind).start()

    def relay_y(self, piece):
        self.land(piece, 1)
        self.copy(piece, 2).start()
        self.copy(piece, 3).start()

    def relay_x(self, piece):
        self.land(piece, 2)
        self.copy(piece, 4).start()

    def finish(self):
        for piece in range(len(self.pieces)):
            for kind in (0, 3, 4):
                self.land(piece, kind)
        for piece in range(len(self.pieces)):
            for kind in range(5):
                self.copy(piece, kind).wait_send()

    def own_view(self, number):
        kind, ref, shard = self.kinds[number], self.fulls[number], self.shards[number]
        if kind == "qkv":
            return ref.at[:, :, aligned(self.row, shard.shape[2]), :]
        if kind == "up":
            return ref.at[:, aligned(self.row, shard.shape[1]), :]
        return ref.at[:, :, aligned(self.row, shard.shape[2])]


def gathered_shape(kind, shape):
    if kind == "qkv":
        return shape[:2] + (shape[2] * 4, shape[3])
    if kind == "up":
        return (shape[0], shape[1] * 4, shape[2])
    return shape[:2] + (shape[2] * 4,)


class OwnCopy:
    def __init__(self, src, stage, dst, sem_in, sem_out):
        self.first = pltpu.make_async_copy(src, stage, sem_in)
        self.second = pltpu.make_async_copy(stage, dst, sem_out)

    def begin(self):
        self.first.start()

    def settle(self):
        self.first.wait()
        self.second.start()

    def finish(self):
        self.second.wait()


def line_from(shard, full, width, cols, place, zs, zr):
    def at(block):
        return full.at[:, :, aligned(block, width)]

    line = LineGather(at, cols, place, zs, zr)

    def first():
        for side in range(2):
            peer = place + 1 if side == 0 else place - 1

            @pl.when(line.sends(side, 0))
            def _():
                send(shard, at(place), zs.at[side, 0], zr.at[side, 0], "col", peer).start()

    return line, first, at(place)


def prologue(cols, x_img, x_txt, qkv, out, table, bias):
    shards = (x_img, x_txt, qkv, out)
    width = x_img.shape[2]
    rows = 4
    kinds = ("qkv", "out")
    full_shapes = [s.shape[:2] + (s.shape[2] * cols,) for s in shards[:2]]
    full_shapes += [gathered_shape(k, s.shape) for k, s in zip(kinds, shards[2:])]
    table_shape = table.shape

    def kernel(*refs):
        shard = refs[:4]
        table_ref, bias_ref = refs[4:6]
        full = refs[6:10]
        mods_ref = refs[10]
        stage = refs[11:15]
        parts = refs[15]
        local_in, local_out, zs, zr, ws, wr, ms, mr = refs[16:]
        place = lax.axis_index("col")
        row = lax.axis_index("row")
        flow = WeightFlow(kinds, shard[2:], full[2:], 1, ws, wr)
        lines = [line_from(shard[n], full[n], width, cols, place, zs.at[n], zr.at[n]) for n in range(2)]
        owns = [OwnCopy(shard[n], stage[n], lines[n][2], local_in.at[n], local_out.at[n]) for n in range(2)]
        owns += [
            OwnCopy(shard[2 + n], stage[2 + n], flow.own_view(n), local_in.at[2 + n], local_out.at[2 + n])
            for n in range(2)
        ]
        for own in owns:
            own.begin()
        greet(others("row", rows) + others("col", cols) + [("dp", flow.mate)])

        def part_copy(step):
            return send(
                table_ref, parts.at[step - 1], ms.at[step - 1], mr.at[step - 1], "row", lax.rem(row + step, rows)
            )

        for step in range(1, rows):
            part_copy(step).start()
        for _, first, _ in lines:
            first()
        flow.start(1)
        flow.start(0)
        for step in range(1, rows):
            part_copy(step).wait()
        total = bias_ref[...]
        for index in range(rows):
            gap = lax.rem(row - index + rows, rows)
            theirs = parts[jnp.maximum(gap - 1, 0)]
            total = total + jnp.where(gap == 0, table_ref[...], theirs)
        mods_ref[place] = total

        def mod_copy(step):
            return send(
                mods_ref.at[place],
                mods_ref.at[place],
                ms.at[rows - 2 + step],
                mr.at[rows - 2 + step],
                "col",
                lax.rem(place + step, cols),
            )

        for step in range(1, cols):
            mod_copy(step).start()
        for own in owns:
            own.settle()
        flow.relay_y(0)
        for line, _, _ in lines:
            line.arrive(0)
            line.start(1)
        flow.relay_y(1)
        flow.relay_x(0)
        for step in range(2, cols - 1):
            for line, _, _ in lines:
                line.arrive(step - 1)
                line.start(step)
        flow.relay_y(2)
        flow.relay_x(1)
        flow.relay_y(3)
        flow.relay_x(2)
        flow.relay_x(3)
        for line, _, _ in lines:
            line.arrive(cols - 2)
        for step in range(1, cols):
            source_place = lax.rem(place - step + cols, cols)
            at = mods_ref.at[source_place]
            send(at, at, ms.at[rows - 2 + step], mr.at[rows - 2 + step], "col", source_place).wait_recv()
            mod_copy(step).wait_send()
        for line, _, _ in lines:
            line.finish()
        flow.finish()
        for own in owns:
            own.finish()

    return communicate(
        kernel,
        "prologue",
        0,
        out_shape=[struct(s, BF) for s in full_shapes] + [struct((cols,) + table_shape, F32)],
        in_specs=[ANY] * 4 + [VM, VM],
        out_specs=[ANY] * 4 + [VM],
        scratch_shapes=[pltpu.VMEM(s.shape, BF) for s in shards]
        + [
            pltpu.VMEM((rows - 1,) + table_shape, F32),
            pltpu.SemaphoreType.DMA((4,)),
            pltpu.SemaphoreType.DMA((4,)),
            pltpu.SemaphoreType.DMA((2, 2, cols - 1)),
            pltpu.SemaphoreType.DMA((2, 2, cols - 1)),
            pltpu.SemaphoreType.DMA(WeightFlow.sem_shape(2, 1)),
            pltpu.SemaphoreType.DMA(WeightFlow.sem_shape(2, 1)),
            pltpu.SemaphoreType.DMA((rows + cols - 2,)),
            pltpu.SemaphoreType.DMA((rows + cols - 2,)),
        ],
    )(*shards, table, bias)


def gather_keys(cols, kv_img, kv_txt, cot_img, cot_txt):
    two, seqs, img, width = kv_img.shape
    txt = kv_txt.shape[2]
    cots = (cot_img, cot_txt)

    def kernel(*refs):
        img_ref, txt_ref = refs[:2]
        cot_refs = refs[2:4]
        all_ref = refs[4]
        cot_full = refs[5:7]
        stage_img, stage_txt = refs[7:9]
        stage_cot = refs[9:11]
        local, ss, rs, zs, zr = refs[11:]
        row = lax.axis_index("row")
        place = lax.axis_index("col")
        sib, far = flip(row), flip_far(row)
        ins = [
            pltpu.make_async_copy(img_ref, stage_img, local.at[0]),
            pltpu.make_async_copy(txt_ref, stage_txt, local.at[1]),
        ]
        for copy in ins:
            copy.start()
        lines = [line_from(cot_refs[n], cot_full[n], width, cols, place, zs.at[n], zr.at[n]) for n in range(2)]
        owns = [
            OwnCopy(cot_refs[n], stage_cot[n], lines[n][2], local.at[6 + n], local.at[8 + n]) for n in range(2)
        ]
        for own in owns:
            own.begin()

        def img_at(block, index):
            return all_ref.at[block, index, :, pl.ds(0, img), :]

        def txt_at(block, index):
            return all_ref.at[block, index, :, pl.ds(img, txt), :]

        greet(others("row", 4) + others("col", cols))

        def direct(kind, index):
            peer = far if kind == 0 else sib
            return [
                send(img_ref.at[index], img_at(row, index), ss.at[kind, index, 0], rs.at[kind, index, 0], "row", peer),
                send(txt_ref.at[index], txt_at(row, index), ss.at[kind, index, 1], rs.at[kind, index, 1], "row", peer),
            ]

        def onward(index, block):
            return [
                send(img_at(block, index), img_at(block, index), ss.at[2, index, 0], rs.at[2, index, 0], "row", sib),
                send(txt_at(block, index), txt_at(block, index), ss.at[2, index, 1], rs.at[2, index, 1], "row", sib),
            ]

        def land(kind, index, block):
            for number, at in ((0, img_at(block, index)), (1, txt_at(block, index))):
                send(at, at, ss.at[kind, index, number], rs.at[kind, index, number], "row", sib).wait_recv()

        for kind in range(2):
            for index in range(2):
                for copy in direct(kind, index):
                    copy.start()
        for _, first, _ in lines:
            first()
        for copy in ins:
            copy.wait()
        outs = []
        for index in range(2):
            outs.append(pltpu.make_async_copy(stage_img.at[index], img_at(row, index), local.at[2 + index]))
            outs.append(pltpu.make_async_copy(stage_txt.at[index], txt_at(row, index), local.at[4 + index]))
        for copy in outs:
            copy.start()
        for own in owns:
            own.settle()
        land(0, 0, far)
        for copy in onward(0, far):
            copy.start()
        for line, _, _ in lines:
            line.arrive(0)
            line.start(1)
        land(0, 1, far)
        for copy in onward(1, far):
            copy.start()
        for step in range(2, cols - 1):
            for line, _, _ in lines:
                line.arrive(step - 1)
                line.start(step)
        for index in range(2):
            land(1, index, sib)
            land(2, index, flip(far))
        for line, _, _ in lines:
            line.arrive(cols - 2)
        for line, _, _ in lines:
            line.finish()
        for index in range(2):
            for kind in range(2):
                for copy in direct(kind, index):
                    copy.wait_send()
            for copy in onward(index, far):
                copy.wait_send()
        for copy in outs:
            copy.wait()
        for own in owns:
            own.finish()

    return communicate(
        kernel,
        "gather_keys",
        1,
        out_shape=[struct((4, two, seqs, img + txt, width), BF)]
        + [struct(c.shape[:2] + (width * cols,), BF) for c in cots],
        in_specs=[ANY] * 4,
        out_specs=[ANY] * 3,
        scratch_shapes=[
            pltpu.VMEM(kv_img.shape, BF),
            pltpu.VMEM(kv_txt.shape, BF),
            pltpu.VMEM(cot_img.shape, BF),
            pltpu.VMEM(cot_txt.shape, BF),
            pltpu.SemaphoreType.DMA((10,)),
            pltpu.SemaphoreType.DMA((3, 2, 2)),
            pltpu.SemaphoreType.DMA((3, 2, 2)),
            pltpu.SemaphoreType.DMA((2, 2, cols - 1)),
            pltpu.SemaphoreType.DMA((2, 2, cols - 1)),
        ],
    )(kv_img, kv_txt, cot_img, cot_txt)


def attend(q_img, q_txt, keys):
    seqs, img, width = q_img.shape
    txt = q_txt.shape[1]
    tokens = img + txt
    blocks = keys.shape[0]
    pairs = width // (2 * HD)
    scale = HD ** (-0.5)

    def kernel(qi_ref, qt_ref, k_ref, v_ref, oi_ref, ot_ref, lse_ref):
        queries = jnp.concatenate([qi_ref[...], qt_ref[...]], axis=0)
        key_block = k_ref[...].reshape(blocks * tokens, 2 * HD)
        value_block = v_ref[...].reshape(blocks * tokens, 2 * HD)
        low = lax.broadcasted_iota(jnp.int32, (tokens, 2 * HD), 1) < HD
        results, sums = [], []
        for head in range(2):
            mine = low if head == 0 else jnp.logical_not(low)
            chosen = jnp.where(mine, queries, jnp.zeros_like(queries))
            scores = (
                lax.dot_general(
                    chosen, key_block, (((1,), (1,)), ((), ())), preferred_element_type=F32
                )
                * scale
            )
            highest = jnp.max(scores, axis=-1, keepdims=True)
            grown = jnp.exp(scores - highest)
            total = jnp.sum(grown, axis=-1, keepdims=True)
            weights = (grown * (1.0 / total)).astype(BF)
            results.append(jnp.dot(weights, value_block, preferred_element_type=F32))
            sums.append(jnp.broadcast_to(highest + jnp.log(total), (tokens, 2 * HD)))
        attended = jnp.where(low, results[0], results[1]).astype(BF)
        oi_ref[...] = attended[:img]
        ot_ref[...] = attended[img:]
        lse_ref[...] = jnp.where(low, sums[0], sums[1])

    lanes = 2 * HD
    q_img_spec = pl.BlockSpec((None, img, lanes), lambda s, h: (s, 0, h))
    q_txt_spec = pl.BlockSpec((None, txt, lanes), lambda s, h: (s, 0, h))
    return pl.pallas_call(
        kernel,
        name="attend",
        grid=(seqs, pairs),
        in_specs=[
            q_img_spec,
            q_txt_spec,
            pl.BlockSpec((blocks, None, None, tokens, lanes), lambda s, h: (0, 0, s, 0, h)),
            pl.BlockSpec((blocks, None, None, tokens, lanes), lambda s, h: (0, 1, s, 0, h)),
        ],
        out_specs=[
            q_img_spec,
            q_txt_spec,
            pl.BlockSpec((None, None, tokens, lanes), lambda s, h: (s, h, 0, 0)),
        ],
        out_shape=[
            struct(q_img.shape, BF),
            struct(q_txt.shape, BF),
            struct((seqs, pairs, tokens, lanes), F32),
        ],
        compiler_params=pltpu.CompilerParams(vmem_limit_bytes=VMEM_LIMIT),
    )(q_img, q_txt, keys, keys)


def attend_back(q_img, q_txt, keys, o_img, o_txt, do_img, do_txt, lse):
    seqs, img, width = q_img.shape
    txt = q_txt.shape[1]
    tokens = img + txt
    blocks = keys.shape[0]
    pairs = width // (2 * HD)
    lanes = 2 * HD
    scale = HD ** (-0.5)
    over_last = (((1,), (1,)), ((), ()))
    over_first = (((0,), (0,)), ((), ()))

    def kernel(qi, qt, k_ref, v_ref, oi, ot, di, dt, lse_ref, dqi, dqt, dk_ref, dv_ref):
        queries = jnp.concatenate([qi[...], qt[...]], axis=0)
        attended = jnp.concatenate([oi[...], ot[...]], axis=0)
        d_attended = jnp.concatenate([di[...], dt[...]], axis=0)
        key_block = k_ref[...].reshape(blocks * tokens, lanes)
        value_block = v_ref[...].reshape(blocks * tokens, lanes)
        low = lax.broadcasted_iota(jnp.int32, (tokens, lanes), 1) < HD
        product = d_attended.astype(F32) * attended.astype(F32)
        d_q = []
        d_k = jnp.zeros((blocks * tokens, lanes), F32)
        d_v = jnp.zeros((blocks * tokens, lanes), F32)
        for head in range(2):
            mine = low if head == 0 else jnp.logical_not(low)
            zero = jnp.zeros_like(queries)
            q_head = jnp.where(mine, queries, zero)
            d_head = jnp.where(mine, d_attended, zero)
            centre = jnp.sum(jnp.where(mine, product, 0.0), axis=-1, keepdims=True)
            log_total = lse_ref[:, head * HD : head * HD + 1]
            scores = (
                lax.dot_general(q_head, key_block, over_last, preferred_element_type=F32) * scale
            )
            weights = jnp.exp(scores - log_total)
            d_weights = lax.dot_general(d_head, value_block, over_last, preferred_element_type=F32)
            d_scores = (weights * (d_weights - centre)).astype(BF)
            d_v = d_v + lax.dot_general(
                weights.astype(BF), d_head, over_first, preferred_element_type=F32
            )
            d_k = d_k + lax.dot_general(d_scores, q_head, over_first, preferred_element_type=F32)
            d_q.append(jnp.dot(d_scores, key_block, preferred_element_type=F32))
        d_queries = (jnp.where(low, d_q[0], d_q[1]) * scale).astype(BF)
        dqi[...] = d_queries[:img]
        dqt[...] = d_queries[img:]
        dk_ref[...] = (d_k * scale).astype(BF).reshape(blocks, tokens, lanes)
        dv_ref[...] = d_v.astype(BF).reshape(blocks, tokens, lanes)

    img_spec = pl.BlockSpec((None, img, lanes), lambda s, h: (s, 0, h))
    txt_spec = pl.BlockSpec((None, txt, lanes), lambda s, h: (s, 0, h))
    sums = pl.BlockSpec((blocks, None, tokens, lanes), lambda s, h: (0, s, 0, h))
    return pl.pallas_call(
        kernel,
        name="attend_back",
        grid=(seqs, pairs),
        in_specs=[
            img_spec,
            txt_spec,
            pl.BlockSpec((blocks, None, None, tokens, lanes), lambda s, h: (0, 0, s, 0, h)),
            pl.BlockSpec((blocks, None, None, tokens, lanes), lambda s, h: (0, 1, s, 0, h)),
            img_spec,
            txt_spec,
            img_spec,
            txt_spec,
            pl.BlockSpec((None, None, tokens, lanes), lambda s, h: (s, h, 0, 0)),
        ],
        out_specs=[img_spec, txt_spec, sums, sums],
        out_shape=[
            struct(q_img.shape, BF),
            struct(q_txt.shape, BF),
            struct((blocks, seqs, tokens, width), BF),
            struct((blocks, seqs, tokens, width), BF),
        ],
        compiler_params=pltpu.CompilerParams(vmem_limit_bytes=VMEM_LIMIT),
    )(q_img, q_txt, keys, keys, o_img, o_txt, do_img, do_txt, lse)


OVER_FIRST = (((0,), (0,)), ((), ()))
OVER_LAST = (((1,), (1,)), ((), ()))


def chunk_rows(img, txt, size):
    spans = [(1, 0, txt)]
    for first in range(0, img, size):
        spans.append((0, first, min(size, img - first)))
    return spans


def line_buffers(spans, slots, width):
    bufs = []
    for _, _, size in spans:
        bufs += [pltpu.VMEM((2, slots, size, width), BF)] * 2
    return bufs


def line_reduces(spans, parts, cols, place, width, bufs, ss, rs):
    reduces = []
    for number, (which, first, size) in enumerate(spans):
        src = parts[which]

        def load(block, src=src, first=first, size=size):
            return src[pl.ds(first, size), aligned(block, width)]

        reduces.append(
            LineReduce(load, cols, place, bufs[2 * number], bufs[2 * number + 1], ss.at[number], rs.at[number])
        )
    return reduces


def line_gathers(spans, outs, cols, place, width, ss, rs):
    gathers = []
    for number, (which, first, size) in enumerate(spans):
        dst = outs[which]

        def at(block, dst=dst, first=first, size=size):
            return dst.at[pl.ds(first, size), aligned(block, width)]

        gathers.append(LineGather(at, cols, place, ss.at[number], rs.at[number]))
    return gathers


class LineSum:
    def __init__(self, spans, parts, outs, cols, place, width, bufs, sems):
        self.spans, self.outs, self.place, self.width = spans, outs, place, width
        self.slots = cols - 1
        self.reduces = line_reduces(spans, parts, cols, place, width, bufs, sems[0], sems[1])
        self.gathers = line_gathers(spans, outs, cols, place, width, sems[2], sems[3])
        self.turns = len(spans) + 2 * self.slots

    def advance(self, number, step):
        which, first, size = self.spans[number]
        dst = self.outs[which]
        slots = self.slots
        if step < slots:
            self.reduces[number].step(step)
        elif step == slots:

            def store(value):
                dst[pl.ds(first, size), aligned(self.place, self.width)] = value.astype(BF)

            self.reduces[number].total(store)
            self.gathers[number].start(0)
        elif step < 2 * slots:
            self.gathers[number].arrive(step - slots - 1)
            self.gathers[number].start(step - slots)
        else:
            self.gathers[number].arrive(slots - 1)

    def turn(self, turn):
        for number in range(len(self.spans)):
            step = turn - number
            if 0 <= step <= 2 * self.slots:
                self.advance(number, step)

    def finish(self):
        for number in range(len(self.spans)):
            self.reduces[number].finish()
            self.gathers[number].finish()


def sum_branch(cols, part_img, part_txt, w_up, w_down):
    img, full = part_img.shape
    txt = part_txt.shape[0]
    width = full // cols
    spans = chunk_rows(img, txt, img // 4)
    count = len(spans)
    slots = cols - 1
    kinds = ("up", "down")
    weights = (w_up, w_down)
    subs = 2

    def kernel(*refs):
        parts, refs = refs[:2], refs[2:]
        shards, refs = refs[:2], refs[2:]
        outs, refs = refs[:2], refs[2:]
        fulls, refs = refs[:2], refs[2:]
        stages, refs = refs[:2], refs[2:]
        bufs, refs = refs[: 2 * count], refs[2 * count :]
        sems, (local_in, local_out, ws, wr) = refs[:4], refs[4:]
        place = lax.axis_index("col")
        line = LineSum(spans, parts, outs, cols, place, width, bufs, sems)
        flow = WeightFlow(kinds, shards, fulls, subs, ws, wr)
        owns = [
            OwnCopy(shards[n], stages[n], flow.own_view(n), local_in.at[n], local_out.at[n]) for n in range(2)
        ]
        for own in owns:
            own.begin()
        greet(others("row", 4) + others("col", cols) + [("dp", flow.mate)])
        flow.start(1)
        line.turn(0)
        flow.start(0)
        for own in owns:
            own.settle()
        pieces = len(flow.pieces)
        y_next = x_next = 0
        for turn in range(1, line.turns):
            line.turn(turn)
            while y_next < pieces and y_next * line.turns <= (turn - 2) * pieces:
                flow.relay_y(y_next)
                y_next += 1
                if y_next >= 2:
                    flow.relay_x(x_next)
                    x_next += 1
        while x_next < pieces:
            if y_next < pieces:
                flow.relay_y(y_next)
                y_next += 1
            flow.relay_x(x_next)
            x_next += 1
        flow.finish()
        line.finish()
        for own in owns:
            own.finish()

    return communicate(
        kernel,
        "sum_branch",
        2,
        out_shape=[struct(part_img.shape, BF), struct(part_txt.shape, BF)]
        + [struct(gathered_shape(k, w.shape), BF) for k, w in zip(kinds, weights)],
        in_specs=[VM, VM, ANY, ANY],
        out_specs=[VM, VM, ANY, ANY],
        scratch_shapes=[pltpu.VMEM(w.shape, BF) for w in weights]
        + line_buffers(spans, slots, width)
        + [pltpu.SemaphoreType.DMA((count, 2, slots))] * 4
        + [pltpu.SemaphoreType.DMA((2,))] * 2
        + [pltpu.SemaphoreType.DMA(WeightFlow.sem_shape(2, subs))] * 2,
    )(part_img, part_txt, *weights)


class Sibling:
    def __init__(self, pairs, ss, rs):
        self.pairs, self.ss, self.rs = pairs, ss, rs

    def copy(self, number):
        src, dst = self.pairs[number]
        return send(src, dst, self.ss.at[number], self.rs.at[number], "row", flip(lax.axis_index("row")))

    def start(self):
        for number in range(len(self.pairs)):
            self.copy(number).start()

    def land(self, *numbers):
        for number in numbers:
            self.copy(number).wait_recv()

    def finish(self):
        for number in range(len(self.pairs)):
            self.copy(number).wait_send()


def row_parts(ref, buf, core):
    size = ref.shape[1] // 4
    return [(ref.at[:, aligned(2 * y + core, size)], buf.at[y]) for y in range(2)]


def token_product(left_own, left_sib, right_own, right_sib):
    return lax.dot_general(left_own, right_own, OVER_FIRST, preferred_element_type=F32) + lax.dot_general(
        left_sib, right_sib, OVER_FIRST, preferred_element_type=F32
    )


def sum_hidden(cols, back, hidden, d_pre, act, d_mlp, first_hidden, attended):
    img, full = back[0].shape
    txt = back[1].shape[0]
    tokens = (img, txt)
    width = full // cols
    units = d_pre[0].shape[1]
    block = full // 4
    spans = chunk_rows(img, txt, img // 4)
    count = len(spans)
    slots = cols - 1
    tile = 512 if units % 512 == 0 else units

    def kernel(*refs):
        parts, hid, pre, acts, mlp, one, att = (refs[2 * n : 2 * n + 2] for n in range(7))
        refs = refs[14:]
        outs, refs = refs[:2], refs[2:]
        up_own, up_far, down_near = refs[:3]
        one_sib, att_sib = refs[3:5], refs[5:7]
        refs = refs[7:]
        hid_sib, pre_sib, act_sib, mlp_sib = (refs[2 * n : 2 * n + 2] for n in range(4))
        refs = refs[8:]
        down_own, far_out, far_in = refs[:3]
        refs = refs[3:]
        bufs, refs = refs[: 2 * count], refs[2 * count :]
        sems, (ss, rs, ys, yr) = refs[:4], refs[4:]
        place = lax.axis_index("col")
        row = lax.axis_index("row")
        core, y_of = lax.rem(row, 2), row // 2
        other = 1 - core
        far = flip_far(row)
        line = LineSum(spans, parts, outs, cols, place, width, bufs, sems)
        pairs = []
        for s in range(2):
            pairs += [(acts[s], act_sib[s])] + row_parts(mlp[s], mlp_sib[s], other)
        for s in range(2):
            pairs += [(pre[s], pre_sib[s])] + row_parts(hid[s], hid_sib[s], other)
        for s in range(2):
            pairs += [(att[s], att_sib[s])] + row_parts(one[s], one_sib[s], other)
        sibling = Sibling(pairs, ss, rs)
        greet(others("row", 4) + others("col", cols))
        line.turn(0)
        sibling.start()
        line.turn(1)

        def down(s, y, write):
            right_own = mlp[s][:, aligned(2 * y + core, block)]
            right_sib = mlp_sib[s][y]

            @pl.loop(0, units // tile)
            def _(at):
                cut = aligned(at, tile)
                write(cut, token_product(acts[s][:, cut], act_sib[s][:, cut], right_own, right_sib))

        def up(s, y, write):
            left_own = hid[s][:, aligned(2 * y + core, block)]
            left_sib = hid_sib[s][y]

            @pl.loop(0, units // tile)
            def _(at):
                cut = aligned(at, tile)
                write(cut, token_product(left_own, left_sib, pre[s][:, cut], pre_sib[s][:, cut]))

        def across(s):
            return send(far_out.at[s], far_in.at[s], ys.at[s], yr.at[s], "row", far)

        def down_to_far(s):
            sibling.land(3 * s, 3 * s + 1, 3 * s + 2)

            def write(cut, value):
                far_out[s, cut, :] = value.astype(BF)

            down(s, 1 - y_of, write)
            across(s).start()

        def down_here(s):
            def write(cut, value):
                down_own[s, cut, :] = value

            down(s, y_of, write)

        def up_to_far(s):
            sibling.land(6 + 3 * s, 7 + 3 * s, 8 + 3 * s)

            def write(cut, value):
                up_far[s, :, cut] = value.astype(BF)

            up(s, 1 - y_of, write)

        def up_here(s):
            def write(cut, value):
                up_own[s, :, cut] = value

            up(s, y_of, write)

        def down_sum(s):
            across(s).wait_recv()

            @pl.loop(0, units // tile)
            def _(at):
                cut = aligned(at, tile)
                down_near[s, cut, :] = (down_own[s, cut, :] + far_in[s, cut, :].astype(F32)).astype(BF)

        work = {
            1: lambda: down_to_far(0),
            2: lambda: down_to_far(1),
            3: lambda: down_here(0),
            4: lambda: (down_here(1), up_to_far(1)),
            5: lambda: up_to_far(0),
            6: lambda: up_here(0),
            7: lambda: up_here(1),
            8: lambda: down_sum(0),
        }
        for turn in range(1, line.turns):
            if turn > 1:
                line.turn(turn)
            if turn in work:
                work[turn]()
        down_sum(1)
        sibling.land(*range(12, 18))
        sibling.finish()
        for s in range(2):
            across(s).wait_send()
        line.finish()

    arrays = list(back) + list(hidden) + list(d_pre) + list(act) + list(d_mlp) + list(first_hidden) + list(attended)
    return communicate(
        kernel,
        "sum_hidden",
        3,
        out_shape=[struct(b.shape, BF) for b in back]
        + [
            struct((2, block, units), F32),
            struct((2, block, units), BF),
            struct((2, units, block), BF),
        ]
        + [struct((2, t, block), BF) for t in tokens]
        + [struct(a.shape, BF) for a in attended],
        in_specs=[VM] * 10 + [ANY] * 4,
        out_specs=[VM] * 5 + [ANY] * 4,
        scratch_shapes=[pltpu.VMEM((2, t, block), BF) for t in tokens]
        + [pltpu.VMEM((t, units), BF) for t in tokens]
        + [pltpu.VMEM((t, units), BF) for t in tokens]
        + [pltpu.VMEM((2, t, block), BF) for t in tokens]
        + [
            pltpu.VMEM((2, units, block), F32),
            pltpu.VMEM((2, units, block), BF),
            pltpu.VMEM((2, units, block), BF),
        ]
        + line_buffers(spans, slots, width)
        + [pltpu.SemaphoreType.DMA((count, 2, slots))] * 4
        + [pltpu.SemaphoreType.DMA((18,))] * 2
        + [pltpu.SemaphoreType.DMA((2,))] * 2,
    )(*arrays)


class GradFlow:
    def __init__(self, pods, product, outs, far_out, far_in, pod_out, pod_in, ys, yr, xs, xr):
        self.pods, self.product, self.outs = pods, product, outs
        self.far_out, self.far_in, self.pod_out, self.pod_in = far_out, far_in, pod_out, pod_in
        self.ys, self.yr, self.xs, self.xr = ys, yr, xs, xr
        row = lax.axis_index("row")
        self.y_of, self.far = row // 2, flip_far(row)

    @staticmethod
    def rounds(pods):
        return pods.bit_length() - 1

    @staticmethod
    def scratch(pods, count, shape):
        rounds = GradFlow.rounds(pods)
        return (
            [pltpu.VMEM((count,) + shape, BF)] * 2
            + [pltpu.VMEM((count, rounds) + shape, BF)] * 2
            + [pltpu.SemaphoreType.DMA((count,))] * 2
            + [pltpu.SemaphoreType.DMA((count, rounds))] * 2
        )

    def across(self, piece):
        return send(
            self.far_out.at[piece], self.far_in.at[piece], self.ys.at[piece], self.yr.at[piece], "row", self.far
        )

    def over(self, piece, turn):
        pod = lax.axis_index("dp")
        step = 2**turn
        peer = pod + step - 2 * step * lax.rem(pod // step, 2)
        return send(
            self.pod_out.at[piece, turn],
            self.pod_in.at[piece, turn],
            self.xs.at[piece, turn],
            self.xr.at[piece, turn],
            "dp",
            peer,
        )

    def to_far(self, piece):
        self.far_out[piece] = self.product(piece, 1 - self.y_of).astype(BF)
        self.across(piece).start()

    def here(self, piece):
        self.outs(piece)[...] = self.product(piece, self.y_of)

    def to_pod(self, piece):
        self.across(piece).wait_recv()
        self.pod_out[piece, 0] = (self.outs(piece)[...] + self.far_in[piece].astype(F32)).astype(BF)
        self.over(piece, 0).start()

    def done(self, piece):
        rounds = self.rounds(self.pods)
        for turn in range(rounds):
            self.over(piece, turn).wait_recv()
            total = self.pod_out[piece, turn].astype(F32) + self.pod_in[piece, turn].astype(F32)
            if turn == rounds - 1:
                self.outs(piece)[...] = total
            else:
                self.pod_out[piece, turn + 1] = total.astype(BF)
                self.over(piece, turn + 1).start()

    def finish(self, piece):
        self.across(piece).wait_send()
        for turn in range(self.rounds(self.pods)):
            self.over(piece, turn).wait_send()

    @staticmethod
    def friends(pods):
        pod = lax.axis_index("dp")
        found = []
        for turn in range(GradFlow.rounds(pods)):
            step = 2**turn
            found.append(("dp", pod + step - 2 * step * lax.rem(pod // step, 2)))
        return found


def sum_keys(pods, cols, d_key, d_value, part_img, part_txt, img, attended, attended_sib, d_branch):
    blocks, seqs, tokens, width = d_key.shape
    txt = tokens - img
    img_rows, full = part_img.shape
    block = full // 4
    spans = chunk_rows(img_rows, part_txt.shape[0], img_rows // 4)
    count = len(spans)
    slots = cols - 1
    lots = [(which, seq) for which in range(2) for seq in range(seqs)]
    lot_count = len(lots)

    def kernel(*refs):
        dk_ref, dv_ref = refs[:2]
        parts = refs[2:4]
        att, att_sib, bra = refs[4:6], refs[6:8], refs[8:10]
        kv_img, kv_txt = refs[10:12]
        line_out = refs[12:14]
        grad_ref = refs[14]
        near_in, far_out, far_in, ns, nr, fs, fr = refs[15:22]
        bra_sib = refs[22:24]
        ss, rs = refs[24:26]
        grad_scratch = refs[26:34]
        refs = refs[34:]
        bufs, refs = refs[: 2 * count], refs[2 * count :]
        rss, rsr = refs
        row = lax.axis_index("row")
        place = lax.axis_index("col")
        core = lax.rem(row, 2)
        sib, far = flip(row), flip_far(row)
        sources = (dk_ref, dv_ref)
        reduces = line_reduces(spans, parts, cols, place, width, bufs, rss, rsr)
        sibling = Sibling(
            [pair for s in range(2) for pair in row_parts(bra[s], bra_sib[s], 1 - core)], ss, rs
        )

        def product(s, y):
            return token_product(
                att[s][...], att_sib[s][...], bra[s][:, aligned(2 * y + core, block)], bra_sib[s][y]
            )

        grads = GradFlow(pods, product, lambda s: grad_ref.at[s], *grad_scratch)
        greet(others("row", 4) + others("col", cols) + GradFlow.friends(pods))

        def near(lot, number):
            which, seq = lots[lot]
            target = flip(far) if number == 0 else sib
            return send(
                sources[which].at[target, seq],
                near_in.at[lot, number],
                ns.at[lot, number],
                nr.at[lot, number],
                "row",
                sib,
            )

        def across(lot):
            return send(far_out.at[lot], far_in.at[lot], fs.at[lot], fr.at[lot], "row", far)

        for lot in range(lot_count):
            near(lot, 0).start()
        sibling.start()
        for lot in range(lot_count):
            near(lot, 1).start()

        def line_step(number, step):
            which, first, size = spans[number]
            dst = line_out[which]
            if step < slots:
                reduces[number].step(step)
            else:

                def store(value):
                    dst[pl.ds(first, size), :] = value

                reduces[number].total(store)

        def near_step(lot):
            which, seq = lots[lot]
            near(lot, 0).wait_recv()
            far_out[lot] = (sources[which][far, seq].astype(F32) + near_in[lot, 0].astype(F32)).astype(BF)
            across(lot).start()

        def far_step(lot):
            which, seq = lots[lot]
            near(lot, 1).wait_recv()
            across(lot).wait_recv()
            total = (
                sources[which][row, seq].astype(F32)
                + near_in[lot, 1].astype(F32)
                + far_in[lot].astype(F32)
            ).astype(BF)
            kv_img[which, seq] = total[:img]
            kv_txt[which, seq] = total[img:]

        for number in range(count):
            line_step(number, 0)
        for lot in range(lot_count):
            near_step(lot)
        sibling.land(0, 1, 2, 3)
        for s in range(2):
            grads.to_far(s)
        for turn in range(1, slots):
            for number in range(count):
                line_step(number, turn)
            if turn == 1:
                for s in range(2):
                    grads.here(s)
            far_step(turn - 1)
        for lot in range(slots - 1, lot_count):
            far_step(lot)
        for s in range(2):
            grads.to_pod(s)
        for number in range(count):
            line_step(number, slots)
        for s in range(2):
            grads.done(s)
        sibling.finish()
        for lot in range(lot_count):
            for number in range(2):
                near(lot, number).wait_send()
            across(lot).wait_send()
        for number in range(count):
            reduces[number].finish()
        for s in range(2):
            grads.finish(s)

    return communicate(
        kernel,
        "sum_keys",
        4,
        out_shape=[
            struct((2, seqs, img, width), BF),
            struct((2, seqs, txt, width), BF),
            struct((img_rows, width), F32),
            struct((part_txt.shape[0], width), F32),
            struct((2, width, block), F32),
        ],
        in_specs=[VM] * 10,
        out_specs=[VM] * 5,
        scratch_shapes=[
            pltpu.VMEM((lot_count, 2, tokens, width), BF),
            pltpu.VMEM((lot_count, tokens, width), BF),
            pltpu.VMEM((lot_count, tokens, width), BF),
            pltpu.SemaphoreType.DMA((lot_count, 2)),
            pltpu.SemaphoreType.DMA((lot_count, 2)),
            pltpu.SemaphoreType.DMA((lot_count,)),
            pltpu.SemaphoreType.DMA((lot_count,)),
        ]
        + [pltpu.VMEM((2, b.shape[0], block), BF) for b in d_branch]
        + [pltpu.SemaphoreType.DMA((4,))] * 2
        + GradFlow.scratch(pods, 2, (width, block))
        + line_buffers(spans, slots, width)
        + [pltpu.SemaphoreType.DMA((count, 2, slots))] * 2,
    )(d_key, d_value, part_img, part_txt, *attended, *attended_sib, *d_branch)


def sum_last(
    pods, cols, d_q, d_kv, qkv, hidden, hidden_sib, xs, cots, branch, d_two, mlp, stat_cols, tables, b_down, up_rows, ada
):
    seqs = tables.shape[2]
    tokens = [x.shape[0] for x in xs]
    counts = [t // seqs for t in tokens]
    width = xs[0].shape[1]
    full = width * cols
    block = full // 4
    spans = chunk_rows(tokens[0], tokens[1], tokens[0] // 4)
    count = len(spans)
    slots = cols - 1
    pieces = [(s, k) for s in range(2) for k in range(3)]
    lanes = tokens[0] + 128
    firsts = (0, tokens[0])
    mods_rows = 2 * seqs * 6
    up_count = up_rows.shape[0]
    pack_rows = mods_rows + 8 + up_count

    def kernel(*refs):
        takes = iter(refs)

        def two():
            return (next(takes), next(takes))

        dq, dkv = two(), two()
        qkv_ref = next(takes)
        hid, hid_sib, x_ref, cot_ref, bra, dtwo, mlp_ref, stat = (two() for _ in range(8))
        table_ref, down_ref, up_ref, ada_ref = (next(takes) for _ in range(4))
        out_ref, dx_ref = two(), two()
        grad_ref, every_ref, silu_ref = (next(takes) for _ in range(3))
        dq_sib, dkv_sib, parts, d_one, grown = (two() for _ in range(5))
        sums_mine, sums_in, pack_mine, pack_in, silu_mine, silu_in = (next(takes) for _ in range(6))
        ss, rs, ms, mr, ps, pr, es, er, cs, cr = (next(takes) for _ in range(10))
        grad_scratch = [next(takes) for _ in range(8)]
        bufs = [next(takes) for _ in range(2 * count)]
        rss, rsr = next(takes), next(takes)
        row = lax.axis_index("row")
        place = lax.axis_index("col")
        pod = lax.axis_index("dp")
        core = lax.rem(row, 2)
        mine = aligned(place, width)
        reduces = line_reduces(spans, parts, cols, place, width, bufs, rss, rsr)
        sibling = Sibling([pair for s in range(2) for pair in ((dq[s], dq_sib[s]), (dkv[s], dkv_sib[s]))], ss, rs)

        def projected(own, s, k):
            return own[0][s][...] if k == 0 else own[1][s][k - 1]

        def product(piece, y):
            s, k = pieces[piece]
            return token_product(
                hid[s][:, aligned(2 * y + core, block)],
                hid_sib[s][y],
                projected((dq, dkv), s, k),
                projected((dq_sib, dkv_sib), s, k),
            )

        def out_view(piece):
            s, k = pieces[piece]
            return grad_ref.at[s, k]

        grads = GradFlow(pods, product, out_view, *grad_scratch)
        greet(others("col", cols) + others("row", 4) + others("dp", pods))
        sibling.start()

        for number, (s, first, size) in enumerate(spans):
            rows = pl.ds(first, size)
            term = lax.dot_general(dq[s][rows, :], qkv_ref[s, 0], OVER_LAST, preferred_element_type=F32)
            for k in range(2):
                term = term + lax.dot_general(
                    dkv[s][k, rows, :], qkv_ref[s, k + 1], OVER_LAST, preferred_element_type=F32
                )
            parts[s][rows, :] = term.astype(BF)
            reduces[number].step(0)
        for s in range(2):
            sibling.land(2 * s, 2 * s + 1)
            for k in range(3):
                grads.to_far(3 * s + k)
        for number in range(count):
            reduces[number].step(1)
        for piece in range(6):
            grads.here(piece)

        def segment(s, q):
            return pl.ds(q * counts[s], counts[s])

        def modulation(s, q, position):
            return table_ref[place, s, q, pl.ds(position, 1), :]

        def put(index, value):
            pack_mine[pl.ds(index, 1), :] = value

        def over_tokens(value):
            return jnp.sum(value, axis=0, keepdims=True)

        def early(s):
            d_out = d_down = None
            for q in range(seqs):
                rows = segment(s, q)
                at = (s * seqs + q) * 6
                column = stat[s][rows, :]
                cot = cot_ref[s][rows, :].astype(F32)
                d_hidden = dtwo[s][rows, mine].astype(F32)
                attn = bra[s][rows, mine].astype(F32) + modulation(s, q, 6)
                gate_a, gate_m = modulation(s, q, 2), modulation(s, q, 5)
                middle = x_ref[s][rows, :].astype(F32) + gate_a * attn
                mlp_branch = mlp_ref[s][rows, :] + down_ref[pl.ds(s, 1), :]
                out_ref[s][rows, :] = (middle + gate_m * mlp_branch).astype(BF)
                normed = (middle - column[:, 2:3]) * column[:, 3:4]
                d_normed = d_hidden * (1.0 + modulation(s, q, 4))
                d_middle = cot + column[:, 3:4] * (d_normed - column[:, 4:5] - normed * column[:, 5:6])
                dx_ref[s][rows, :] = d_middle
                put(at + 2, over_tokens(d_middle * attn))
                put(at + 3, over_tokens(d_hidden))
                put(at + 4, over_tokens(d_hidden * normed))
                put(at + 5, over_tokens(cot * mlp_branch))
                first, second = over_tokens(d_middle * gate_a), over_tokens(cot * gate_m)
                d_out = first if d_out is None else d_out + first
                d_down = second if d_down is None else d_down + second
            put(mods_rows + 4 + s, d_out)
            put(mods_rows + 6 + s, d_down)
            put(mods_rows + 2 * s, over_tokens(dq[s][...].astype(F32)))
            put(mods_rows + 2 * s + 1, over_tokens(dkv[s][1].astype(F32)))

        pack_mine[pl.ds(mods_rows + 8, up_count), :] = up_ref[...]
        early(1)
        for number in range(count):
            for turn in range(2, slots):
                reduces[number].step(turn)
        early(0)
        grads.to_pod(0)
        grads.to_pod(1)
        for number, (s, first, size) in enumerate(spans):

            def store(value, s=s, first=first, size=size):
                d_one[s][pl.ds(first, size), :] = value

            reduces[number].total(store)

        one_row = lax.broadcasted_iota(jnp.int32, (8, width), 0)
        pick = [jnp.where(one_row == k, 1.0, 0.0).astype(F32) for k in range(2)]
        for s in range(2):
            for q in range(seqs):
                rows = segment(s, q)
                at = (s * seqs + q) * 6
                column = stat[s][rows, :]
                normed = (x_ref[s][rows, :].astype(F32) - column[:, 0:1]) * column[:, 1:2]
                d_hidden = d_one[s][rows, :]
                put(at, over_tokens(d_hidden))
                put(at + 1, over_tokens(d_hidden * normed))
                value = d_hidden * (1.0 + modulation(s, q, 1))
                d_one[s][rows, :] = value
                grown[s][rows, :] = value * normed
            exact = lax.Precision.HIGHEST
            sums_mine[:, pl.ds(firsts[s], tokens[s])] = lax.dot_general(
                pick[0], d_one[s][...], OVER_LAST, precision=exact, preferred_element_type=F32
            ) + lax.dot_general(pick[1], grown[s][...], OVER_LAST, precision=exact, preferred_element_type=F32)

        def small(step):
            return send(
                sums_mine, sums_in.at[step - 1], ms.at[step - 1], mr.at[step - 1], "col", lax.rem(place + step, cols)
            )

        for step in range(1, cols):
            small(step).start()

        def pack_copy(step):
            return send(
                pack_mine, pack_in.at[step - 1], ps.at[step - 1], pr.at[step - 1], "row", lax.rem(row + step, 4)
            )

        for step in range(1, 4):
            pack_copy(step).start()
        grads.to_pod(2)
        total = sums_mine[...]
        for step in range(1, cols):
            small(step).wait()
            total = total + sums_in[step - 1]
        lane = lax.broadcasted_iota(jnp.int32, (8, 128), 1)
        sublane = lax.broadcasted_iota(jnp.int32, (8, 128), 0)
        spread = jnp.where(sublane == lane // HD, 1.0 / full, 0.0).astype(F32)
        for s in range(2):
            means = lax.dot_general(
                total[:, firsts[s] : firsts[s] + tokens[s]],
                spread,
                OVER_FIRST,
                precision=lax.Precision.HIGHEST,
                preferred_element_type=F32,
            )
            column = stat[s][...]
            normed = (x_ref[s][...].astype(F32) - column[:, 0:1]) * column[:, 1:2]
            dx_ref[s][...] = dx_ref[s][...] + column[:, 1:2] * (
                d_one[s][...] - means[:, 0:1] - normed * means[:, HD : HD + 1]
            )
        grads.to_pod(3)

        def ordered(own, theirs, index, size):
            value = jnp.zeros_like(own)
            for number in range(size):
                gap = lax.rem(index - number + size, size)
                value = value + jnp.where(gap == 0, own, theirs[jnp.maximum(gap - 1, 0)])
            return value

        for step in range(1, 4):
            pack_copy(step).wait()
        packed = ordered(pack_mine[...], pack_in, row, 4)
        every_ref[pod] = packed

        def every_copy(step):
            at = every_ref.at[pod]
            return send(at, at, es.at[step - 1], er.at[step - 1], "dp", lax.rem(pod + step, pods))

        for step in range(1, pods):
            every_copy(step).start()
        d_silu = jnp.zeros((8, width), F32)
        for s in range(2):
            for k in range(6):
                rows = [packed[(s * seqs + q) * 6 + k : (s * seqs + q) * 6 + k + 1] for q in range(seqs)]
                value = jnp.concatenate(rows, axis=0)
                high = value.astype(BF)
                rest = value - high.astype(F32)
                mid = rest.astype(BF)
                low = (rest - mid.astype(F32)).astype(BF)
                terms = jnp.concatenate(
                    [high.astype(F32), mid.astype(F32), low.astype(F32), jnp.zeros((8 - 3 * seqs, width), F32)], axis=0
                ).astype(BF)
                d_silu = d_silu + lax.dot_general(terms, ada_ref[s, k], OVER_LAST, preferred_element_type=F32)
        silu_mine[...] = d_silu[:seqs] + d_silu[seqs : 2 * seqs] + d_silu[2 * seqs : 3 * seqs]

        def silu_copy(step):
            return send(
                silu_mine, silu_in.at[step - 1], cs.at[step - 1], cr.at[step - 1], "col", lax.rem(place + step, cols)
            )

        for step in range(1, cols):
            silu_copy(step).start()
        for piece in (4, 5):
            grads.to_pod(piece)
        for step in range(1, cols):
            silu_copy(step).wait()
        silu_ref[...] = ordered(silu_mine[...], silu_in, place, cols)
        for piece in range(6):
            grads.done(piece)
        for step in range(1, pods):
            source = lax.rem(pod - step + pods, pods)
            at = every_ref.at[source]
            send(at, at, es.at[step - 1], er.at[step - 1], "dp", source).wait_recv()
            every_copy(step).wait_send()
        sibling.finish()
        for number in range(count):
            reduces[number].finish()
        for piece in range(6):
            grads.finish(piece)

    arrays = (
        list(d_q)
        + list(d_kv)
        + [qkv]
        + list(hidden)
        + list(hidden_sib)
        + list(xs)
        + list(cots)
        + list(branch)
        + list(d_two)
        + list(mlp)
        + list(stat_cols)
        + [tables, b_down, up_rows, ada]
    )
    dma = pltpu.SemaphoreType.DMA
    return communicate(
        kernel,
        "sum_last",
        5,
        out_shape=[struct((t, width), BF) for t in tokens]
        + [struct((t, width), F32) for t in tokens]
        + [
            struct((2, 3, block, width), F32),
            struct((pods, pack_rows, width), F32),
            struct((seqs, width), F32),
        ],
        in_specs=[VM] * len(arrays),
        out_specs=[VM] * 7,
        scratch_shapes=[pltpu.VMEM(a.shape, BF) for a in d_q]
        + [pltpu.VMEM(a.shape, BF) for a in d_kv]
        + [pltpu.VMEM((t, full), BF) for t in tokens]
        + [pltpu.VMEM((t, width), F32) for t in tokens] * 2
        + [
            pltpu.VMEM((8, lanes), F32),
            pltpu.VMEM((slots, 8, lanes), F32),
            pltpu.VMEM((pack_rows, width), F32),
            pltpu.VMEM((3, pack_rows, width), F32),
            pltpu.VMEM((seqs, width), F32),
            pltpu.VMEM((slots, seqs, width), F32),
        ]
        + [dma((4,))] * 2
        + [dma((slots,))] * 2
        + [dma((3,))] * 2
        + [dma((pods - 1,))] * 2
        + [dma((slots,))] * 2
        + GradFlow.scratch(pods, 6, (block, width))
        + line_buffers(spans, slots, width)
        + [dma((count, 2, slots))] * 2,
    )(*arrays)


def gelu_pair(inputs):
    inner = GELU_ROOT * (inputs + GELU_CUBIC * inputs * inputs * inputs)
    tanh_value = jnp.tanh(inner)
    result = 0.5 * inputs * (1.0 + tanh_value)
    derivative = 0.5 * (1.0 + tanh_value) + 0.5 * inputs * (
        1.0 - tanh_value * tanh_value
    ) * GELU_ROOT * (1.0 + 3.0 * GELU_CUBIC * inputs * inputs)
    return (result, derivative)


def stats(values):
    mean = jnp.mean(values, axis=-1, keepdims=True)
    centred = values - mean
    inverse = lax.rsqrt(jnp.mean(centred * centred, axis=-1, keepdims=True) + EPSILON)
    return mean, inverse


def dot_f32(left, right):
    return jnp.einsum("td,de->te", left, right, preferred_element_type=F32)


def dot_back(left, right):
    return jnp.einsum("te,de->td", left, right, preferred_element_type=F32)


def dot_tokens(left, right):
    return jnp.einsum("td,te->de", left, right, preferred_element_type=F32)


def local(
    dp_count,
    row_count,
    col_count,
    x_img,
    x_txt,
    condition,
    w_qkv,
    b_qv,
    w_out,
    b_out,
    w_up,
    b_up,
    w_down,
    b_down,
    w_ada,
    b_ada,
    cot_img,
    cot_txt,
):
    seqs, img, width = x_img.shape
    txt = x_txt.shape[1]
    full = width * col_count
    counts = (img, txt)

    cond_wide = condition.astype(F32)
    cond_act = jax.nn.silu(cond_wide).astype(BF)
    ada = jnp.transpose(w_ada, (0, 2, 1, 3))
    table = jnp.einsum("sc,zkcd->zskd", cond_act, ada, preferred_element_type=F32)
    table = jnp.pad(table, ((0, 0), (0, 0), (0, 2), (0, 0)))
    bias_six = jnp.broadcast_to(b_ada[:, None], (2, seqs, 6, width))
    bias_rest = jnp.broadcast_to(b_out[:, None, None], (2, seqs, 2, width))
    *x_full, qkv_full, out_full, tables = prologue(
        col_count,
        x_img,
        x_txt,
        jnp.transpose(w_qkv, (0, 2, 1, 3)),
        w_out,
        table,
        jnp.concatenate([bias_six, bias_rest], axis=2),
    )
    wide = jnp.transpose(tables, (1, 2, 3, 0, 4)).reshape(2, seqs, 8, full)

    def mod(stream, position):
        return wide[stream, :, position][:, None, :]

    resid = [array.astype(F32) for array in x_full]
    stats_one = [stats(array) for array in resid]
    normed_one = [(resid[s] - stats_one[s][0]) * stats_one[s][1] for s in range(2)]
    hidden_one = [
        (normed_one[s] * (1.0 + mod(s, 1)) + mod(s, 0)).astype(BF).reshape(seqs * counts[s], full)
        for s in range(2)
    ]
    queries, keyed = [], []
    for s in range(2):
        shape = (seqs, counts[s], width)
        q = (dot_f32(hidden_one[s], qkv_full[s, 0]) + b_qv[s, 0]).astype(BF).reshape(shape)
        k = dot_f32(hidden_one[s], qkv_full[s, 1]).astype(BF).reshape(shape)
        v = (dot_f32(hidden_one[s], qkv_full[s, 2]) + b_qv[s, 1]).astype(BF).reshape(shape)
        queries.append(q)
        keyed.append(jnp.stack([k, v], axis=0))
    keys, *cot_full = gather_keys(col_count, keyed[0], keyed[1], cot_img, cot_txt)
    o_img, o_txt, lse = attend(queries[0], queries[1], keys)
    attended = [o_img.reshape(seqs * img, width), o_txt.reshape(seqs * txt, width)]
    out_terms = [dot_f32(attended[s], out_full[s]).astype(BF) for s in range(2)]
    *branch_sum, up_full, down_full = sum_branch(col_count, out_terms[0], out_terms[1], w_up, w_down)
    attn_branch = [
        branch_sum[s].reshape(seqs, counts[s], full).astype(F32) + mod(s, 6) for s in range(2)
    ]
    middle = [resid[s] + mod(s, 2) * attn_branch[s] for s in range(2)]
    stats_two = [stats(array) for array in middle]
    normed_two = [(middle[s] - stats_two[s][0]) * stats_two[s][1] for s in range(2)]
    hidden_two = [
        (normed_two[s] * (1.0 + mod(s, 4)) + mod(s, 3)).astype(BF).reshape(seqs * counts[s], full)
        for s in range(2)
    ]
    d_mlp_bf = [
        (cot_full[s].astype(F32) * mod(s, 5)).astype(BF).reshape(seqs * counts[s], full)
        for s in range(2)
    ]
    act, d_pre, d_pre_bf, down_terms, up_back = [], [], [], [], []
    for s in range(2):
        pre = dot_f32(hidden_two[s], up_full[s]) + b_up[s]
        value, slope = gelu_pair(pre)
        act.append(value.astype(BF))
        d_pre.append(dot_back(d_mlp_bf[s], down_full[s]) * slope)
        d_pre_bf.append(d_pre[s].astype(BF))
        up_back.append(dot_back(d_pre_bf[s], up_full[s]).astype(BF))
        down_terms.append(dot_f32(act[s], down_full[s]).astype(BF))

    d_two_img, d_two_txt, up_own, up_far, down_near, *paired = sum_hidden(
        col_count, up_back, hidden_two, d_pre_bf, act, d_mlp_bf, hidden_one, attended
    )
    hidden_pairs, attended_pairs = paired[:2], paired[2:]

    far_perm = [(r, (r + 2) % 4) for r in range(row_count)]

    def pod_sum(rounded):
        step = 1
        while step < dp_count:
            perm = [(d, d ^ step) for d in range(dp_count)]
            value = rounded.astype(F32) + lax.ppermute(rounded, "dp", perm).astype(F32)
            rounded = value.astype(BF)
            step *= 2
        return value

    grad_down = pod_sum(down_near)
    up_near = (up_own + lax.ppermute(up_far, "row", far_perm).astype(F32)).astype(BF)

    d_hidden_two = [d_two_img, d_two_txt]
    d_hidden_two = [
        d_hidden_two[s].reshape(seqs, counts[s], full).astype(F32) for s in range(2)
    ]
    d_branch_bf, stat_cols = [], []
    for s in range(2):
        grown = d_hidden_two[s] * (1.0 + mod(s, 4))
        first = jnp.mean(grown, axis=-1, keepdims=True)
        second = jnp.mean(grown * normed_two[s], axis=-1, keepdims=True)
        d_middle = cot_full[s].astype(F32) + stats_two[s][1] * (grown - first - normed_two[s] * second)
        d_branch_bf.append((d_middle * mod(s, 2)).astype(BF).reshape(seqs * counts[s], full))
        columns = [*stats_one[s], *stats_two[s], first, second, jnp.zeros_like(first), jnp.zeros_like(first)]
        stat_cols.append(jnp.concatenate(columns, axis=-1).reshape(seqs * counts[s], 8))
    d_att = [
        dot_back(d_branch_bf[s], out_full[s]).astype(BF).reshape(seqs, counts[s], width)
        for s in range(2)
    ]
    dq_img, dq_txt, d_key, d_value = attend_back(
        queries[0], queries[1], keys, o_img, o_txt, d_att[0], d_att[1], lse
    )
    d_key, d_value, up_near = lax.optimization_barrier((d_key, d_value, up_near))
    grad_up = pod_sum(up_near)
    kv_img, kv_txt, mlp_img, mlp_txt, grad_out = sum_keys(
        dp_count,
        col_count,
        d_key,
        d_value,
        down_terms[0],
        down_terms[1],
        img,
        attended,
        attended_pairs,
        d_branch_bf,
    )

    flat = [(seqs * c, width) for c in counts]
    up_rows = jnp.concatenate([jnp.sum(d_pre[s], axis=0).reshape(-1, width) for s in range(2)], axis=0)
    out_img, out_txt, dx_img, dx_txt, grad_qkv, every, d_silu = sum_last(
        dp_count,
        col_count,
        [dq_img.reshape(flat[0]), dq_txt.reshape(flat[1])],
        [kv_img.reshape((2,) + flat[0]), kv_txt.reshape((2,) + flat[1])],
        qkv_full,
        hidden_one,
        hidden_pairs,
        [x_img.reshape(flat[0]), x_txt.reshape(flat[1])],
        [cot_img.reshape(flat[0]), cot_txt.reshape(flat[1])],
        branch_sum,
        [d_two_img, d_two_txt],
        [mlp_img, mlp_txt],
        stat_cols,
        tables,
        b_down,
        up_rows,
        ada,
    )
    grad_qkv = jnp.transpose(grad_qkv, (0, 2, 1, 3))
    mods_count = 2 * seqs * 6
    rest = jnp.sum(every[:, mods_count:], axis=0)
    grad_bqv = rest[:4].reshape(2, 2, width)
    grad_bout = rest[4:6]
    grad_bdown = rest[6:8]
    grad_bup = rest[8:].reshape(2, -1)
    all_mods = every[:, :mods_count].reshape(dp_count, 2, seqs, 6, width)
    all_cond = lax.all_gather(cond_act, "dp", axis=0, tiled=False).astype(F32)
    grad_ada = jnp.einsum(
        "psc,pzskd->zkcd", all_cond, all_mods, precision=lax.Precision.HIGHEST
    )
    grad_ada = jnp.transpose(grad_ada, (0, 2, 1, 3))
    grad_bada = jnp.sum(all_mods, axis=(0, 2))
    sigmoid_cond = jax.nn.sigmoid(cond_wide)
    d_condition = d_silu * sigmoid_cond * (1.0 + cond_wide * (1.0 - sigmoid_cond))
    return (
        out_img.reshape(x_img.shape),
        out_txt.reshape(x_txt.shape),
        dx_img.reshape(x_img.shape),
        dx_txt.reshape(x_txt.shape),
        d_condition,
        grad_qkv,
        grad_bqv,
        grad_out,
        grad_bout,
        grad_up,
        grad_bup,
        grad_down,
        grad_bdown,
        grad_ada,
        grad_bada,
    )


def solution(mesh):
    placed = (
        P("dp", "row", "col"),
        P("dp", "row", "col"),
        P("dp", "row"),
        P(None, "row", None, "col"),
        P(None, None, "col"),
        P(None, "col", "row"),
        P(None, "col"),
        P(None, "row", "col"),
        P(None, "col"),
        P(None, "col", "row"),
        P(None, "col"),
        P(None, "row", None, "col"),
        P(None, None, "col"),
        P("dp", "row", "col"),
        P("dp", "row", "col"),
    )
    return jax.shard_map(
        partial(local, mesh.shape["dp"], mesh.shape["row"], mesh.shape["col"]),
        mesh=mesh,
        in_specs=placed,
        out_specs=(
            P("dp", "row", "col"),
            P("dp", "row", "col"),
            P("dp", "row", "col"),
            P("dp", "row", "col"),
            P("dp", "row"),
            P(None, "row", None, "col"),
            P(None, None, "col"),
            P(None, "col", "row"),
            P(None, "col"),
            P(None, "row", "col"),
            P(None, "col"),
            P(None, "col", "row"),
            P(None, "col"),
            P(None, "row", None, "col"),
            P(None, None, "col"),
        ),
        check_vma=False,
    )
```

time: 1700 us -> 577 us (0.34)
  waiting for transfers between devices: 928 us -> 0.01 us
  Pallas kernels: 0 us -> 402 us
  local copies, waits for them, and re-layouts: 279 us -> 46.2 us
  blocking collectives: 166 us -> 4.34 us
  matrix products: 150 us -> 61.3 us
  starting transfers between devices: 89.8 us -> 2.45 us
    psum x1 -> x0, waiting for transfers between devices: 436 us -> none  [local(): lax.psum((grad_qkv, grad_bqv, grad_out, grad_bout, grad_up, grad_bup, gra...]
    pallas_call x0 -> x8, Pallas kernels: none -> 402 us  [the longest x1 79.3 us: sum_branch(): communicate(kernel, 'sum_branch', 2, out_shape=[struct(part_img.shape, BF...]
    all_gather x8 -> x0, waiting for transfers between devices: 209 us -> none  [the longest x4 80.8 us: gather_features(): lax.all_gather(part_img, 'col', axis=2, tiled=True)]
    all_to_all x19 -> x0, waiting for transfers between devices: 161 us -> none  [the longest x2 34.9 us: to_sequences(): lax.all_to_all(item_block, 'row', split_axis=0, concat_axis=1, tiled=True)]
    reduce_scatter x8 -> x0, waiting for transfers between devices: 119 us -> none  [the longest x4 104 us: reduce_columns(): lax.psum_scatter(term_img, 'col', scatter_dimension=2, tiled=True)]
    psum x9 -> x0, blocking collectives: 97.6 us -> none  [the longest x4 39 us: mean_pair(): lax.psum((jnp.sum(first_part, axis=-1), jnp.sum(second_part, axis=-1)), '...]
    all_to_all x24 -> x0, local copies, waits for them, and re-layouts: 93.9 us -> none  [the longest x2 22.2 us: local(): lax.all_to_all(spread(d_qkv[0]), 'row', split_axis=2, concat_axis=1, tile...]
    dot_general x51 -> x20, matrix products: 150 us -> 61.3 us  [the longest x12 32.9 us: dot_f32(): return jnp.einsum('td,de->te', left, right, preferred_element_type=F32)]
  transfers between devices with their start and end apart: 36 -> 3, of which waited for: 23 -> 0; matrix products, arithmetic and copies ran while one was open for 25% -> 14% of each run, Pallas kernels for 0% -> 27%
where the time goes in v1:
time: 577 us; the launch traced here: 567 us
  Pallas kernels  402 us (70%)
  matrix products  61.3 us (11%)
  other arithmetic  48.9 us (8%)
  local copies, waits for them, and re-layouts  46.2 us (8%)
    pallas_call x1, Pallas kernels, sum_branch(): communicate(kernel, 'sum_branch', 2, out_shape=[struct(part_img.shape, BF...  79.3 us
    pallas_call x1, Pallas kernels, sum_last(): communicate(kernel, 'sum_last', 5, out_shape=[struct((t, width), BF) for...  76.2 us
    pallas_call x1, Pallas kernels, sum_hidden(): communicate(kernel, 'sum_hidden', 3, out_shape=[struct(b.shape, BF) for b...  74 us
    pallas_call x1, Pallas kernels, sum_keys(): communicate(kernel, 'sum_keys', 4, out_shape=[struct((2, seqs, img, width...  58.2 us
    pallas_call x1, Pallas kernels, prologue(): communicate(kernel, 'prologue', 0, out_shape=[struct(s, BF) for s in full...  49.7 us
    pallas_call x1, Pallas kernels, gather_keys(): communicate(kernel, 'gather_keys', 1, out_shape=[struct((4, two, seqs, im...  34.2 us
    dot_general x12, matrix products, dot_f32(): return jnp.einsum('td,de->te', left, right, preferred_element_type=F32)  32.9 us
    unnamed x115, local copies, waits for them, and re-layouts  23.1 us
  transfers between devices with their start and end apart: 3, of which 0 were waited for; matrix products, arithmetic and copies ran while one was open for 14% of the time, Pallas kernels for 27%

profile of v1, /device:TPU:0, one launch (start us, length us, event | category | flops | bytes accessed | tf_op | source)
XLA Modules:
  0.0 567.3 jit_solution(16503339318413880288)
XLA Ops:
  3.6 2.6 fusion.134
  7.5 49.7 %prologue.1 = (bf16[2,256,1536]{2,1,0:T(8,128)(2,1)}, bf16[2,32,1536]{2,1,0:T(8,128)(2,1)}, bf16[2,3,1536,384]{3,2,1,0:T(8,128)(2,1)}, bf16[2,384,1536]{2,1,0:T(8,128)(2,1)}, f32[4,2,2,8,384]{4,3,2,1,0:T(8,128)}) custom-call(bf16[2,256,384]{2,1,0:T(8,128)(2,1)} %refs_0_.1, bf16[2,32,384]{2,1,0:T(8,128)(2,1)} %refs_1_.1, bf16[2,3,384,384]{3,2,1,0:T(8,128)(2,1)} %bitcast.267, ...), custom_call_target="tpu_custom_call" | custom-call | tf_op jit(solution)/shard_map/prologue/pallas_call | solution.py:429
  75.2 34.2 %gather_keys.1 = (bf16[4,2,2,288,384]{4,3,2,1,0:T(8,128)(2,1)}, bf16[2,256,1536]{2,1,0:T(8,128)(2,1)}, bf16[2,32,1536]{2,1,0:T(8,128)(2,1)}) custom-call(bf16[2,2,256,384]{3,2,1,0:T(8,128)(2,1)} %pad_maximum_fusion.refs_0_, bf16[2,2,32,384]{3,2,1,0:T(8,128)(2,1)} %pad_maximum_fusion.1.refs_1_, bf16[2,256,384]{2,1,0:T(8,128)(2,1)} %refs_2_.2, ...), custom_call_target="tpu_custom_call" | custom-call | tf_op jit(solution)/shard_map/gather_keys/pallas_call | solution.py:552
  109.4 14.1 %attend.1 = (bf16[2,256,384]{2,1,0:T(8,128)(2,1)}, bf16[2,32,384]{2,1,0:T(8,128)(2,1)}, f32[2,3,288,128]{3,2,1,0:T(8,128)}) custom-call(bf16[2,256,384]{2,1,0:T(8,128)(2,1)} %bitcast.268, bf16[2,32,384]{2,1,0:T(8,128)(2,1)} %bitcast.292, bf16[4,2,2,288,384]{4,3,2,1,0:T(8,128)(2,1)} %get-tuple-element.62.k_ref.v_ref, ...), custom_call_target="tpu_custom_call" | custom-call | tf_op jit(solution)/shard_map/attend/pallas_call | solution.py:611
  125.8 3.5 convolution_convert_fusion.refs_0_
  129.3 79.3 %sum_branch.1 = (bf16[512,1536]{1,0:T(8,128)(2,1)}, bf16[64,1536]{1,0:T(8,128)(2,1)}, bf16[2,1536,1536]{2,1,0:T(8,128)(2,1)}, bf16[2,1536,1536]{2,1,0:T(8,128)(2,1)}) custom-call(bf16[512,1536]{1,0:T(8,128)(2,1)} %convolution_convert_fusion.refs_0_, bf16[64,1536]{1,0:T(8,128)(2,1)} %convolution_convert_fusion.1.refs_1_, bf16[2,384,1536]{2,1,0:T(8,128)(2,1)} %refs_2_.3, ...), custom_call_target="tpu_custom_call" | custom-call | tf_op jit(solution)/shard_map/sum_branch/pallas_call | solution.py:847
  215.6 4.9 multiply_convert_fusion.1
  222.7 4.7 fusion.61.refs_1_
  229.0 4.3 multiply_convert_fusion
  233.3 5.1 fusion.146
  238.4 3.7 fusion.49.refs_0_
  242.2 74.0 %sum_hidden.1 = (bf16[512,1536]{1,0:T(8,128)(2,1)}, bf16[64,1536]{1,0:T(8,128)(2,1)}, f32[2,384,1536]{2,1,0:T(8,128)}, bf16[2,384,1536]{2,1,0:T(8,128)(2,1)}, bf...) custom-call(bf16[512,1536]{1,0:T(8,128)(2,1)} %fusion.49.refs_0_, ...), custom_call_target="tpu_custom_call" | custom-call | tf_op jit(solution)/shard_map/sum_hidden/pallas_call | solution.py:1020
  354.8 3.5 fusion.38
  361.3 16.7 %attend_back.1 = (bf16[2,256,384]{2,1,0:T(8,128)(2,1)}, bf16[2,32,384]{2,1,0:T(8,128)(2,1)}, bf16[4,2,288,384]{3,2,1,0:T(8,128)(2,1)}, bf16[4,2,288,384]{3,2,1,0:T(8,128)(2,1)}) custom-call(bf16[2,256,384]{2,1,0:T(8,128)(2,1)} %bitcast.269, bf16[2,32,384]{2,1,0:T(8,128)(2,1)} %bitcast.293, bf16[4,2,2,288,384]{4,3,2,1,0:T(8,128)(2,1)} %get-tuple-element.62.k_ref.v_ref, ...), custom_call_target="tpu_custom_call" | custom-call | tf_op jit(solution)/shard_map/attend_back/pallas_call | solution.py:684
  378.6 3.9 fusion.58.refs_3_
  382.5 3.9 add_convert_fusion
  386.9 6.0 %fusion.46.refs_2_ = bf16[512,1536]{1,0:T(8,128)(2,1)} fusion(bf16[512,1536]{1,0:T(8,128)(2,1)S(1)} %copy-done.14, bf16[2,1536,1536]{2,1,0:T(8,128)(2,1)} %get-tuple-element.68), kind=kOutput, calls=%fused_computation.58 | convolution fusion | flops 2416705536 | bytes 7864320 | tf_op jit(solution)/shard_map/td,de->te/dot_general | solution.py:1607
  392.9 58.2 %sum_keys.1 = (bf16[2,2,256,384]{3,2,1,0:T(8,128)(2,1)}, bf16[2,2,32,384]{3,2,1,0:T(8,128)(2,1)}, f32[512,384]{1,0:T(8,128)}, f32[64,384]{1,0:T(8,128)}, f32[2,384,384]{2,1,0:T(8,128)}) custom-call(bf16[4,2,288,384]{3,2,1,0:T(8,128)(2,1)} %get-tuple-element.81.refs_0_, bf16[4,2,288,384]{3,2,1,0:T(8,128)(2,1)} %get-tuple-element.82.refs_1_, ...), custom_call_target="tpu_custom_call" | custom-call | tf_op jit(solution)/shard_map/sum_keys/pallas_call | solution.py:1254
  451.1 76.2 %sum_last.1 = (bf16[512,384]{1,0:T(8,128)(2,1)}, bf16[64,384]{1,0:T(8,128)(2,1)}, f32[512,384]{1,0:T(8,128)}, f32[64,384]{1,0:T(8,128)}, f32[2,3,384,384]{3,2,1,...) custom-call(bf16[512,384]{1,0:T(8,128)(2,1)} %bitcast.290, bf16[64,384]{1,0:T(8,128)(2,1)} %bitcast.299, ...), custom_call_target="tpu_custom_call" | custom-call | tf_op jit(solution)/shard_map/sum_last/pallas_call | solution.py:1553
  532.2 4.3 all-gather.1
  536.6 6.0 %convolution_bitcast_fusion = f32[2,384,6,384]{1,3,2,0:T(8,128)} fusion(f32[2,2,2,6,384]{4,0,3,2,1:T(2,128)S(1)} %bitcast.291, bf16[2,2,384,1,1]{2,1,0,4,3:T(2,128)(2,1)S(1)} %bitcast.305), kind=kOutput, calls=%fused_computation.62 | convolution fusion | flops 84934656 | bytes 7154688 | tf_op jit(solution)/shard_map/psc,pzskd->zkcd/dot_general | solution.py:1792
  542.5 8.0 %copy.66 = f32[2,384,6,384]{3,1,2,0:T(8,128)} copy(f32[2,384,6,384]{1,3,2,0:T(8,128)} %convolution_bitcast_fusion) | data formatting | bytes 14155776
  551.2 5.0 convert_add_fusion.1
  556.2 4.7 convert_add_fusion.2
  (201 shorter events, 88.9 us)
Async XLA Ops:
  57.2 7.3 %copy-start.17 = (f32[4,2,2,8,384]{4,3,2,1,0:T(8,128)S(1)}, f32[4,2,2,8,384]{4,3,2,1,0:T(8,128)}, u32[]{:S(2)}) copy-start(f32[4,2,2,8,384]{4,3,2,1,0:T(8,128)} %get-tuple-element.59.refs_21_) | copy-start | bytes 589828
  57.2 7.5 %copy-start.5 = (bf16[2,32,1536]{2,1,0:T(8,128)(2,1)S(1)}, bf16[2,32,1536]{2,1,0:T(8,128)(2,1)}, u32[]{:S(2)}) copy-start(bf16[2,32,1536]{2,1,0:T(8,128)(2,1)} %get-tuple-element.61) | copy-start | bytes 589828
  58.3 9.8 %copy-start.39 = (f32[2,32]{1,0:T(2,128)}, f32[2,32]{1,0:T(2,128)S(1)}, u32[]{:S(2)}) copy-start(f32[2,32]{1,0:T(2,128)S(1)} %broadcast_multiply_fusion.6) | copy-start | bytes 772
  59.5 8.7 %copy-start.43 = (f32[2,32]{1,0:T(2,128)}, f32[2,32]{1,0:T(2,128)S(1)}, u32[]{:S(2)}) copy-start(f32[2,32]{1,0:T(2,128)S(1)} %add_rsqrt_fusion.3) | copy-start | bytes 772
  59.5 8.7 %copy-start.7 = (bf16[2,3,1536,384]{3,2,1,0:T(8,128)(2,1)S(1)}, bf16[2,3,1536,384]{3,2,1,0:T(8,128)(2,1)}, u32[]{:S(2)}) copy-start(bf16[2,3,1536,384]{3,2,1,0:T(8,128)(2,1)} %get-tuple-element.60.refs_4_) | copy-start | bytes 21233668
  129.3 193.7 %copy-start.24 = (f32[2,1536]{1,0:T(2,128)}, f32[2,1536]{1,0:T(2,128)S(1)}, u32[]{:S(2)}) copy-start(f32[2,1536]{1,0:T(2,128)S(1)} %get-tuple-element.197) | copy-start | bytes 36868
  209.8 113.2 %copy-start.35 = (f32[2,32]{1,0:T(2,128)}, f32[2,32]{1,0:T(2,128)S(1)}, u32[]{:S(2)}) copy-start(f32[2,32]{1,0:T(2,128)S(1)} %broadcast_multiply_fusion.5) | copy-start | bytes 772
  211.0 112.1 %copy-start.38 = (f32[2,32]{1,0:T(2,128)}, f32[2,32]{1,0:T(2,128)S(1)}, u32[]{:S(2)}) copy-start(f32[2,32]{1,0:T(2,128)S(1)} %add_rsqrt_fusion.2) | copy-start | bytes 772
  211.0 112.9 %copy-start.25 = (f32[2,1536]{1,0:T(2,128)}, f32[2,1536]{1,0:T(2,128)S(1)}, u32[]{:S(2)}) copy-start(f32[2,1536]{1,0:T(2,128)S(1)} %get-tuple-element.202) | copy-start | bytes 36868
  211.0 112.9 %copy-start.26 = (f32[2,1536]{1,0:T(2,128)}, f32[2,1536]{1,0:T(2,128)S(1)}, u32[]{:S(2)}) copy-start(f32[2,1536]{1,0:T(2,128)S(1)} %get-tuple-element.203) | copy-start | bytes 36868
  213.8 6.7 %copy-start.45 = (bf16[2,1536,1536]{2,1,0:T(8,128)(2,1)S(1)}, bf16[2,1536,1536]{2,1,0:T(8,128)(2,1)}, u32[]{:S(2)}) copy-start(bf16[2,1536,1536]{2,1,0:T(8,128)(2,1)} %get-tuple-element.68) | copy-start | bytes 28311556
  215.3 108.5 %copy-start.34 = (f32[2,256]{1,0:T(2,128)}, f32[2,256]{1,0:T(2,128)S(1)}, u32[]{:S(2)}) copy-start(f32[2,256]{1,0:T(2,128)S(1)} %get-tuple-element.177) | copy-start | bytes 6148
  215.4 107.7 %copy-start.28 = (f32[2,1536]{1,0:T(2,128)}, f32[2,1536]{1,0:T(2,128)S(1)}, u32[]{:S(2)}) copy-start(f32[2,1536]{1,0:T(2,128)S(1)} %get-tuple-element.195) | copy-start | bytes 36868
  222.7 6.3 %copy-start.46 = (bf16[2,1536,1536]{2,1,0:T(8,128)(2,1)S(1)}, bf16[2,1536,1536]{2,1,0:T(8,128)(2,1)}, u32[]{:S(2)}) copy-start(bf16[2,1536,1536]{2,1,0:T(8,128)(2,1)} %get-tuple-element.69) | copy-start | bytes 28311556
  227.4 96.5 %copy-start.29 = (f32[2,1536]{1,0:T(2,128)}, f32[2,1536]{1,0:T(2,128)S(1)}, u32[]{:S(2)}) copy-start(f32[2,1536]{1,0:T(2,128)S(1)} %get-tuple-element.200) | copy-start | bytes 36868
  316.2 66.4 %collective-permute-start = (bf16[2,384,1536]{2,1,0:T(8,128)(2,1)}, bf16[2,384,1536]{2,1,0:T(8,128)(2,1)}, u32[]{:S(2)}, u32[]{:S(2)}) collective-permute-start(bf16[2,384,1536]{2,1,0:T(8,128)(2,1)} %get-tuple-element.80), channel_id=1, source_target_pairs={{0,8},{4,12},{8,0},{12,4},{1,9},{5,13},{9,1},{13,5},{2,10},{6,14},... | collective-permute-start | bytes 7077896 | tf_op jit(solution)/shard_map/ppermute | solution.py:1725
  316.5 234.6 %collective-permute-start.2 = (bf16[2,1536,384]{2,1,0:T(8,128)(2,1)}, bf16[2,1536,384]{2,1,0:T(8,128)(2,1)}, u32[]{:S(2)}, u32[]{:S(2)}) collective-permute-start(bf16[2,1536,384]{2,1,0:T(8,128)(2,1)} %get-tuple-element.100), channel_id=1, source_target_pairs={{0,16},{16,0},{1,17},{17,1},{2,18},{18,2},{3,19},{19,3},{4,20},{20... | collective-permute-start | bytes 7077896 | tf_op jit(solution)/shard_map/ppermute | solution.py:1719
  361.3 16.7 %copy-start.36 = (f32[4,384]{1,0:T(4,128)S(1)}, f32[4,384]{1,0:T(4,128)}, u32[]{:S(2)}) copy-start(f32[4,384]{1,0:T(4,128)} %reshape.485) | copy-start | bytes 18436
  361.3 16.7 %copy-start.37 = (f32[4,384]{1,0:T(4,128)S(1)}, f32[4,384]{1,0:T(4,128)}, u32[]{:S(2)}) copy-start(f32[4,384]{1,0:T(4,128)} %reshape.484) | copy-start | bytes 18436
  361.3 17.3 %copy-start.30 = (bf16[64,1536]{1,0:T(8,128)(2,1)S(1)}, bf16[64,1536]{1,0:T(8,128)(2,1)}, u32[]{:S(2)}) copy-start(bf16[64,1536]{1,0:T(8,128)(2,1)} %get-tuple-element.192.refs_7_) | copy-start | bytes 589828
  386.5 169.7 %collective-permute-start.1 = (bf16[2,384,1536]{2,1,0:T(8,128)(2,1)S(1)}, bf16[2,384,1536]{2,1,0:T(8,128)(2,1)}, u32[]{:S(2)}, u32[]{:S(2)}) collective-permute-start(bf16[2,384,1536]{2,1,0:T(8,128)(2,1)S(1)} %add_convert_fusion), channel_id=1, source_target_pairs={{0,16},{16,0},{1,17},{17,1},{2,18},{18,2},{3,19},{19,3},{4,20},{20... | collective-permute-start | bytes 7077896 | tf_op jit(solution)/shard_map/ppermute | solution.py:1719
  451.1 79.8 %copy-start.42 = (bf16[2,384]{1,0:T(2,128)(2,1)S(1)}, bf16[2,384]{1,0:T(2,128)(2,1)}, u32[]{:S(2)}) copy-start(bf16[2,384]{1,0:T(2,128)(2,1)} %param.17) | copy-start | bytes 4612
  556.2 6.9 %copy-start.32 = (f32[64,384]{1,0:T(8,128)S(1)}, f32[64,384]{1,0:T(8,128)}, u32[]{:S(2)}) copy-start(f32[64,384]{1,0:T(8,128)} %get-tuple-element.94) | copy-start | bytes 294916
  556.2 7.6 %copy-start.12 = (f32[2,3,384,384]{3,2,1,0:T(8,128)S(1)}, f32[2,3,384,384]{3,2,1,0:T(8,128)}, u32[]{:S(2)}) copy-start(f32[2,3,384,384]{3,2,1,0:T(8,128)} %get-tuple-element.96) | copy-start | bytes 10616836
  (26 other events, 115.2 us)

commit v2 on v1

--- a/solution.py
+++ b/solution.py
@@ -1,11 +1,10 @@
-from functools import partial
-
 import jax
 import jax.numpy as jnp
 from jax import lax
 from jax.experimental import pallas as pl
 from jax.experimental.pallas import tpu as pltpu
 from jax.sharding import PartitionSpec as P
+
 
 HD = 64
 EPSILON = 1e-06
@@ -188,10 +187,9 @@
                     self.copy(side, slot).wait_send()
 
 
-def communicate(kernel, name, collective_id, **kwargs):
+def communicate(kernel, collective_id, **kwargs):
     return pl.pallas_call(
         kernel,
-        name=name,
         compiler_params=pltpu.CompilerParams(
             collective_id=collective_id, has_side_effects=True, vmem_limit_bytes=VMEM_LIMIT
         ),
@@ -200,18 +198,22 @@
 
 
 class WeightFlow:
-    def __init__(self, kinds, shards, fulls, subs, send_sems, recv_sems):
-        self.kinds, self.shards, self.fulls, self.subs = kinds, shards, fulls, subs
+    def __init__(self, kinds, streams, shards, fulls, subs, send_sems, recv_sems):
+        self.kinds, self.streams, self.shards, self.fulls, self.subs = kinds, streams, shards, fulls, subs
         self.send_sems, self.recv_sems = send_sems, recv_sems
-        self.pieces = [(n, s, u) for n in range(len(kinds)) for s in range(2) for u in range(subs)]
+        self.pieces = WeightFlow.listed(streams, subs)
         self.row = lax.axis_index("row")
         self.half = lax.rem(lax.axis_index("dp"), 2)
         self.mate = flip(lax.axis_index("dp"))
         self.sib, self.far = flip(self.row), flip_far(self.row)
 
     @staticmethod
-    def sem_shape(count, subs):
-        return (count * 2 * subs, 5)
+    def listed(streams, subs):
+        return [(n, s, u) for n in range(len(streams)) for s in streams[n] for u in range(subs)]
+
+    @staticmethod
+    def sem_shape(streams, subs):
+        return (len(WeightFlow.listed(streams, subs)), 5)
 
     def split(self, depth, sub, part):
         if part is None:
@@ -223,6 +225,7 @@
     def view(self, piece, block, part):
         number, stream, sub = self.pieces[piece]
         kind, ref, shard = self.kinds[number], self.fulls[number], self.shards[number]
+        stream -= self.streams[number][0]
         if kind == "qkv" or kind == "up":
             depth = shard.shape[-2]
             if part is None:
@@ -334,26 +337,27 @@
     return line, first, at(place)
 
 
-def prologue(cols, x_img, x_txt, qkv, out, table, bias):
+def prologue(pods, cols, x_img, x_txt, qkv, out, table, bias, cond):
     shards = (x_img, x_txt, qkv, out)
     width = x_img.shape[2]
     rows = 4
-    kinds = ("qkv", "out")
+    kinds, streams = ("qkv", "out"), ((0, 1), (0, 1))
     full_shapes = [s.shape[:2] + (s.shape[2] * cols,) for s in shards[:2]]
     full_shapes += [gathered_shape(k, s.shape) for k, s in zip(kinds, shards[2:])]
     table_shape = table.shape
 
     def kernel(*refs):
         shard = refs[:4]
-        table_ref, bias_ref = refs[4:6]
-        full = refs[6:10]
-        mods_ref = refs[10]
-        stage = refs[11:15]
-        parts = refs[15]
-        local_in, local_out, zs, zr, ws, wr, ms, mr = refs[16:]
+        table_ref, bias_ref, cond_ref = refs[4:7]
+        full = refs[7:11]
+        mods_ref, every_cond = refs[11:13]
+        stage = refs[13:17]
+        parts = refs[17]
+        local_in, local_out, zs, zr, ws, wr, ms, mr, cs, cr = refs[18:]
+        pod = lax.axis_index("dp")
         place = lax.axis_index("col")
         row = lax.axis_index("row")
-        flow = WeightFlow(kinds, shard[2:], full[2:], 1, ws, wr)
+        flow = WeightFlow(kinds, streams, shard[2:], full[2:], 1, ws, wr)
         lines = [line_from(shard[n], full[n], width, cols, place, zs.at[n], zr.at[n]) for n in range(2)]
         owns = [OwnCopy(shard[n], stage[n], lines[n][2], local_in.at[n], local_out.at[n]) for n in range(2)]
         owns += [
@@ -362,7 +366,16 @@
         ]
         for own in owns:
             own.begin()
-        greet(others("row", rows) + others("col", cols) + [("dp", flow.mate)])
+        greet(others("row", rows) + others("col", cols) + others("dp", pods))
+
+        def cond_copy(step):
+            return send(
+                cond_ref, every_cond.at[pod], cs.at[step - 1], cr.at[step - 1], "dp", lax.rem(pod + step, pods)
+            )
+
+        for step in range(1, pods):
+            cond_copy(step).start()
+        every_cond[pod] = cond_ref[...]
 
         def part_copy(step):
             return send(
@@ -425,14 +438,19 @@
         flow.finish()
         for own in owns:
             own.finish()
+        for step in range(1, pods):
+            source = lax.rem(pod - step + pods, pods)
+            at = every_cond.at[source]
+            send(at, at, cs.at[step - 1], cr.at[step - 1], "dp", source).wait_recv()
+            cond_copy(step).wait_send()
 
     return communicate(
         kernel,
-        "prologue",
         0,
-        out_shape=[struct(s, BF) for s in full_shapes] + [struct((cols,) + table_shape, F32)],
-        in_specs=[ANY] * 4 + [VM, VM],
-        out_specs=[ANY] * 4 + [VM],
+        out_shape=[struct(s, BF) for s in full_shapes]
+        + [struct((cols,) + table_shape, F32), struct((pods,) + cond.shape, F32)],
+        in_specs=[ANY] * 4 + [VM] * 3,
+        out_specs=[ANY] * 4 + [VM] * 2,
         scratch_shapes=[pltpu.VMEM(s.shape, BF) for s in shards]
         + [
             pltpu.VMEM((rows - 1,) + table_shape, F32),
@@ -440,217 +458,276 @@
             pltpu.SemaphoreType.DMA((4,)),
             pltpu.SemaphoreType.DMA((2, 2, cols - 1)),
             pltpu.SemaphoreType.DMA((2, 2, cols - 1)),
-            pltpu.SemaphoreType.DMA(WeightFlow.sem_shape(2, 1)),
-            pltpu.SemaphoreType.DMA(WeightFlow.sem_shape(2, 1)),
+            pltpu.SemaphoreType.DMA(WeightFlow.sem_shape(streams, 1)),
+            pltpu.SemaphoreType.DMA(WeightFlow.sem_shape(streams, 1)),
             pltpu.SemaphoreType.DMA((rows + cols - 2,)),
             pltpu.SemaphoreType.DMA((rows + cols - 2,)),
+            pltpu.SemaphoreType.DMA((pods - 1,)),
+            pltpu.SemaphoreType.DMA((pods - 1,)),
         ],
-    )(*shards, table, bias)
-
-
-def gather_keys(cols, kv_img, kv_txt, cot_img, cot_txt):
-    two, seqs, img, width = kv_img.shape
-    txt = kv_txt.shape[2]
-    cots = (cot_img, cot_txt)
+    )(*shards, table, bias, cond)
+
+
+def front(cols, x_full, wide, qkv, b_qv, cots, w_up):
+    seqs = wide.shape[1]
+    full = wide.shape[3]
+    width = full // cols
+    tokens = [x.shape[0] for x in x_full]
+    counts = [t // seqs for t in tokens]
+    joint = sum(counts)
+    lanes = 2 * HD
+    pairs = width // lanes
+    scale = HD ** (-0.5)
+    kinds, streams, subs = ("up",), ((0,),), 2
+    up_shape = (1,) + gathered_shape("up", w_up.shape)[1:]
+    lots = [(which, q) for which in range(2) for q in range(seqs)]
+    over_last = (((1,), (1,)), ((), ()))
 
     def kernel(*refs):
-        img_ref, txt_ref = refs[:2]
-        cot_refs = refs[2:4]
-        all_ref = refs[4]
-        cot_full = refs[5:7]
-        stage_img, stage_txt = refs[7:9]
-        stage_cot = refs[9:11]
-        local, ss, rs, zs, zr = refs[11:]
+        takes = iter(refs)
+
+        def two():
+            return (next(takes), next(takes))
+
+        x_any = two()
+        wide_ref, qkv_any, bias_ref = (next(takes) for _ in range(3))
+        cot_refs = two()
+        up_shard = next(takes)
+        hidden, queries = two(), two()
+        keys = next(takes)
+        attended = two()
+        lse_ref = next(takes)
+        cot_full = two()
+        up_full = next(takes)
+        x_ref = two()
+        qkv_ref = next(takes)
+        stage_cot = two()
+        stage_up = next(takes)
+        loads, local, ks, kr, zs, zr, ws, wr = (next(takes) for _ in range(8))
         row = lax.axis_index("row")
         place = lax.axis_index("col")
         sib, far = flip(row), flip_far(row)
-        ins = [
-            pltpu.make_async_copy(img_ref, stage_img, local.at[0]),
-            pltpu.make_async_copy(txt_ref, stage_txt, local.at[1]),
+        x_loads = [pltpu.make_async_copy(x_any[s], x_ref[s], loads.at[s]) for s in range(2)]
+        w_loads = [
+            pltpu.make_async_copy(qkv_any.at[s, k], qkv_ref.at[s, k], loads.at[2 + 3 * s + k])
+            for k in (1, 2, 0)
+            for s in range(2)
         ]
-        for copy in ins:
-            copy.start()
+        for load in x_loads + w_loads:
+            load.start()
+        flow = WeightFlow(kinds, streams, (up_shard,), (up_full,), subs, ws, wr)
         lines = [line_from(cot_refs[n], cot_full[n], width, cols, place, zs.at[n], zr.at[n]) for n in range(2)]
-        owns = [
-            OwnCopy(cot_refs[n], stage_cot[n], lines[n][2], local.at[6 + n], local.at[8 + n]) for n in range(2)
-        ]
+        owns = [OwnCopy(cot_refs[n], stage_cot[n], lines[n][2], local.at[n], local.at[2 + n]) for n in range(2)]
+        owns.append(OwnCopy(up_shard.at[pl.ds(0, 1)], stage_up, flow.own_view(0), local.at[4], local.at[5]))
         for own in owns:
             own.begin()
-
-        def img_at(block, index):
-            return all_ref.at[block, index, :, pl.ds(0, img), :]
-
-        def txt_at(block, index):
-            return all_ref.at[block, index, :, pl.ds(img, txt), :]
-
-        greet(others("row", 4) + others("col", cols))
-
-        def direct(kind, index):
-            peer = far if kind == 0 else sib
-            return [
-                send(img_ref.at[index], img_at(row, index), ss.at[kind, index, 0], rs.at[kind, index, 0], "row", peer),
-                send(txt_ref.at[index], txt_at(row, index), ss.at[kind, index, 1], rs.at[kind, index, 1], "row", peer),
-            ]
-
-        def onward(index, block):
-            return [
-                send(img_at(block, index), img_at(block, index), ss.at[2, index, 0], rs.at[2, index, 0], "row", sib),
-                send(txt_at(block, index), txt_at(block, index), ss.at[2, index, 1], rs.at[2, index, 1], "row", sib),
-            ]
-
-        def land(kind, index, block):
-            for number, at in ((0, img_at(block, index)), (1, txt_at(block, index))):
-                send(at, at, ss.at[kind, index, number], rs.at[kind, index, number], "row", sib).wait_recv()
-
-        for kind in range(2):
-            for index in range(2):
-                for copy in direct(kind, index):
-                    copy.start()
+        greet(others("row", 4) + others("col", cols) + [("dp", flow.mate)])
         for _, first, _ in lines:
             first()
-        for copy in ins:
-            copy.wait()
-        outs = []
-        for index in range(2):
-            outs.append(pltpu.make_async_copy(stage_img.at[index], img_at(row, index), local.at[2 + index]))
-            outs.append(pltpu.make_async_copy(stage_txt.at[index], txt_at(row, index), local.at[4 + index]))
-        for copy in outs:
-            copy.start()
+        flow.copy(0, 1).start()
+
+        for s in range(2):
+            x_loads[s].wait()
+            rows = min(64, counts[s])
+            for q in range(seqs):
+                shift, grow = wide_ref[s, q, 0:1, :], 1.0 + wide_ref[s, q, 1:2, :]
+
+                @pl.loop(0, counts[s] // rows)
+                def _(at):
+                    cut = pl.ds(pl.multiple_of(q * counts[s] + at * rows, rows), rows)
+                    resid = x_ref[s][cut, :].astype(F32)
+                    mean, inverse = stats(resid)
+                    hidden[s][cut, :] = ((resid - mean) * inverse * grow + shift).astype(BF)
+
+        def key_copy(kind, lot):
+            which, q = lots[lot]
+            at = keys.at[far if kind == 2 else row, which, q]
+            return send(at, at, ks.at[kind, lot], kr.at[kind, lot], "row", far if kind == 0 else sib)
+
+        def key_land(kind, lot):
+            which, q = lots[lot]
+            at = keys.at[(far, sib, flip(far))[kind], which, q]
+            send(at, at, ks.at[kind, lot], kr.at[kind, lot], "row", sib).wait_recv()
+
+        def project(s, k):
+            return jnp.dot(hidden[s][...], qkv_ref[s, k], preferred_element_type=F32)
+
+        for which in range(2):
+            for s in range(2):
+                w_loads[2 * which + s].wait()
+                value = project(s, which + 1)
+                if which == 1:
+                    value = value + bias_ref[s, 1:2, :]
+                value = value.astype(BF)
+                first = 0 if s == 0 else counts[0]
+                for q in range(seqs):
+                    keys[row, which, q, pl.ds(first, counts[s]), :] = value[q * counts[s] : (q + 1) * counts[s]]
+            for q in range(seqs):
+                key_copy(0, which * seqs + q).start()
+                key_copy(1, which * seqs + q).start()
+        for piece in range(1, len(flow.pieces)):
+            flow.copy(piece, 1).start()
         for own in owns:
             own.settle()
-        land(0, 0, far)
-        for copy in onward(0, far):
-            copy.start()
+        for s in range(2):
+            w_loads[4 + s].wait()
+            queries[s][...] = (project(s, 0) + bias_ref[s, 0:1, :]).astype(BF)
+        flow.start(0)
+        for lot in range(len(lots)):
+            key_land(0, lot)
+            key_copy(2, lot).start()
+            if lot == 0:
+                flow.relay_y(0)
+                for line, _, _ in lines:
+                    line.arrive(0)
+                    line.start(1)
         for line, _, _ in lines:
-            line.arrive(0)
-            line.start(1)
-        land(0, 1, far)
-        for copy in onward(1, far):
-            copy.start()
-        for step in range(2, cols - 1):
-            for line, _, _ in lines:
+            for step in range(2, cols - 1):
                 line.arrive(step - 1)
                 line.start(step)
-        for index in range(2):
-            land(1, index, sib)
-            land(2, index, flip(far))
+        flow.relay_x(0)
+        for lot in range(len(lots)):
+            key_land(1, lot)
+            key_land(2, lot)
+
+        low = lax.broadcasted_iota(jnp.int32, (joint, lanes), 1) < HD
+        for q in range(seqs):
+            img_rows, txt_rows = pl.ds(q * counts[0], counts[0]), pl.ds(q * counts[1], counts[1])
+
+            @pl.loop(0, pairs)
+            def _(pair):
+                cut = aligned(pair, lanes)
+                asked = jnp.concatenate([queries[0][img_rows, cut], queries[1][txt_rows, cut]], axis=0)
+                key_block = keys[:, 0, q, :, cut].reshape(4 * joint, lanes)
+                value_block = keys[:, 1, q, :, cut].reshape(4 * joint, lanes)
+                results, sums = [], []
+                for head in range(2):
+                    mine = low if head == 0 else jnp.logical_not(low)
+                    chosen = jnp.where(mine, asked, jnp.zeros_like(asked))
+                    scores = (
+                        lax.dot_general(chosen, key_block, over_last, preferred_element_type=F32) * scale
+                    )
+                    highest = jnp.max(scores, axis=-1, keepdims=True)
+                    grown = jnp.exp(scores - highest)
+                    total = jnp.sum(grown, axis=-1, keepdims=True)
+                    weights = (grown * (1.0 / total)).astype(BF)
+                    results.append(jnp.dot(weights, value_block, preferred_element_type=F32))
+                    sums.append(jnp.broadcast_to(highest + jnp.log(total), (joint, lanes)))
+                result = jnp.where(low, results[0], results[1]).astype(BF)
+                attended[0][img_rows, cut] = result[: counts[0]]
+                attended[1][txt_rows, cut] = result[counts[0] :]
+                lse_ref[q, pair] = jnp.where(low, sums[0], sums[1])
+
+            if q == 0:
+                for piece in range(1, len(flow.pieces)):
+                    flow.relay_y(piece)
+        for piece in range(1, len(flow.pieces)):
+            flow.relay_x(piece)
         for line, _, _ in lines:
             line.arrive(cols - 2)
         for line, _, _ in lines:
             line.finish()
-        for index in range(2):
-            for kind in range(2):
-                for copy in direct(kind, index):
-                    copy.wait_send()
-            for copy in onward(index, far):
-                copy.wait_send()
-        for copy in outs:
-            copy.wait()
+        for lot in range(len(lots)):
+            for kind in range(3):
+                key_copy(kind, lot).wait_send()
+        flow.finish()
         for own in owns:
             own.finish()
 
+    dma = pltpu.SemaphoreType.DMA
     return communicate(
         kernel,
-        "gather_keys",
         1,
-        out_shape=[struct((4, two, seqs, img + txt, width), BF)]
-        + [struct(c.shape[:2] + (width * cols,), BF) for c in cots],
-        in_specs=[ANY] * 4,
-        out_specs=[ANY] * 3,
-        scratch_shapes=[
-            pltpu.VMEM(kv_img.shape, BF),
-            pltpu.VMEM(kv_txt.shape, BF),
-            pltpu.VMEM(cot_img.shape, BF),
-            pltpu.VMEM(cot_txt.shape, BF),
-            pltpu.SemaphoreType.DMA((10,)),
-            pltpu.SemaphoreType.DMA((3, 2, 2)),
-            pltpu.SemaphoreType.DMA((3, 2, 2)),
-            pltpu.SemaphoreType.DMA((2, 2, cols - 1)),
-            pltpu.SemaphoreType.DMA((2, 2, cols - 1)),
+        out_shape=[struct((t, full), BF) for t in tokens]
+        + [struct((t, width), BF) for t in tokens]
+        + [struct((4, 2, seqs, joint, width), BF)]
+        + [struct((t, width), BF) for t in tokens]
+        + [struct((seqs, pairs, joint, lanes), F32)]
+        + [struct(c.shape[:2] + (full,), BF) for c in cots]
+        + [struct(up_shape, BF)],
+        in_specs=[ANY, ANY, VM, ANY, VM, ANY, ANY, ANY],
+        out_specs=[VM] * 8 + [ANY] * 3,
+        scratch_shapes=[pltpu.VMEM(x.shape, BF) for x in x_full]
+        + [pltpu.VMEM(qkv.shape, BF)]
+        + [pltpu.VMEM(c.shape, BF) for c in cots]
+        + [
+            pltpu.VMEM((1,) + w_up.shape[1:], BF),
+            dma((8,)),
+            dma((6,)),
+            dma((3, len(lots))),
+            dma((3, len(lots))),
+            dma((2, 2, cols - 1)),
+            dma((2, 2, cols - 1)),
+            dma(WeightFlow.sem_shape(streams, subs)),
+            dma(WeightFlow.sem_shape(streams, subs)),
         ],
-    )(kv_img, kv_txt, cot_img, cot_txt)
-
-
-def attend(q_img, q_txt, keys):
-    seqs, img, width = q_img.shape
-    txt = q_txt.shape[1]
-    tokens = img + txt
-    blocks = keys.shape[0]
-    pairs = width // (2 * HD)
-    scale = HD ** (-0.5)
-
-    def kernel(qi_ref, qt_ref, k_ref, v_ref, oi_ref, ot_ref, lse_ref):
-        queries = jnp.concatenate([qi_ref[...], qt_ref[...]], axis=0)
-        key_block = k_ref[...].reshape(blocks * tokens, 2 * HD)
-        value_block = v_ref[...].reshape(blocks * tokens, 2 * HD)
-        low = lax.broadcasted_iota(jnp.int32, (tokens, 2 * HD), 1) < HD
-        results, sums = [], []
-        for head in range(2):
-            mine = low if head == 0 else jnp.logical_not(low)
-            chosen = jnp.where(mine, queries, jnp.zeros_like(queries))
-            scores = (
-                lax.dot_general(
-                    chosen, key_block, (((1,), (1,)), ((), ())), preferred_element_type=F32
-                )
-                * scale
-            )
-            highest = jnp.max(scores, axis=-1, keepdims=True)
-            grown = jnp.exp(scores - highest)
-            total = jnp.sum(grown, axis=-1, keepdims=True)
-            weights = (grown * (1.0 / total)).astype(BF)
-            results.append(jnp.dot(weights, value_block, preferred_element_type=F32))
-            sums.append(jnp.broadcast_to(highest + jnp.log(total), (tokens, 2 * HD)))
-        attended = jnp.where(low, results[0], results[1]).astype(BF)
-        oi_ref[...] = attended[:img]
-        ot_ref[...] = attended[img:]
-        lse_ref[...] = jnp.where(low, sums[0], sums[1])
-
-    lanes = 2 * HD
-    q_img_spec = pl.BlockSpec((None, img, lanes), lambda s, h: (s, 0, h))
-    q_txt_spec = pl.BlockSpec((None, txt, lanes), lambda s, h: (s, 0, h))
-    return pl.pallas_call(
-        kernel,
-        name="attend",
-        grid=(seqs, pairs),
-        in_specs=[
-            q_img_spec,
-            q_txt_spec,
-            pl.BlockSpec((blocks, None, None, tokens, lanes), lambda s, h: (0, 0, s, 0, h)),
-            pl.BlockSpec((blocks, None, None, tokens, lanes), lambda s, h: (0, 1, s, 0, h)),
-        ],
-        out_specs=[
-            q_img_spec,
-            q_txt_spec,
-            pl.BlockSpec((None, None, tokens, lanes), lambda s, h: (s, h, 0, 0)),
-        ],
-        out_shape=[
-            struct(q_img.shape, BF),
-            struct(q_txt.shape, BF),
-            struct((seqs, pairs, tokens, lanes), F32),
-        ],
-        compiler_params=pltpu.CompilerParams(vmem_limit_bytes=VMEM_LIMIT),
-    )(q_img, q_txt, keys, keys)
-
-
-def attend_back(q_img, q_txt, keys, o_img, o_txt, do_img, do_txt, lse):
-    seqs, img, width = q_img.shape
-    txt = q_txt.shape[1]
+    )(*x_full, wide, qkv, b_qv, *cots, w_up)
+
+
+def attend_back(q, keys, attended, lse, x_full, cot_full, branch, d_two, wide, out_full):
+    seqs, img, width = q[0].shape
+    txt = q[1].shape[1]
+    counts = (img, txt)
     tokens = img + txt
     blocks = keys.shape[0]
     pairs = width // (2 * HD)
     lanes = 2 * HD
+    full = x_full[0].shape[2]
     scale = HD ** (-0.5)
     over_last = (((1,), (1,)), ((), ()))
     over_first = (((0,), (0,)), ((), ()))
 
-    def kernel(qi, qt, k_ref, v_ref, oi, ot, di, dt, lse_ref, dqi, dqt, dk_ref, dv_ref):
-        queries = jnp.concatenate([qi[...], qt[...]], axis=0)
-        attended = jnp.concatenate([oi[...], ot[...]], axis=0)
-        d_attended = jnp.concatenate([di[...], dt[...]], axis=0)
+    def kernel(*refs):
+        takes = iter(refs)
+
+        def two():
+            return (next(takes), next(takes))
+
+        q_ref, o_ref, x_ref, cot_ref, bra, dtwo = (two() for _ in range(6))
+        k_ref, v_ref, lse_ref, wide_ref, out_ref = (next(takes) for _ in range(5))
+        dq, d_branch, stat = (two() for _ in range(3))
+        dk_ref, dv_ref = next(takes), next(takes)
+
+        @pl.when(pl.program_id(1) == 0)
+        def _():
+            lane = lax.broadcasted_iota(jnp.int32, (1, lanes), 1)
+            for s in range(2):
+                rows = 32
+                mods = [wide_ref[s, k : k + 1, :] for k in range(7)]
+
+                @pl.loop(0, counts[s] // rows)
+                def _(at):
+                    cut = aligned(at, rows)
+                    resid = x_ref[s][cut, :].astype(F32)
+                    mean_one, inverse_one = stats(resid)
+                    attn = bra[s][cut, :].astype(F32) + mods[6]
+                    middle = resid + mods[2] * attn
+                    mean, inverse = stats(middle)
+                    normed = (middle - mean) * inverse
+                    grown = dtwo[s][cut, :].astype(F32) * (1.0 + mods[4])
+                    first = jnp.mean(grown, axis=-1, keepdims=True)
+                    second = jnp.mean(grown * normed, axis=-1, keepdims=True)
+                    d_middle = cot_ref[s][cut, :].astype(F32) + inverse * (grown - first - normed * second)
+                    d_branch[s][cut, :] = (d_middle * mods[2]).astype(BF)
+                    columns = (mean_one, inverse_one, mean, inverse, first, second)
+                    packed = jnp.zeros((rows, lanes), F32)
+                    for number, column in enumerate(columns):
+                        packed = jnp.where(lane == number, column, packed)
+                    stat[s][cut, :] = packed
+
+        queries = jnp.concatenate([q_ref[0][...], q_ref[1][...]], axis=0)
+        result = jnp.concatenate([o_ref[0][...], o_ref[1][...]], axis=0)
+        d_attended = jnp.concatenate(
+            [
+                lax.dot_general(d_branch[s][...], out_ref[s], over_last, preferred_element_type=F32).astype(BF)
+                for s in range(2)
+            ],
+            axis=0,
+        )
         key_block = k_ref[...].reshape(blocks * tokens, lanes)
         value_block = v_ref[...].reshape(blocks * tokens, lanes)
         low = lax.broadcasted_iota(jnp.int32, (tokens, lanes), 1) < HD
-        product = d_attended.astype(F32) * attended.astype(F32)
+        product = d_attended.astype(F32) * result.astype(F32)
         d_q = []
         d_k = jnp.zeros((blocks * tokens, lanes), F32)
         d_v = jnp.zeros((blocks * tokens, lanes), F32)
@@ -673,38 +750,69 @@
             d_k = d_k + lax.dot_general(d_scores, q_head, over_first, preferred_element_type=F32)
             d_q.append(jnp.dot(d_scores, key_block, preferred_element_type=F32))
         d_queries = (jnp.where(low, d_q[0], d_q[1]) * scale).astype(BF)
-        dqi[...] = d_queries[:img]
-        dqt[...] = d_queries[img:]
+        dq[0][...] = d_queries[:img]
+        dq[1][...] = d_queries[img:]
         dk_ref[...] = (d_k * scale).astype(BF).reshape(blocks, tokens, lanes)
         dv_ref[...] = d_v.astype(BF).reshape(blocks, tokens, lanes)
 
-    img_spec = pl.BlockSpec((None, img, lanes), lambda s, h: (s, 0, h))
-    txt_spec = pl.BlockSpec((None, txt, lanes), lambda s, h: (s, 0, h))
+    heads = [pl.BlockSpec((None, c, lanes), lambda s, h: (s, 0, h)) for c in counts]
+    rows = [pl.BlockSpec((None, c, full), lambda s, h: (s, 0, 0)) for c in counts]
+    columns = [pl.BlockSpec((None, c, lanes), lambda s, h: (s, 0, 0)) for c in counts]
     sums = pl.BlockSpec((blocks, None, tokens, lanes), lambda s, h: (0, s, 0, h))
     return pl.pallas_call(
         kernel,
         name="attend_back",
         grid=(seqs, pairs),
-        in_specs=[
-            img_spec,
-            txt_spec,
+        in_specs=heads * 2
+        + rows * 4
+        + [
             pl.BlockSpec((blocks, None, None, tokens, lanes), lambda s, h: (0, 0, s, 0, h)),
             pl.BlockSpec((blocks, None, None, tokens, lanes), lambda s, h: (0, 1, s, 0, h)),
-            img_spec,
-            txt_spec,
-            img_spec,
-            txt_spec,
             pl.BlockSpec((None, None, tokens, lanes), lambda s, h: (s, h, 0, 0)),
+            pl.BlockSpec((2, None, 8, full), lambda s, h: (0, s, 0, 0)),
+            pl.BlockSpec((2, lanes, full), lambda s, h: (0, h, 0)),
         ],
-        out_specs=[img_spec, txt_spec, sums, sums],
-        out_shape=[
-            struct(q_img.shape, BF),
-            struct(q_txt.shape, BF),
-            struct((blocks, seqs, tokens, width), BF),
-            struct((blocks, seqs, tokens, width), BF),
+        out_specs=heads + rows + columns + [sums, sums],
+        out_shape=[struct(a.shape, BF) for a in q]
+        + [struct(a.shape, BF) for a in x_full]
+        + [struct((seqs, c, lanes), F32) for c in counts]
+        + [struct((blocks, seqs, tokens, width), BF)] * 2,
+        compiler_params=pltpu.CompilerParams(vmem_limit_bytes=VMEM_LIMIT),
+    )(*q, *attended, *x_full, *cot_full, *branch, *d_two, keys, keys, lse, wide, out_full)
+
+
+def outer_sums(cond_rows, every, seqs):
+    terms, depth = cond_rows.shape
+    pods, _, width = every.shape
+    kinds = 6
+    room = -(-3 * terms // 16) * 16
+
+    def kernel(cond_ref, every_ref, out_ref):
+        first = pl.program_id(0) * (seqs * kinds)
+        for kind in range(kinds):
+            value = jnp.concatenate(
+                [every_ref[p, pl.ds(first + q * kinds + kind, 1), :] for p in range(pods) for q in range(seqs)], axis=0
+            )
+            high = value.astype(BF).astype(F32)
+            mid = (value - high).astype(BF).astype(F32)
+            low = (value - high - mid).astype(BF).astype(F32)
+            blank = [jnp.zeros((room - 3 * terms, width), F32)] if room > 3 * terms else []
+            right = jnp.concatenate([high, mid, low] + blank, axis=0).astype(BF)
+            out_ref[kind] = lax.dot_general(cond_ref[...], right, OVER_FIRST, preferred_element_type=F32)
+
+    left = jnp.pad(jnp.concatenate([cond_rows] * 3, axis=0), ((0, room - 3 * terms), (0, 0))).astype(BF)
+    return pl.pallas_call(
+        kernel,
+        name="outer_sums",
+        grid=(2,),
+        in_specs=[
+            pl.BlockSpec(left.shape, lambda z: (0, 0)),
+            pl.BlockSpec(every.shape, lambda z: (0, 0, 0)),
         ],
+        out_specs=pl.BlockSpec((None, kinds, depth, width), lambda z: (z, 0, 0, 0)),
+        out_shape=struct((2, kinds, depth, width), F32),
         compiler_params=pltpu.CompilerParams(vmem_limit_bytes=VMEM_LIMIT),
-    )(q_img, q_txt, keys, keys, o_img, o_txt, do_img, do_txt, lse)
+    )(left, every)
 
 
 OVER_FIRST = (((0,), (0,)), ((), ()))
@@ -797,8 +905,9 @@
     spans = chunk_rows(img, txt, img // 4)
     count = len(spans)
     slots = cols - 1
-    kinds = ("up", "down")
+    kinds, streams = ("up", "down"), ((1,), (0, 1))
     weights = (w_up, w_down)
+    full_shapes = [(len(z),) + gathered_shape(k, w.shape)[1:] for k, z, w in zip(kinds, streams, weights)]
     subs = 2
 
     def kernel(*refs):
@@ -811,9 +920,16 @@
         sems, (local_in, local_out, ws, wr) = refs[:4], refs[4:]
         place = lax.axis_index("col")
         line = LineSum(spans, parts, outs, cols, place, width, bufs, sems)
-        flow = WeightFlow(kinds, shards, fulls, subs, ws, wr)
+        flow = WeightFlow(kinds, streams, shards, fulls, subs, ws, wr)
         owns = [
-            OwnCopy(shards[n], stages[n], flow.own_view(n), local_in.at[n], local_out.at[n]) for n in range(2)
+            OwnCopy(
+                shards[n].at[pl.ds(streams[n][0], len(streams[n]))],
+                stages[n],
+                flow.own_view(n),
+                local_in.at[n],
+                local_out.at[n],
+            )
+            for n in range(2)
         ]
         for own in owns:
             own.begin()
@@ -824,21 +940,20 @@
         for own in owns:
             own.settle()
         pieces = len(flow.pieces)
-        y_next = x_next = 0
+        y_turn = [1 + (4 * piece) // 3 for piece in range(pieces)]
         for turn in range(1, line.turns):
             line.turn(turn)
-            while y_next < pieces and y_next * line.turns <= (turn - 2) * pieces:
-                flow.relay_y(y_next)
-                y_next += 1
-                if y_next >= 2:
-                    flow.relay_x(x_next)
-                    x_next += 1
-        while x_next < pieces:
-            if y_next < pieces:
-                flow.relay_y(y_next)
-                y_next += 1
-            flow.relay_x(x_next)
-            x_next += 1
+            for piece in range(pieces):
+                if y_turn[piece] == turn:
+                    flow.relay_y(piece)
+                if y_turn[piece] + 2 == turn:
+                    flow.relay_x(piece)
+        for piece in range(pieces):
+            if y_turn[piece] >= line.turns:
+                flow.relay_y(piece)
+        for piece in range(pieces):
+            if y_turn[piece] + 2 >= line.turns:
+                flow.relay_x(piece)
         flow.finish()
         line.finish()
         for own in owns:
@@ -846,17 +961,16 @@
 
     return communicate(
         kernel,
-        "sum_branch",
         2,
         out_shape=[struct(part_img.shape, BF), struct(part_txt.shape, BF)]
-        + [struct(gathered_shape(k, w.shape), BF) for k, w in zip(kinds, weights)],
+        + [struct(shape, BF) for shape in full_shapes],
         in_specs=[VM, VM, ANY, ANY],
         out_specs=[VM, VM, ANY, ANY],
-        scratch_shapes=[pltpu.VMEM(w.shape, BF) for w in weights]
+        scratch_shapes=[pltpu.VMEM((len(z),) + w.shape[1:], BF) for z, w in zip(streams, weights)]
         + line_buffers(spans, slots, width)
         + [pltpu.SemaphoreType.DMA((count, 2, slots))] * 4
         + [pltpu.SemaphoreType.DMA((2,))] * 2
-        + [pltpu.SemaphoreType.DMA(WeightFlow.sem_shape(2, subs))] * 2,
+        + [pltpu.SemaphoreType.DMA(WeightFlow.sem_shape(streams, subs))] * 2,
     )(part_img, part_txt, *weights)
 
 
@@ -890,161 +1004,6 @@
     return lax.dot_general(left_own, right_own, OVER_FIRST, preferred_element_type=F32) + lax.dot_general(
         left_sib, right_sib, OVER_FIRST, preferred_element_type=F32
     )
-
-
-def sum_hidden(cols, back, hidden, d_pre, act, d_mlp, first_hidden, attended):
-    img, full = back[0].shape
-    txt = back[1].shape[0]
-    tokens = (img, txt)
-    width = full // cols
-    units = d_pre[0].shape[1]
-    block = full // 4
-    spans = chunk_rows(img, txt, img // 4)
-    count = len(spans)
-    slots = cols - 1
-    tile = 512 if units % 512 == 0 else units
-
-    def kernel(*refs):
-        parts, hid, pre, acts, mlp, one, att = (refs[2 * n : 2 * n + 2] for n in range(7))
-        refs = refs[14:]
-        outs, refs = refs[:2], refs[2:]
-        up_own, up_far, down_near = refs[:3]
-        one_sib, att_sib = refs[3:5], refs[5:7]
-        refs = refs[7:]
-        hid_sib, pre_sib, act_sib, mlp_sib = (refs[2 * n : 2 * n + 2] for n in range(4))
-        refs = refs[8:]
-        down_own, far_out, far_in = refs[:3]
-        refs = refs[3:]
-        bufs, refs = refs[: 2 * count], refs[2 * count :]
-        sems, (ss, rs, ys, yr) = refs[:4], refs[4:]
-        place = lax.axis_index("col")
-        row = lax.axis_index("row")
-        core, y_of = lax.rem(row, 2), row // 2
-        other = 1 - core
-        far = flip_far(row)
-        line = LineSum(spans, parts, outs, cols, place, width, bufs, sems)
-        pairs = []
-        for s in range(2):
-            pairs += [(acts[s], act_sib[s])] + row_parts(mlp[s], mlp_sib[s], other)
-        for s in range(2):
-            pairs += [(pre[s], pre_sib[s])] + row_parts(hid[s], hid_sib[s], other)
-        for s in range(2):
-            pairs += [(att[s], att_sib[s])] + row_parts(one[s], one_sib[s], other)
-        sibling = Sibling(pairs, ss, rs)
-        greet(others("row", 4) + others("col", cols))
-        line.turn(0)
-        sibling.start()
-        line.turn(1)
-
-        def down(s, y, write):
-            right_own = mlp[s][:, aligned(2 * y + core, block)]
-            right_sib = mlp_sib[s][y]
-
-            @pl.loop(0, units // tile)
-            def _(at):
-                cut = aligned(at, tile)
-                write(cut, token_product(acts[s][:, cut], act_sib[s][:, cut], right_own, right_sib))
-
-        def up(s, y, write):
-            left_own = hid[s][:, aligned(2 * y + core, block)]
-            left_sib = hid_sib[s][y]
-
-            @pl.loop(0, units // tile)
-            def _(at):
-                cut = aligned(at, tile)
-                write(cut, token_product(left_own, left_sib, pre[s][:, cut], pre_sib[s][:, cut]))
-
-        def across(s):
-            return send(far_out.at[s], far_in.at[s], ys.at[s], yr.at[s], "row", far)
-
-        def down_to_far(s):
-            sibling.land(3 * s, 3 * s + 1, 3 * s + 2)
-
-            def write(cut, value):
-                far_out[s, cut, :] = value.astype(BF)
-
-            down(s, 1 - y_of, write)
-            across(s).start()
-
-        def down_here(s):
-            def write(cut, value):
-                down_own[s, cut, :] = value
-
-            down(s, y_of, write)
-
-        def up_to_far(s):
-            sibling.land(6 + 3 * s, 7 + 3 * s, 8 + 3 * s)
-
-            def write(cut, value):
-                up_far[s, :, cut] = value.astype(BF)
-
-            up(s, 1 - y_of, write)
-
-        def up_here(s):
-            def write(cut, value):
-                up_own[s, :, cut] = value
-
-            up(s, y_of, write)
-
-        def down_sum(s):
-            across(s).wait_recv()
-
-            @pl.loop(0, units // tile)
-            def _(at):
-                cut = aligned(at, tile)
-                down_near[s, cut, :] = (down_own[s, cut, :] + far_in[s, cut, :].astype(F32)).astype(BF)
-
-        work = {
-            1: lambda: down_to_far(0),
-            2: lambda: down_to_far(1),
-            3: lambda: down_here(0),
-            4: lambda: (down_here(1), up_to_far(1)),
-            5: lambda: up_to_far(0),
-            6: lambda: up_here(0),
-            7: lambda: up_here(1),
-            8: lambda: down_sum(0),
-        }
-        for turn in range(1, line.turns):
-            if turn > 1:
-                line.turn(turn)
-            if turn in work:
-                work[turn]()
-        down_sum(1)
-        sibling.land(*range(12, 18))
-        sibling.finish()
-        for s in range(2):
-            across(s).wait_send()
-        line.finish()
-
-    arrays = list(back) + list(hidden) + list(d_pre) + list(act) + list(d_mlp) + list(first_hidden) + list(attended)
-    return communicate(
-        kernel,
-        "sum_hidden",
-        3,
-        out_shape=[struct(b.shape, BF) for b in back]
-        + [
-            struct((2, block, units), F32),
-            struct((2, block, units), BF),
-            struct((2, units, block), BF),
-        ]
-        + [struct((2, t, block), BF) for t in tokens]
-        + [struct(a.shape, BF) for a in attended],
-        in_specs=[VM] * 10 + [ANY] * 4,
-        out_specs=[VM] * 5 + [ANY] * 4,
-        scratch_shapes=[pltpu.VMEM((2, t, block), BF) for t in tokens]
-        + [pltpu.VMEM((t, units), BF) for t in tokens]
-        + [pltpu.VMEM((t, units), BF) for t in tokens]
-        + [pltpu.VMEM((2, t, block), BF) for t in tokens]
-        + [
-            pltpu.VMEM((2, units, block), F32),
-            pltpu.VMEM((2, units, block), BF),
-            pltpu.VMEM((2, units, block), BF),
-        ]
-        + line_buffers(spans, slots, width)
-        + [pltpu.SemaphoreType.DMA((count, 2, slots))] * 4
-        + [pltpu.SemaphoreType.DMA((18,))] * 2
-        + [pltpu.SemaphoreType.DMA((2,))] * 2,
-    )(*arrays)
 
 
 class GradFlow:
@@ -1125,8 +1084,147 @@
         return found
 
 
+def sum_hidden(pods, cols, back, hidden, d_pre, act, d_mlp, first_hidden, attended):
+    img, full = back[0].shape
+    txt = back[1].shape[0]
+    tokens = (img, txt)
+    width = full // cols
+    units = d_pre[0].shape[1]
+    block = full // 4
+    spans = chunk_rows(img, txt, img // 4)
+    count = len(spans)
+    slots = cols - 1
+    tile = 512 if units % 512 == 0 else units
+
+    def kernel(*refs):
+        parts, hid, pre, acts, mlp, one, att = (refs[2 * n : 2 * n + 2] for n in range(7))
+        refs = refs[14:]
+        outs, refs = refs[:2], refs[2:]
+        up_own, up_far, grad_down = refs[:3]
+        one_sib, att_sib = refs[3:5], refs[5:7]
+        refs = refs[7:]
+        hid_sib, pre_sib, act_sib, mlp_sib = (refs[2 * n : 2 * n + 2] for n in range(4))
+        refs = refs[8:]
+        grad_scratch, refs = refs[:8], refs[8:]
+        bufs, refs = refs[: 2 * count], refs[2 * count :]
+        sems, (ss, rs) = refs[:4], refs[4:]
+        place = lax.axis_index("col")
+        row = lax.axis_index("row")
+        core, y_of = lax.rem(row, 2), row // 2
+        other = 1 - core
+        line = LineSum(spans, parts, outs, cols, place, width, bufs, sems)
+        pairs = []
+        for s in (1, 0):
+            pairs += [(acts[s], act_sib[s])] + row_parts(mlp[s], mlp_sib[s], other)
+        for s in (1, 0):
+            pairs += [(pre[s], pre_sib[s])] + row_parts(hid[s], hid_sib[s], other)
+        for s in (1, 0):
+            pairs += [(att[s], att_sib[s])] + row_parts(one[s], one_sib[s], other)
+        sibling = Sibling(pairs, ss, rs)
+
+        def down(piece, y):
+            s = 1 - piece // 4
+            cut = pl.ds((piece % 4) * (units // 4), units // 4)
+            return token_product(
+                acts[s][:, cut], act_sib[s][:, cut], mlp[s][:, aligned(2 * y + core, block)], mlp_sib[s][y]
+            )
+
+        def down_view(piece):
+            return grad_down.at[1 - piece // 4, pl.ds((piece % 4) * (units // 4), units // 4), :]
+
+        grads = GradFlow(pods, down, down_view, *grad_scratch)
+        greet(others("row", 4) + others("col", cols) + GradFlow.friends(pods))
+        sibling.start()
+        line.turn(0)
+
+        def up(s, y, write):
+            left_own = hid[s][:, aligned(2 * y + core, block)]
+            left_sib = hid_sib[s][y]
+
+            @pl.loop(0, units // tile)
+            def _(at):
+                cut = aligned(at, tile)
+                write(cut, token_product(left_own, left_sib, pre[s][:, cut], pre_sib[s][:, cut]))
+
+        def up_to_far(s):
+            sibling.land(9 - 3 * s, 10 - 3 * s, 11 - 3 * s)
+
+            def write(cut, value):
+                up_far[s, :, cut] = value.astype(BF)
+
+            up(s, 1 - y_of, write)
+
+        def up_here(s):
+            def write(cut, value):
+                up_own[s, :, cut] = value
+
+            up(s, y_of, write)
+
+        def down_to_far(s):
+            sibling.land(3 - 3 * s, 4 - 3 * s, 5 - 3 * s)
+            for piece in range(4):
+                grads.to_far(4 * (1 - s) + piece)
+
+        def down_here(s):
+            for piece in range(4):
+                grads.here(4 * (1 - s) + piece)
+
+        work = {
+            0: lambda: down_to_far(1),
+            1: lambda: down_to_far(0),
+            2: lambda: down_here(1),
+            3: lambda: down_here(0),
+            4: lambda: grads.to_pod(0),
+            5: lambda: grads.to_pod(1),
+            6: lambda: grads.to_pod(2),
+            7: lambda: grads.to_pod(3),
+            8: lambda: (grads.to_pod(4), grads.to_pod(5)),
+            10: lambda: grads.to_pod(6),
+        }
+        for turn in range(line.turns):
+            if turn > 0:
+                line.turn(turn)
+            if turn in work:
+                work[turn]()
+        grads.to_pod(7)
+        for s in (1, 0):
+            up_to_far(s)
+            up_here(s)
+        sibling.land(*range(12, 18))
+        for piece in range(8):
+            grads.done(piece)
+        sibling.finish()
+        for piece in range(8):
+            grads.finish(piece)
+        line.finish()
+
+    arrays = list(back) + list(hidden) + list(d_pre) + list(act) + list(d_mlp) + list(first_hidden) + list(attended)
+    return communicate(
+        kernel,
+        3,
+        out_shape=[struct(b.shape, BF) for b in back]
+        + [
+            struct((2, block, units), F32),
+            struct((2, block, units), BF),
+            struct((2, units, block), F32),
+        ]
+        + [struct((2, t, block), BF) for t in tokens]
+        + [struct(a.shape, BF) for a in attended],
+        in_specs=[VM] * 10 + [ANY] * 4,
+        out_specs=[VM] * 5 + [ANY] * 4,
+        scratch_shapes=[pltpu.VMEM((2, t, block), BF) for t in tokens]
+        + [pltpu.VMEM((t, units), BF) for t in tokens]
+        + [pltpu.VMEM((t, units), BF) for t in tokens]
+        + [pltpu.VMEM((2, t, block), BF) for t in tokens]
+        + GradFlow.scratch(pods, 8, (units // 4, block))
+        + line_buffers(spans, slots, width)
+        + [pltpu.SemaphoreType.DMA((count, 2, slots))] * 4
+        + [pltpu.SemaphoreType.DMA((18,))] * 2,
+    )(*arrays)
+
+
 def sum_keys(pods, cols, d_key, d_value, part_img, part_txt, img, attended, attended_sib, d_branch):
-    blocks, seqs, tokens, width = d_key.shape
+    _, seqs, tokens, width = d_key.shape
     txt = tokens - img
     img_rows, full = part_img.shape
     block = full // 4
@@ -1253,7 +1351,6 @@
 
     return communicate(
         kernel,
-        "sum_keys",
         4,
         out_shape=[
             struct((2, seqs, img, width), BF),
@@ -1282,7 +1379,7 @@
 
 
 def sum_last(
-    pods, cols, d_q, d_kv, qkv, hidden, hidden_sib, xs, cots, branch, d_two, mlp, stat_cols, tables, b_down, up_rows, ada
+    pods, cols, d_q, d_kv, qkv, hidden, hidden_sib, xs, cots, branch, d_two, mlp, stat_cols, tables, b_down, up_rows, slope, ada
 ):
     seqs = tables.shape[2]
     tokens = [x.shape[0] for x in xs]
@@ -1293,7 +1390,7 @@
     spans = chunk_rows(tokens[0], tokens[1], tokens[0] // 4)
     count = len(spans)
     slots = cols - 1
-    pieces = [(s, k) for s in range(2) for k in range(3)]
+    pieces = [(s, k) for s in (1, 0) for k in range(3)]
     lanes = tokens[0] + 128
     firsts = (0, tokens[0])
     mods_rows = 2 * seqs * 6
@@ -1307,24 +1404,38 @@
             return (next(takes), next(takes))
 
         dq, dkv = two(), two()
-        qkv_ref = next(takes)
-        hid, hid_sib, x_ref, cot_ref, bra, dtwo, mlp_ref, stat = (two() for _ in range(8))
-        table_ref, down_ref, up_ref, ada_ref = (next(takes) for _ in range(4))
+        qkv_any = next(takes)
+        hid, hid_sib, x_ref, cot_ref, bra_any, dtwo_any, mlp_ref, stat = (two() for _ in range(8))
+        table_ref, down_ref, up_ref, slope_ref, ada_any = (next(takes) for _ in range(5))
         out_ref, dx_ref = two(), two()
-        grad_ref, every_ref, silu_ref = (next(takes) for _ in range(3))
+        grad_ref, every_ref, rest_ref, mods_sum, silu_ref = (next(takes) for _ in range(5))
         dq_sib, dkv_sib, parts, d_one, grown = (two() for _ in range(5))
         sums_mine, sums_in, pack_mine, pack_in, silu_mine, silu_in = (next(takes) for _ in range(6))
         ss, rs, ms, mr, ps, pr, es, er, cs, cr = (next(takes) for _ in range(10))
         grad_scratch = [next(takes) for _ in range(8)]
         bufs = [next(takes) for _ in range(2 * count)]
         rss, rsr = next(takes), next(takes)
+        qkv_ref, ada_ref = next(takes), next(takes)
+        bra, dtwo = two(), two()
+        loads = next(takes)
         row = lax.axis_index("row")
         place = lax.axis_index("col")
         pod = lax.axis_index("dp")
         core = lax.rem(row, 2)
         mine = aligned(place, width)
+        w_loads = [
+            pltpu.make_async_copy(qkv_any.at[s, k], qkv_ref.at[s, k], loads.at[3 * s + k])
+            for s in (1, 0)
+            for k in range(3)
+        ]
+        late_loads = [pltpu.make_async_copy(ada_any, ada_ref, loads.at[6])]
+        for s in range(2):
+            late_loads.append(pltpu.make_async_copy(bra_any[s].at[:, mine], bra[s], loads.at[7 + s]))
+            late_loads.append(pltpu.make_async_copy(dtwo_any[s].at[:, mine], dtwo[s], loads.at[9 + s]))
+        for load in w_loads + late_loads:
+            load.start()
         reduces = line_reduces(spans, parts, cols, place, width, bufs, rss, rsr)
-        sibling = Sibling([pair for s in range(2) for pair in ((dq[s], dq_sib[s]), (dkv[s], dkv_sib[s]))], ss, rs)
+        sibling = Sibling([pair for s in (1, 0) for pair in ((dq[s], dq_sib[s]), (dkv[s], dkv_sib[s]))], ss, rs)
 
         def projected(own, s, k):
             return own[0][s][...] if k == 0 else own[1][s][k - 1]
@@ -1345,9 +1456,14 @@
         grads = GradFlow(pods, product, out_view, *grad_scratch)
         greet(others("col", cols) + others("row", 4) + others("dp", pods))
         sibling.start()
-
+        sibling.land(0, 1)
+        for k in range(3):
+            grads.to_far(k)
         for number, (s, first, size) in enumerate(spans):
             rows = pl.ds(first, size)
+            if first == 0:
+                for k in range(3):
+                    w_loads[3 * (1 - s) + k].wait()
             term = lax.dot_general(dq[s][rows, :], qkv_ref[s, 0], OVER_LAST, preferred_element_type=F32)
             for k in range(2):
                 term = term + lax.dot_general(
@@ -1355,14 +1471,15 @@
                 )
             parts[s][rows, :] = term.astype(BF)
             reduces[number].step(0)
-        for s in range(2):
-            sibling.land(2 * s, 2 * s + 1)
-            for k in range(3):
-                grads.to_far(3 * s + k)
+        sibling.land(2, 3)
+        for k in range(3):
+            grads.to_far(3 + k)
         for number in range(count):
             reduces[number].step(1)
         for piece in range(6):
             grads.here(piece)
+        for load in late_loads:
+            load.wait()
 
         def segment(s, q):
             return pl.ds(q * counts[s], counts[s])
@@ -1383,8 +1500,8 @@
                 at = (s * seqs + q) * 6
                 column = stat[s][rows, :]
                 cot = cot_ref[s][rows, :].astype(F32)
-                d_hidden = dtwo[s][rows, mine].astype(F32)
-                attn = bra[s][rows, mine].astype(F32) + modulation(s, q, 6)
+                d_hidden = dtwo[s][rows, :].astype(F32)
+                attn = bra[s][rows, :].astype(F32) + modulation(s, q, 6)
                 gate_a, gate_m = modulation(s, q, 2), modulation(s, q, 5)
                 middle = x_ref[s][rows, :].astype(F32) + gate_a * attn
                 mlp_branch = mlp_ref[s][rows, :] + down_ref[pl.ds(s, 1), :]
@@ -1521,7 +1638,7 @@
             grads.to_pod(piece)
         for step in range(1, cols):
             silu_copy(step).wait()
-        silu_ref[...] = ordered(silu_mine[...], silu_in, place, cols)
+        silu_ref[...] = ordered(silu_mine[...], silu_in, place, cols) * slope_ref[...]
         for piece in range(6):
             grads.done(piece)
         for step in range(1, pods):
@@ -1529,6 +1646,11 @@
             at = every_ref.at[source]
             send(at, at, es.at[step - 1], er.at[step - 1], "dp", source).wait_recv()
             every_copy(step).wait_send()
+        rest_ref[...] = sum(every_ref[p, pl.ds(mods_rows, 8 + up_count), :] for p in range(pods))
+        for s in range(2):
+            mods_sum[pl.ds(6 * s, 6), :] = sum(
+                every_ref[p, pl.ds((s * seqs + q) * 6, 6), :] for p in range(pods) for q in range(seqs)
+            )
         sibling.finish()
         for number in range(count):
             reduces[number].finish()
@@ -1547,22 +1669,23 @@
         + list(d_two)
         + list(mlp)
         + list(stat_cols)
-        + [tables, b_down, up_rows, ada]
+        + [tables, b_down, up_rows, slope, ada]
     )
     dma = pltpu.SemaphoreType.DMA
     return communicate(
         kernel,
-        "sum_last",
         5,
         out_shape=[struct((t, width), BF) for t in tokens]
         + [struct((t, width), F32) for t in tokens]
         + [
             struct((2, 3, block, width), F32),
             struct((pods, pack_rows, width), F32),
+            struct((8 + up_count, width), F32),
+            struct((12, width), F32),
             struct((seqs, width), F32),
         ],
-        in_specs=[VM] * len(arrays),
-        out_specs=[VM] * 7,
+        in_specs=[VM] * 4 + [ANY] + [VM] * 8 + [ANY] * 4 + [VM] * 8 + [ANY],
+        out_specs=[VM] * 9,
         scratch_shapes=[pltpu.VMEM(a.shape, BF) for a in d_q]
         + [pltpu.VMEM(a.shape, BF) for a in d_kv]
         + [pltpu.VMEM((t, full), BF) for t in tokens]
@@ -1582,7 +1705,10 @@
         + [dma((slots,))] * 2
         + GradFlow.scratch(pods, 6, (block, width))
         + line_buffers(spans, slots, width)
-        + [dma((count, 2, slots))] * 2,
+        + [dma((count, 2, slots))] * 2
+        + [pltpu.VMEM(qkv.shape, BF), pltpu.VMEM(ada.shape, BF)]
+        + [pltpu.VMEM((t, width), BF) for t in tokens] * 2
+        + [dma((11,))],
     )(*arrays)
 
 
@@ -1609,10 +1735,6 @@
 
 def dot_back(left, right):
     return jnp.einsum("te,de->td", left, right, preferred_element_type=F32)
-
-
-def dot_tokens(left, right):
-    return jnp.einsum("td,te->de", left, right, preferred_element_type=F32)
 
 
 def local(
@@ -1642,12 +1764,14 @@
 
     cond_wide = condition.astype(F32)
     cond_act = jax.nn.silu(cond_wide).astype(BF)
+    sigmoid_cond = jax.nn.sigmoid(cond_wide)
     ada = jnp.transpose(w_ada, (0, 2, 1, 3))
     table = jnp.einsum("sc,zkcd->zskd", cond_act, ada, preferred_element_type=F32)
     table = jnp.pad(table, ((0, 0), (0, 0), (0, 2), (0, 0)))
     bias_six = jnp.broadcast_to(b_ada[:, None], (2, seqs, 6, width))
     bias_rest = jnp.broadcast_to(b_out[:, None, None], (2, seqs, 2, width))
-    *x_full, qkv_full, out_full, tables = prologue(
+    *x_full, qkv_full, out_full, tables, all_cond = prologue(
+        dp_count,
         col_count,
         x_img,
         x_txt,
@@ -1655,32 +1779,24 @@
         w_out,
         table,
         jnp.concatenate([bias_six, bias_rest], axis=2),
+        jnp.pad(cond_act.astype(F32), ((0, 8 - seqs), (0, 0))),
     )
     wide = jnp.transpose(tables, (1, 2, 3, 0, 4)).reshape(2, seqs, 8, full)
 
     def mod(stream, position):
         return wide[stream, :, position][:, None, :]
 
+    flat = [a.reshape(seqs * counts[s], full) for s, a in enumerate(x_full)]
+    *front_out, cot_one, cot_two, up_one = front(
+        col_count, flat, wide, qkv_full, b_qv, (cot_img, cot_txt), w_up
+    )
+    cot_full = [cot_one, cot_two]
+    hidden_one, queries, keys = front_out[:2], front_out[2:4], front_out[4]
+    attended, lse = front_out[5:7], front_out[7]
     resid = [array.astype(F32) for array in x_full]
-    stats_one = [stats(array) for array in resid]
-    normed_one = [(resid[s] - stats_one[s][0]) * stats_one[s][1] for s in range(2)]
-    hidden_one = [
-        (normed_one[s] * (1.0 + mod(s, 1)) + mod(s, 0)).astype(BF).reshape(seqs * counts[s], full)
-        for s in range(2)
-    ]
-    queries, keyed = [], []
-    for s in range(2):
-        shape = (seqs, counts[s], width)
-        q = (dot_f32(hidden_one[s], qkv_full[s, 0]) + b_qv[s, 0]).astype(BF).reshape(shape)
-        k = dot_f32(hidden_one[s], qkv_full[s, 1]).astype(BF).reshape(shape)
-        v = (dot_f32(hidden_one[s], qkv_full[s, 2]) + b_qv[s, 1]).astype(BF).reshape(shape)
-        queries.append(q)
-        keyed.append(jnp.stack([k, v], axis=0))
-    keys, *cot_full = gather_keys(col_count, keyed[0], keyed[1], cot_img, cot_txt)
-    o_img, o_txt, lse = attend(queries[0], queries[1], keys)
-    attended = [o_img.reshape(seqs * img, width), o_txt.reshape(seqs * txt, width)]
     out_terms = [dot_f32(attended[s], out_full[s]).astype(BF) for s in range(2)]
-    *branch_sum, up_full, down_full = sum_branch(col_count, out_terms[0], out_terms[1], w_up, w_down)
+    *branch_sum, up_two, down_full = sum_branch(col_count, out_terms[0], out_terms[1], w_up, w_down)
+    up_full = [up_one[0], up_two[0]]
     attn_branch = [
         branch_sum[s].reshape(seqs, counts[s], full).astype(F32) + mod(s, 6) for s in range(2)
     ]
@@ -1705,7 +1821,8 @@
         up_back.append(dot_back(d_pre_bf[s], up_full[s]).astype(BF))
         down_terms.append(dot_f32(act[s], down_full[s]).astype(BF))
 
-    d_two_img, d_two_txt, up_own, up_far, down_near, *paired = sum_hidden(
+    d_two_img, d_two_txt, up_own, up_far, grad_down, *paired = sum_hidden(
+        dp_count,
         col_count, up_back, hidden_two, d_pre_bf, act, d_mlp_bf, hidden_one, attended
     )
     hidden_pairs, attended_pairs = paired[:2], paired[2:]
@@ -1716,52 +1833,49 @@
         step = 1
         while step < dp_count:
             perm = [(d, d ^ step) for d in range(dp_count)]
-            value = rounded.astype(F32) + lax.ppermute(rounded, "dp", perm).astype(F32)
+            moved = lax.ppermute(rounded, "dp", perm)
+            value = rounded.astype(F32) + moved.astype(F32)
             rounded = value.astype(BF)
             step *= 2
         return value
 
-    grad_down = pod_sum(down_near)
-    up_near = (up_own + lax.ppermute(up_far, "row", far_perm).astype(F32)).astype(BF)
-
-    d_hidden_two = [d_two_img, d_two_txt]
-    d_hidden_two = [
-        d_hidden_two[s].reshape(seqs, counts[s], full).astype(F32) for s in range(2)
-    ]
-    d_branch_bf, stat_cols = [], []
-    for s in range(2):
-        grown = d_hidden_two[s] * (1.0 + mod(s, 4))
-        first = jnp.mean(grown, axis=-1, keepdims=True)
-        second = jnp.mean(grown * normed_two[s], axis=-1, keepdims=True)
-        d_middle = cot_full[s].astype(F32) + stats_two[s][1] * (grown - first - normed_two[s] * second)
-        d_branch_bf.append((d_middle * mod(s, 2)).astype(BF).reshape(seqs * counts[s], full))
-        columns = [*stats_one[s], *stats_two[s], first, second, jnp.zeros_like(first), jnp.zeros_like(first)]
-        stat_cols.append(jnp.concatenate(columns, axis=-1).reshape(seqs * counts[s], 8))
-    d_att = [
-        dot_back(d_branch_bf[s], out_full[s]).astype(BF).reshape(seqs, counts[s], width)
-        for s in range(2)
-    ]
-    dq_img, dq_txt, d_key, d_value = attend_back(
-        queries[0], queries[1], keys, o_img, o_txt, d_att[0], d_att[1], lse
+    def up_near(own, far):
+        return (own + lax.ppermute(far, "row", far_perm).astype(F32)).astype(BF)
+
+    near_one = up_near(up_own[0], up_far[0])
+
+    d_two = [d_two_img, d_two_txt]
+    shaped = [[a.reshape(seqs, counts[s], full) for a in (branch_sum[s], d_two[s])] for s in range(2)]
+    dq_img, dq_txt, *d_branch, stat_img, stat_txt, d_key, d_value = attend_back(
+        [queries[s].reshape(seqs, counts[s], width) for s in range(2)],
+        keys,
+        [attended[s].reshape(seqs, counts[s], width) for s in range(2)],
+        lse,
+        x_full,
+        cot_full,
+        [shaped[0][0], shaped[1][0]],
+        [shaped[0][1], shaped[1][1]],
+        wide,
+        out_full,
     )
-    d_key, d_value, up_near = lax.optimization_barrier((d_key, d_value, up_near))
-    grad_up = pod_sum(up_near)
+    d_branch_bf = [d_branch[s].reshape(seqs * counts[s], full) for s in range(2)]
+    stat_cols = [stat_img.reshape(seqs * img, 2 * HD), stat_txt.reshape(seqs * txt, 2 * HD)]
+    d_key, d_value, near_one, down_terms, far_two = lax.optimization_barrier(
+        (d_key, d_value, near_one, down_terms, up_far[1])
+    )
+    grad_up_one = pod_sum(near_one)
+    near_two = up_near(up_own[1], far_two)
     kv_img, kv_txt, mlp_img, mlp_txt, grad_out = sum_keys(
-        dp_count,
-        col_count,
-        d_key,
-        d_value,
-        down_terms[0],
-        down_terms[1],
-        img,
-        attended,
-        attended_pairs,
-        d_branch_bf,
+        dp_count, col_count, d_key, d_value, *down_terms, img, attended, attended_pairs, d_branch_bf
     )
+
+    kv_img, kv_txt, near_two = lax.optimization_barrier((kv_img, kv_txt, near_two))
+    grad_up_two = pod_sum(near_two)
+    grad_up = jnp.stack([grad_up_one, grad_up_two], axis=0)
 
     flat = [(seqs * c, width) for c in counts]
     up_rows = jnp.concatenate([jnp.sum(d_pre[s], axis=0).reshape(-1, width) for s in range(2)], axis=0)
-    out_img, out_txt, dx_img, dx_txt, grad_qkv, every, d_silu = sum_last(
+    out_img, out_txt, dx_img, dx_txt, grad_qkv, every, rest, mods_sum, d_condition = sum_last(
         dp_count,
         col_count,
         [dq_img.reshape(flat[0]), dq_txt.reshape(flat[1])],
@@ -1772,30 +1886,23 @@
         [x_img.reshape(flat[0]), x_txt.reshape(flat[1])],
         [cot_img.reshape(flat[0]), cot_txt.reshape(flat[1])],
         branch_sum,
-        [d_two_img, d_two_txt],
+        d_two,
         [mlp_img, mlp_txt],
         stat_cols,
         tables,
         b_down,
         up_rows,
+        sigmoid_cond * (1.0 + cond_wide * (1.0 - sigmoid_cond)),
         ada,
     )
     grad_qkv = jnp.transpose(grad_qkv, (0, 2, 1, 3))
-    mods_count = 2 * seqs * 6
-    rest = jnp.sum(every[:, mods_count:], axis=0)
     grad_bqv = rest[:4].reshape(2, 2, width)
     grad_bout = rest[4:6]
     grad_bdown = rest[6:8]
     grad_bup = rest[8:].reshape(2, -1)
-    all_mods = every[:, :mods_count].reshape(dp_count, 2, seqs, 6, width)
-    all_cond = lax.all_gather(cond_act, "dp", axis=0, tiled=False).astype(F32)
-    grad_ada = jnp.einsum(
-        "psc,pzskd->zkcd", all_cond, all_mods, precision=lax.Precision.HIGHEST
-    )
+    grad_ada = outer_sums(all_cond[:, :seqs].reshape(dp_count * seqs, width), every, seqs)
     grad_ada = jnp.transpose(grad_ada, (0, 2, 1, 3))
-    grad_bada = jnp.sum(all_mods, axis=(0, 2))
-    sigmoid_cond = jax.nn.sigmoid(cond_wide)
-    d_condition = d_silu * sigmoid_cond * (1.0 + cond_wide * (1.0 - sigmoid_cond))
+    grad_bada = mods_sum.reshape(2, 6, width)
     return (
         out_img.reshape(x_img.shape),
         out_txt.reshape(x_txt.shape),
@@ -1833,8 +1940,12 @@
         P("dp", "row", "col"),
         P("dp", "row", "col"),
     )
+
+    def body(*args):
+        return local(mesh.shape["dp"], mesh.shape["row"], mesh.shape["col"], *args)
+
     return jax.shard_map(
-        partial(local, mesh.shape["dp"], mesh.shape["row"], mesh.shape["col"]),
+        body,
         mesh=mesh,
         in_specs=placed,
         out_specs=(

time: 577 us -> 530 us (0.919)
  the two profiles are of different devices: /device:TPU:0 before, /device:TPU:9 now
where the time goes in v2:
time: 530 us; the launch traced here: 521 us
  Pallas kernels  432 us (82%)
  matrix products  38.8 us (7%)
  local copies, waits for them, and re-layouts  25.2 us (5%)
  other arithmetic  20.4 us (4%)
    pallas_call x1, Pallas kernels, sum_hidden(): communicate(kernel, 3, out_shape=[struct(b.shape, BF) for b in back] + [s...  96.2 us
    pallas_call x1, Pallas kernels, sum_last(): communicate(kernel, 5, out_shape=[struct((t, width), BF) for t in tokens]...  76.7 us
    pallas_call x1, Pallas kernels, sum_keys(): communicate(kernel, 4, out_shape=[struct((2, seqs, img, width), BF), stru...  66.7 us
    pallas_call x1, Pallas kernels, sum_branch(): communicate(kernel, 2, out_shape=[struct(part_img.shape, BF), struct(part...  62.9 us
    pallas_call x1, Pallas kernels, front(): communicate(kernel, 1, out_shape=[struct((t, full), BF) for t in tokens]...  50.5 us
    pallas_call x1, Pallas kernels, prologue(): communicate(kernel, 0, out_shape=[struct(s, BF) for s in full_shapes] + [...  47.8 us
    pallas_call x1, Pallas kernels, attend_back(): pl.pallas_call(kernel, name='attend_back', grid=(seqs, pairs), in_specs=h...  26.9 us
    dot_general x6, matrix products, dot_f32(): return jnp.einsum('td,de->te', left, right, preferred_element_type=F32)  21.2 us
  transfers between devices with their start and end apart: 4, of which 0 were waited for; matrix products, arithmetic and copies ran while one was open for 5% of the time, Pallas kernels for 34%

profile of v2, /device:TPU:9, one launch (start us, length us, event | category | flops | bytes accessed | tf_op | source)
XLA Modules:
  0.0 521.2 jit_solution(11024756799122452099)
XLA Ops:
  4.1 2.6 fusion.73
  8.0 47.8 %shard_map.262 = (bf16[2,256,1536]{2,1,0:T(8,128)(2,1)}, bf16[2,32,1536]{2,1,0:T(8,128)(2,1)}, bf16[2,3,1536,384]{3,2,1,0:T(8,128)(2,1)}, bf16[2,384,1536]{2,1,0...) custom-call(bf16[2,256,384]{2,1,0:T(8,128)(2,1)} %refs_0_.1, bf16[2,32,384]{2,1,0:T(8,128)(2,1)} %refs_1_.1, ...), custom_call_target="tpu_custom_call" | custom-call | tf_op jit(solution)/shard_map/pallas_call | solution.py:447
  57.4 50.5 %shard_map.263 = (bf16[512,1536]{1,0:T(8,128)(2,1)}, bf16[64,1536]{1,0:T(8,128)(2,1)}, bf16[512,384]{1,0:T(8,128)(2,1)}, bf16[64,384]{1,0:T(8,128)(2,1)}, bf16[4...) custom-call(bf16[512,1536]{1,0:T(8,128)(2,1)} %bitcast.144, ...), custom_call_target="tpu_custom_call" | custom-call | tf_op jit(solution)/shard_map/pallas_call | solution.py:638
  108.0 1.8 convolution_convert_fusion.1.refs_1_
  109.8 3.1 convolution_convert_fusion.refs_0_
  112.9 62.9 %shard_map.264 = (bf16[512,1536]{1,0:T(8,128)(2,1)}, bf16[64,1536]{1,0:T(8,128)(2,1)}, bf16[1,1536,1536]{2,1,0:T(8,128)(2,1)}, bf16[2,1536,1536]{2,1,0:T(8,128)(2,1)}) custom-call(bf16[512,1536]{1,0:T(8,128)(2,1)} %convolution_convert_fusion.refs_0_, bf16[64,1536]{1,0:T(8,128)(2,1)} %convolution_convert_fusion.1.refs_1_, bf16[2,384,1536]{2,1,0:T(8,128)(2,1)} %refs_2_.1, ...), custom_call_target="tpu_custom_call" | custom-call | tf_op jit(solution)/shard_map/pallas_call | solution.py:962
  178.3 2.3 fusion.51
  183.5 3.9 fusion.78
  187.4 2.2 fusion.45.refs_1_
  191.2 4.4 multiply_convert_fusion
  195.6 5.1 fusion.77
  200.7 3.7 fusion.34.refs_0_
  204.4 96.2 %shard_map.265 = (bf16[512,1536]{1,0:T(8,128)(2,1)}, bf16[64,1536]{1,0:T(8,128)(2,1)}, f32[2,384,1536]{2,1,0:T(8,128)}, bf16[2,384,1536]{2,1,0:T(8,128)(2,1)}, f...) custom-call(bf16[512,1536]{1,0:T(8,128)(2,1)} %fusion.34.refs_0_, ...), custom_call_target="tpu_custom_call" | custom-call | tf_op jit(solution)/shard_map/pallas_call | solution.py:1202
  300.6 1.8 slice_bitcast_fusion
  303.1 26.9 %attend_back.1 = (bf16[2,256,384]{2,1,0:T(8,128)(2,1)}, bf16[2,32,384]{2,1,0:T(8,128)(2,1)}, bf16[2,256,1536]{2,1,0:T(8,128)(2,1)}, bf16[2,32,1536]{2,1,0:T(8,12...) custom-call(bf16[2,256,384]{2,1,0:T(8,128)(2,1)} %bitcast.182, ...), custom_call_target="tpu_custom_call" | custom-call | tf_op jit(solution)/shard_map/attend_back/pallas_call | solution.py:762
  330.1 4.2 fusion.48.refs_3_
  334.3 6.1 %fusion.31.refs_2_ = bf16[512,1536]{1,0:T(8,128)(2,1)} fusion(bf16[512,1536]{1,0:T(8,128)(2,1)S(1)} %copy-done.12, bf16[2,1536,1536]{2,1,0:T(8,128)(2,1)} %get-tuple-element.89), kind=kOutput, calls=%fused_computation.35 | convolution fusion | flops 2416705536 | bytes 7864320 | tf_op jit(solution)/shard_map/td,de->te/dot_general | solution.py:1733
  344.0 66.7 %shard_map.266 = (bf16[2,2,256,384]{3,2,1,0:T(8,128)(2,1)}, bf16[2,2,32,384]{3,2,1,0:T(8,128)(2,1)}, f32[512,384]{1,0:T(8,128)}, f32[64,384]{1,0:T(8,128)}, f32[2,384,384]{2,1,0:T(8,128)}) custom-call(bf16[4,2,288,384]{3,2,1,0:T(8,128)(2,1)} %get-tuple-element.104.refs_0_, bf16[4,2,288,384]{3,2,1,0:T(8,128)(2,1)} %get-tuple-element.105.refs_1_, ...), custom_call_target="tpu_custom_call" | custom-call | tf_op jit(solution)/shard_map/pallas_call | solution.py:1352
  410.7 2.4 fusion.37
  417.3 76.7 %shard_map.267 = (bf16[512,384]{1,0:T(8,128)(2,1)}, bf16[64,384]{1,0:T(8,128)(2,1)}, f32[512,384]{1,0:T(8,128)}, f32[64,384]{1,0:T(8,128)}, f32[2,3,384,384]{3,2...) custom-call(bf16[512,384]{1,0:T(8,128)(2,1)} %bitcast.183, ...), custom_call_target="tpu_custom_call" | custom-call | tf_op jit(solution)/shard_map/pallas_call | solution.py:1675
  500.6 4.5 outer_sums.1
  508.5 2.7 pad_maximum_fusion
  514.7 1.8 copy.74
  518.6 2.2 copy.76
  (128 shorter events, 37.2 us)
Async XLA Ops:
  0.6 6.0 %copy-start.23 = (f32[2,384]{1,0:T(2,128)S(1)}, f32[2,384]{1,0:T(2,128)}, u32[]{:S(2)}) copy-start(f32[2,384]{1,0:T(2,128)} %param.21) | copy-start | bytes 9220
  57.4 50.5 %copy-start.6 = (bf16[2,384,1536]{2,1,0:T(8,128)(2,1)S(1)}, bf16[2,384,1536]{2,1,0:T(8,128)(2,1)}, u32[]{:S(2)}) copy-start(bf16[2,384,1536]{2,1,0:T(8,128)(2,1)} %get-tuple-element.86.refs_16_) | copy-start | bytes 7077892
  112.9 62.9 %copy-start.8 = (bf16[2,32,1536]{2,1,0:T(8,128)(2,1)S(1)}, bf16[2,32,1536]{2,1,0:T(8,128)(2,1)}, u32[]{:S(2)}) copy-start(bf16[2,32,1536]{2,1,0:T(8,128)(2,1)} %get-tuple-element.77.refs_5_) | copy-start | bytes 589828
  112.9 65.3 %copy-start = (bf16[2,256,1536]{2,1,0:T(8,128)(2,1)S(1)}, bf16[2,256,1536]{2,1,0:T(8,128)(2,1)}, u32[]{:S(2)}) copy-start(bf16[2,256,1536]{2,1,0:T(8,128)(2,1)} %get-tuple-element.76.refs_4_) | copy-start | bytes 4718596
  175.8 4.7 copy-start.1
  181.6 5.8 %copy-start.18 = (bf16[2,32,1536]{2,1,0:T(8,128)(2,1)}, bf16[2,32,1536]{2,1,0:T(8,128)(2,1)S(1)}, u32[]{:S(2)}) copy-start(bf16[2,32,1536]{2,1,0:T(8,128)(2,1)S(1)} %multiply_convert_fusion.3) | copy-start | bytes 589828
  181.7 5.6 %copy-start.11 = (bf16[2,32,1536]{2,1,0:T(8,128)(2,1)}, bf16[2,32,1536]{2,1,0:T(8,128)(2,1)S(1)}, u32[]{:S(2)}) copy-start(bf16[2,32,1536]{2,1,0:T(8,128)(2,1)S(1)} %add_convert_fusion.1) | copy-start | bytes 589828
  189.9 5.6 %copy-start.4 = (bf16[2,256,1536]{2,1,0:T(8,128)(2,1)}, bf16[2,256,1536]{2,1,0:T(8,128)(2,1)S(1)}, u32[]{:S(2)}) copy-start(bf16[2,256,1536]{2,1,0:T(8,128)(2,1)S(1)} %multiply_convert_fusion.1) | copy-start | bytes 4718596
  189.9 5.6 %slice-start.4 = ((s8[9437184]{0:T(1024)(128)(4,1)}), s8[4194304]{0:T(1024)(128)(4,1)S(1)}, s32[]{:S(2)}) async-start(s8[9437184]{0:T(1024)(128)(4,1)} %bitcast.195), calls=%async_computation.4 | async-start | bytes 8388608
  191.1 4.4 copy-start.5
  191.1 4.4 slice-start.5
  191.1 4.4 slice-start.6
  302.4 38.0 %collective-permute-start = (bf16[384,1536]{1,0:T(8,128)(2,1)S(1)}, bf16[384,1536]{1,0:T(8,128)(2,1)}, u32[]{:S(2)}, u32[]{:S(2)}) collective-permute-start(bf16[384,1536]{1,0:T(8,128)(2,1)S(1)} %get-tuple-element.172), channel_id=1, source_target_pairs={{0,8},{4,12},{8,0},{12,4},{1,9},{5,13},{9,1},{13,5},{2,10},{6,14},... | collective-permute-start | bytes 3538952 | tf_op jit(solution)/shard_map/ppermute | solution.py:1843
  303.1 31.2 %copy-start.12 = (bf16[512,1536]{1,0:T(8,128)(2,1)S(1)}, bf16[512,1536]{1,0:T(8,128)(2,1)}, u32[]{:S(2)}) copy-start(bf16[512,1536]{1,0:T(8,128)(2,1)} %get-tuple-element.191.refs_6_) | copy-start | bytes 4718596
  330.1 10.3 %slice-start.2 = ((s8[4718592]{0:T(1024)(128)(4,1)}), s8[4194304]{0:T(1024)(128)(4,1)S(1)}, s32[]{:S(2)}) async-start(s8[4718592]{0:T(1024)(128)(4,1)} %bitcast.161), calls=%async_computation.2 | async-start | bytes 8388608
  334.3 6.1 %slice-start.3 = ((s8[4718592]{0:T(1024)(128)(4,1)}), s8[524288]{0:T(1024)(128)(4,1)S(1)}, s32[]{:S(2)}) async-start(s8[4718592]{0:T(1024)(128)(4,1)} %bitcast.161), calls=%async_computation.3 | async-start | bytes 1048576
  341.9 68.8 %collective-permute-start.1 = (bf16[384,1536]{1,0:T(8,128)(2,1)S(1)}, bf16[384,1536]{1,0:T(8,128)(2,1)}, u32[]{:S(2)}, u32[]{:S(2)}) collective-permute-start(bf16[384,1536]{1,0:T(8,128)(2,1)S(1)} %get-tuple-element.114), channel_id=1, source_target_pairs={{0,8},{4,12},{8,0},{12,4},{1,9},{5,13},{9,1},{13,5},{2,10},{6,14},... | collective-permute-start | bytes 3538952 | tf_op jit(solution)/shard_map/ppermute | solution.py:1843
  342.8 163.7 %collective-permute-start.2 = (bf16[384,1536]{1,0:T(8,128)(2,1)S(1)}, bf16[384,1536]{1,0:T(8,128)(2,1)S(1)}, u32[]{:S(2)}, u32[]{:S(2)}) collective-permute-start(bf16[384,1536]{1,0:T(8,128)(2,1)S(1)} %fusion.38), channel_id=1, source_target_pairs={{0,16},{16,0},{1,17},{17,1},{2,18},{18,2},{3,19},{19,3},{4,20},{20... | collective-permute-start | bytes 3538952 | tf_op jit(solution)/shard_map/ppermute | solution.py:1836
  413.1 93.7 %collective-permute-start.3 = (bf16[384,1536]{1,0:T(8,128)(2,1)S(1)}, bf16[384,1536]{1,0:T(8,128)(2,1)}, u32[]{:S(2)}, u32[]{:S(2)}) collective-permute-start(bf16[384,1536]{1,0:T(8,128)(2,1)S(1)} %fusion.37), channel_id=1, source_target_pairs={{0,16},{16,0},{1,17},{17,1},{2,18},{18,2},{3,19},{19,3},{4,20},{20... | collective-permute-start | bytes 3538952 | tf_op jit(solution)/shard_map/ppermute | solution.py:1836
  508.5 4.1 copy-start.17
  508.5 5.0 copy-start.20
  508.5 5.6 %copy-start.22 = (f32[2,384]{1,0:T(2,128)S(1)}, f32[2,384]{1,0:T(2,128)}, u32[]{:S(2)}) copy-start(f32[2,384]{1,0:T(2,128)} %get-tuple-element.224) | copy-start | bytes 9220
  508.5 6.2 %copy-start.9 = (f32[2,3,384,384]{3,2,1,0:T(8,128)S(1)}, f32[2,3,384,384]{3,2,1,0:T(8,128)}, u32[]{:S(2)}) copy-start(f32[2,3,384,384]{3,2,1,0:T(8,128)} %get-tuple-element.128) | copy-start | bytes 10616836
  514.1 4.4 slice-start
  (13 other events, 37.5 us)
